TPU v7x, 128 devices: a whole 4x4x4 slice. The times are simulated.
128 devices in a mesh: row: 16 (over x, y), col: 8 (over z, core).
Axes of the slice: x: 4, y: 4, z: 4, core: 2. Of those that a mesh axis runs over, the one named last changes fastest.
Arguments:
- surface: bfloat16 [16384, 16384], P('row', 'col'), may hold values from -0.0234375 to 0.0234375
- excitation: float32 [16384, 128], P(('row', 'col')), may hold values from -6 to 6
- dtn_blocks: bfloat16 [128, 1024, 1024], P(('row', 'col')), may hold values from -0.09375 to 0.09375
- interp_blocks: bfloat16 [128, 1024, 1024], P(('row', 'col')), may hold values from -0.125 to 0.125
- adjacency: int32 [128, 6], P(('row', 'col')), may hold values from 0 to 127, as said below
Outputs:
- solution: float32 [16384, 128], P(('row', 'col'))
- residual: float32 [16384, 128], P(('row', 'col'))
Inputs may be any that keep to these rules, and one draw needn't show every extreme that they name: `adjacency`: entry [s, k] names a subdomain of the same spatial group as s (equal index // 8); it may name s itself, which adds nothing.
All inputs are finite; a program needn't handle non-finite values.
Results may differ from a plain program's by a relative error of at most 0.02.
Values may be sent and summed in bfloat16 or wider, within the bound.
No kernel may reach another device: no remote copies, remote signals or barrier semaphores. Data moves between devices by JAX's collectives and lax.ppermute only.
A program may use at most 64 MiB of HBM per device.

v0:
```python
import jax
import jax.numpy as jnp
from jax import lax
from jax.sharding import PartitionSpec as P

ITERS = 2
NADJ = 6


damping = 0.25
face_weight = 0.25


def in_order(blocks, dim):
    blocks = jnp.moveaxis(blocks, 0, dim)
    shape = blocks.shape
    return blocks.reshape(*shape[:dim], shape[dim] * shape[dim + 1], *shape[dim + 2 :])


def copy_for_each(shard, axis):
    copies = jnp.broadcast_to(shard, (lax.axis_size(axis), *shard.shape))
    return lax.all_to_all(copies, axis, split_axis=0, concat_axis=0, tiled=True)


def collect(shard, axis, dim):
    return in_order(copy_for_each(shard, axis), dim)


def picked(shard, axis, root):
    return lax.dynamic_index_in_dim(lax.all_gather(shard, axis), root, 0, keepdims=False)


def split_up(shard, dim, peers):
    before, after = (shard.shape[:dim], shard.shape[dim + 1 :])
    return jnp.moveaxis(shard.reshape(*before, peers, -1, *after), dim, 0)


def sent_and_summed(shard, axis, dim):
    peers = lax.axis_size(axis)
    blocks = lax.all_to_all(split_up(shard, dim, peers), axis, 0, 0, tiled=True)
    return jnp.sum(blocks.astype(jnp.float32), axis=0)


def local(surface, excitation, dtn_blocks, interp_blocks, adjacency):
    col_count = lax.axis_size("col")
    row_count = lax.axis_size("row")
    col_index = lax.axis_index("col")
    dtn_block = dtn_blocks[0]
    interp_block = interp_blocks[0]
    local_adjacent = adjacency[0] % col_count
    current = excitation
    residual = excitation
    for sweep in range(ITERS):
        rounded = current.astype(jnp.bfloat16)
        group_block = collect(rounded, "col", 0)
        per_column = row_count // col_count
        received = [
            picked(group_block, "row", col_index * per_column + member)
            for member in range(per_column)
        ]
        column_block = jnp.concatenate(received, axis=0)
        traces = jnp.dot(interp_block, group_block, preferred_element_type=jnp.float32).astype(
            jnp.bfloat16
        )
        segment = collect(traces[None], "col", 0)
        owners = jnp.arange(segment.shape[0], dtype=jnp.int32)
        counts = jnp.sum((local_adjacent[None, :] == owners[:, None]).astype(jnp.float32), axis=1)
        neighbours = jnp.einsum(
            "p,pmn->mn", counts.astype(jnp.bfloat16), segment, preferred_element_type=jnp.float32
        )
        own_wide = traces.astype(jnp.float32)
        combined = jnp.dot(dtn_block, traces, preferred_element_type=jnp.float32) + own_wide
        combined = combined + face_weight * (NADJ * own_wide - neighbours)
        response = combined.astype(jnp.bfloat16)
        surface_part = jnp.dot(surface, column_block, preferred_element_type=jnp.float32)
        volume_part = lax.dot_general(
            interp_block, response, (((0,), (0,)), ((), ())), preferred_element_type=jnp.float32
        )
        summed = sent_and_summed((surface_part + volume_part).astype(jnp.bfloat16), "col", 0)
        residual = excitation - current - summed
        current = current + damping * residual
    return (current, residual)


def solution(mesh):
    in_specs = (
        P("row", "col"),
        P(("row", "col"), None),
        P(("row", "col"), None, None),
        P(("row", "col"), None, None),
        P(("row", "col"), None),
    )
    out_specs = (P(("row", "col"), None), P(("row", "col"), None))
    return jax.shard_map(local, mesh=mesh, in_specs=in_specs, out_specs=out_specs, check_vma=False)
```

profile of v0, /device:TPU:1, one launch (start us, length us, event | category | flops | bytes accessed | tf_op | source)
XLA Modules:
  0.0 174.8 jit_solution(12677278410290793132)
XLA Ops:
  7.2 0.0 all-gather.3.cloned.1.call-start
  7.2 1.0 convert_element_type.53
  8.2 13.2 %all_to_all.30 = bf16[8,128,128]{2,1,0:T(8,128)(2,1)} all-to-all(bf16[8,128,128]{2,1,0:T(8,128)(2,1)S(1)} %broadcast_in_dim.8), channel_id=1, replica_groups=mesh['row'=16,'col'=8] {'col'}, dimensions={0} | all-to-all | bytes 524288 | tf_op jit(solution)/shard_map/all_to_all | solution.py:22
  21.4 0.0 all-gather.3.cloned.1.call-update
  21.5 1.7 fusion.40
  23.1 1.6 broadcast_in_dim.9
  24.7 5.4 %all-to-all-start.1 = ((bf16[8,1,1024,128]{3,2,1,0:T(8,128)(2,1)}), bf16[8,1,1024,128]{3,2,1,0:T(8,128)(2,1)}, u32[]{:S(2)}, u32[]{:S(2)}) async-start(bf16[8,1,1024,128]{3,2,1,0:T(8,128)(2,1)} %broadcast_in_dim.9), calls=%async_computation.1 | async-start | bytes 4194304 | tf_op jit(solution)/shard_map/all_to_all | solution.py:22
  30.2 0.1 convert_reduce_fusion.2
  30.3 26.2 %all-to-all-done.1 = bf16[8,1,1024,128]{3,2,1,0:T(8,128)(2,1)} async-done(((bf16[8,1,1024,128]{3,2,1,0:T(8,128)(2,1)}), bf16[8,1,1024,128]{3,2,1,0:T(8,128)(2,1)}, u32[]{:S(2)}, u32[]{:S(2)}) %all-to-all-start.1) | async-done | bytes 2097184 | tf_op jit(solution)/shard_map/all_to_all | solution.py:22
  56.5 3.0 %fusion.14 = f32[1,1024,128]{2,0,1:T(1,128)S(1)} fusion(bf16[8,1024,128]{2,1,0:T(8,128)(2,1)} %bitcast.9, bf16[8]{0:T(256)(128)(2,1)S(1)} %convert_reduce_fusion.2), kind=kOutput, calls=%fused_computation.14 | convolution fusion | flops 2097152 | bytes 2621456 | tf_op jit(solution)/shard_map/p,pmn->mn/dot_general | solution.py:68
  59.5 2.6 %fusion.8 = f32[128,1024]{1,0:T(8,128)S(1)} fusion(bf16[1,1024,1024]{2,1,0:T(8,128)(2,1)S(1)} %copy-done, bf16[1024,128]{1,0:T(8,128)(2,1)S(1)} %fusion.40, bf16[1,1024,1024]{2,1,0:T(8,128)(2,1)} %param.7, f32[1024,128]{1,0:T(8,128)S(1)} %bitcast.114), kind=kOutput, calls=%fused_computation.8 | convolution fusion | flops 537788416 | bytes 5505024 | tf_op jit(solution)/shard_map/dot_general | solution.py:76
  62.1 10.5 %all-gather.3.cloned.1.call-done = bf16[16,1024,128]{2,1,0:T(8,128)(2,1)} async-done(((bf16[1,1024,128]{2,1,0:T(8,128)(2,1)}), bf16[16,1024,128]{2,1,0:T(8,128)(2,1)}) %all-gather.3.cloned.1.call-update) | async-done | bytes 4194320 | tf_op jit(solution)/shard_map/all_gather | solution.py:30
  72.6 1.1 dynamic-slice_bitcast_fusion.3
  73.7 3.8 %fusion.49 = bf16[16,8,8,128]{3,2,1,0:T(8,128)(2,1)S(1)} fusion(f32[128,1024]{1,0:T(8,128)S(1)} %fusion.8, bf16[1024,2048]{1,0:T(8,128)(2,1)} %param.5, bf16[1024,128]{1,0:T(8,128)(2,1)S(1)} %get-tuple-element.9, bf16[1024,128]{1,0:T(8,128)(2,1)S(1)} %get-tuple-element.8), kind=kOutput, calls=%fused_computation.31 | convolution fusion | flops 538181632 | bytes 5505024 | tf_op jit(solution)/shard_map/dot_general | solution.py:75
  77.4 0.7 copy.52
  78.2 5.3 %all-to-all-start.2 = ((bf16[8,128,128]{1,2,0:T(8,128)(2,1)}), bf16[8,128,128]{1,2,0:T(8,128)(2,1)S(1)}, u32[]{:S(2)}, u32[]{:S(2)}) async-start(bf16[8,128,128]{1,2,0:T(8,128)(2,1)} %bitcast.106), calls=%async_computation.2 | async-start | bytes 524288 | tf_op jit(solution)/shard_map/all_to_all | solution.py:40
  83.4 0.1 copy.25
  83.5 6.4 %all-to-all-done.2 = bf16[8,128,128]{1,2,0:T(8,128)(2,1)S(1)} async-done(((bf16[8,128,128]{1,2,0:T(8,128)(2,1)}), bf16[8,128,128]{1,2,0:T(8,128)(2,1)S(1)}, u32[]{:S(2)}, u32[]{:S(2)}) %all-to-all-start.2) | async-done | bytes 262176 | tf_op jit(solution)/shard_map/all_to_all | solution.py:40
  90.0 0.1 copy.27
  90.1 10.6 %all_to_all.31 = bf16[8,128,128]{2,1,0:T(8,128)(2,1)} all-to-all(bf16[8,128,128]{2,1,0:T(8,128)(2,1)S(1)} %broadcast_in_dim.20), channel_id=1, replica_groups=mesh['row'=16,'col'=8] {'col'}, dimensions={0} | all-to-all | bytes 524288 | tf_op jit(solution)/shard_map/all_to_all | solution.py:22
  100.7 0.0 all-gather.5.cloned.1.call-update
  100.7 1.7 fusion.43
  102.4 0.3 broadcast_in_dim.21
  102.7 29.7 %all_to_all.32 = bf16[8,1,1024,128]{3,2,1,0:T(8,128)(2,1)S(1)} all-to-all(bf16[8,1,1024,128]{3,2,1,0:T(8,128)(2,1)S(1)} %broadcast_in_dim.21), channel_id=1, replica_groups=mesh['row'=16,'col'=8] {'col'}, dimensions={0} | all-to-all | bytes 4194304 | tf_op jit(solution)/shard_map/all_to_all | solution.py:22
  132.3 1.4 fusion.12
  133.7 2.6 %fusion.4 = f32[128,1024]{1,0:T(8,128)S(1)} fusion(bf16[1,1024,1024]{2,1,0:T(8,128)(2,1)S(1)} %copy-done, bf16[128,1024]{0,1:T(8,128)(2,1)S(1)} %fusion.43, bf16[1,1024,1024]{2,1,0:T(8,128)(2,1)} %param.7, f32[1024,128]{1,0:T(8,128)S(1)} %bitcast.113), kind=kOutput, calls=%fused_computation.4 | convolution fusion | flops 537788416 | bytes 5505024 | tf_op jit(solution)/shard_map/dot_general | solution.py:76
  136.3 13.8 %all-gather.5.cloned.1.call-done = bf16[16,1024,128]{2,1,0:T(8,128)(2,1)} async-done(((bf16[1,1024,128]{2,1,0:T(8,128)(2,1)}), bf16[16,1024,128]{2,1,0:T(8,128)(2,1)}) %all-gather.5.cloned.1.call-update) | async-done | bytes 4194320 | tf_op jit(solution)/shard_map/all_gather | solution.py:30
  150.1 1.1 dynamic-slice_bitcast_fusion.1
  151.2 3.7 %fusion.48 = bf16[16,8,8,128]{3,2,1,0:T(8,128)(2,1)S(1)} fusion(f32[128,1024]{1,0:T(8,128)S(1)} %fusion.4, bf16[1024,2048]{1,0:T(8,128)(2,1)} %param.5, bf16[1024,128]{1,0:T(8,128)(2,1)S(1)} %get-tuple-element.7, bf16[1024,128]{1,0:T(8,128)(2,1)S(1)} %get-tuple-element.6), kind=kOutput, calls=%fused_computation.30 | convolution fusion | flops 538181632 | bytes 5505024 | tf_op jit(solution)/shard_map/dot_general | solution.py:75
  154.9 11.5 %all_to_all.33 = bf16[8,128,128]{1,2,0:T(8,128)(2,1)S(1)} all-to-all(bf16[8,128,128]{1,2,0:T(8,128)(2,1)S(1)} %bitcast.115), channel_id=1, replica_groups=mesh['row'=16,'col'=8] {'col'}, dimensions={0} | all-to-all | bytes 524288 | tf_op jit(solution)/shard_map/all_to_all | solution.py:40
  166.5 0.7 copy.33
  167.3 0.7 copy.32
  (15 shorter events, 0.3 us)
Async XLA Ops:
  7.2 14.3 %copy-start = (bf16[1,1024,1024]{2,1,0:T(8,128)(2,1)S(1)}, bf16[1,1024,1024]{2,1,0:T(8,128)(2,1)}, u32[]{:S(2)}) copy-start(bf16[1,1024,1024]{2,1,0:T(8,128)(2,1)} %param.8) | copy-start | bytes 6291460
  7.2 65.4 %all-gather.3.cloned.1.call-start = ((), (), s32[]{:S(2)}) async-start(), calls=%async_computation.6 | async-start | bytes 4456448 | tf_op jit(solution)/shard_map/all_gather | solution.py:30
  24.7 5.4 %copy-start.2 = (s32[1,6]{1,0:T(1,128)S(1)}, s32[1,6]{1,0:T(1,128)}, u32[]{:S(2)}) copy-start(s32[1,6]{1,0:T(1,128)} %param.9) | copy-start | bytes 76
  24.7 31.7 %all-to-all-start.1 = ((bf16[8,1,1024,128]{3,2,1,0:T(8,128)(2,1)}), bf16[8,1,1024,128]{3,2,1,0:T(8,128)(2,1)}, u32[]{:S(2)}, u32[]{:S(2)}) async-start(bf16[8,1,1024,128]{3,2,1,0:T(8,128)(2,1)} %broadcast_in_dim.9), calls=%async_computation.1 | async-start | bytes 4194304 | tf_op jit(solution)/shard_map/all_to_all | solution.py:22
  73.7 9.8 %copy-start.1 = (f32[128,128]{1,0:T(8,128)S(1)}, f32[128,128]{1,0:T(8,128)}, u32[]{:S(2)}) copy-start(f32[128,128]{1,0:T(8,128)} %param.6) | copy-start | bytes 196612
  78.2 11.7 %all-to-all-start.2 = ((bf16[8,128,128]{1,2,0:T(8,128)(2,1)}), bf16[8,128,128]{1,2,0:T(8,128)(2,1)S(1)}, u32[]{:S(2)}, u32[]{:S(2)}) async-start(bf16[8,128,128]{1,2,0:T(8,128)(2,1)} %bitcast.106), calls=%async_computation.2 | async-start | bytes 524288 | tf_op jit(solution)/shard_map/all_to_all | solution.py:40
  83.4 66.6 %all-gather.5.cloned.1.call-start = ((), (), s32[]{:S(2)}) async-start(), calls=%async_computation.7 | async-start | bytes 4456448 | tf_op jit(solution)/shard_map/all_gather | solution.py:30
Sparse Core Ops, SparseCore 0:
  21.6 50.9 all-gather.2
  100.8 49.1 all-gather.4
where the time goes:
time: 176 us; the launch traced here: 175 us
  blocking collectives  64.9 us (37%)
  waiting for transfers between devices  56.9 us (32%)
  matrix products  20.4 us (12%)
  between operations  14.2 us (8%)
  starting transfers between devices  10.7 us (6%)
  local copies, waits for them, and re-layouts  6.58 us (4%)
    all_to_all x3, blocking collectives, copy_for_each(): return lax.all_to_all(copies, axis, split_axis=0, concat_axis=0, tiled=True)  53.4 us
    all_to_all x1, waiting for transfers between devices, copy_for_each(): return lax.all_to_all(copies, axis, split_axis=0, concat_axis=0, tiled=True)  26.2 us
    all_gather x2, waiting for transfers between devices, picked(): lax.all_gather(shard, axis)  24.3 us
    all_to_all x1, blocking collectives, sent_and_summed(): blocks = lax.all_to_all(split_up(shard, dim, peers), axis, 0, 0, tiled=True)  11.5 us
    dot_general x2, matrix products, local(): jnp.dot(surface, column_block, preferred_element_type=jnp.float32)  7.46 us
    all_to_all x1, waiting for transfers between devices, sent_and_summed(): blocks = lax.all_to_all(split_up(shard, dim, peers), axis, 0, 0, tiled=True)  6.37 us
    all_to_all x1, starting transfers between devices, copy_for_each(): return lax.all_to_all(copies, axis, split_axis=0, concat_axis=0, tiled=True)  5.4 us
    all_to_all x1, starting transfers between devices, sent_and_summed(): blocks = lax.all_to_all(split_up(shard, dim, peers), axis, 0, 0, tiled=True)  5.26 us
  transfers between devices with their start and end apart: 4, of which 4 were waited for; matrix products, arithmetic and copies ran while one was open for 9% of the time, Pallas kernels for 0%

commit v1 on v0

v1 whole, which is shorter than its diff:
```python
import jax
import jax.numpy as jnp
from jax import lax
from jax.sharding import PartitionSpec as P

ITERS = 2
NADJ = 6

damping = 0.25
face_weight = 0.25

BF = jnp.bfloat16
F32 = jnp.float32


def dot(a, b):
    return jnp.dot(a, b, preferred_element_type=F32)


def dot_t(a, b):
    return lax.dot_general(a, b, (((0,), (0,)), ((), ())), preferred_element_type=F32)


def exchange(blocks, axis):
    return lax.all_to_all(blocks, axis, split_axis=0, concat_axis=0, tiled=True)


def copy_for_each(shard, axis):
    return exchange(jnp.broadcast_to(shard, (lax.axis_size(axis), *shard.shape)), axis)


def turned(rows, cols):
    per_col = rows // cols
    return [
        (r * cols + c, ((r % per_col) * cols + c) * cols + r // per_col)
        for r in range(rows)
        for c in range(cols)
    ]


def local(surface, excitation, dtn_blocks, interp_blocks, adjacency):
    cols = lax.axis_size("col")
    rows = lax.axis_size("row")
    dtn = dtn_blocks[0]
    interp = interp_blocks[0]
    m, rb = interp.shape
    ms = m // cols
    n, ne = excitation.shape

    with jax.named_scope("slices"):
        slices = exchange(interp.reshape(cols, ms, rb), "col")

    adjacent = adjacency[0] % cols
    owners = jnp.arange(ne, dtype=jnp.int32)
    counts = jnp.sum((adjacent[None, :] == owners[:, None]).astype(F32), axis=1)
    me = (owners == lax.axis_index("col")).astype(F32)
    weights = (1.0 + face_weight * NADJ) * me - face_weight * counts
    extra = jnp.broadcast_to(weights.astype(BF)[None, :], (16, ne))

    own = dot_t(interp, dot(dtn, interp).astype(BF))
    current = excitation
    residual = excitation
    operator = None
    for sweep in range(ITERS):
        rounded = current.astype(BF)
        with jax.named_scope("turn"):
            piece = lax.ppermute(rounded, ("row", "col"), turned(rows, cols))
        with jax.named_scope("columns"):
            column_block = copy_for_each(piece, "row").reshape(rows * n, ne)
        with jax.named_scope("group"):
            if sweep == 0:
                got = copy_for_each(jnp.concatenate([rounded, extra], axis=0), "col")
                group_block = got[:, :n].reshape(cols * n, ne)
                mix = got[:, n, :cols]
            else:
                group_block = copy_for_each(rounded, "col").reshape(cols * n, ne)
        if sweep == 0:
            tall = slices.reshape(m, rb)
            kind = jnp.repeat(jnp.repeat(mix, ms, axis=0), ms, axis=1)
            place = jnp.arange(m, dtype=jnp.int32) % ms
            spread = jnp.where(place[:, None] == place[None, :], kind, jnp.zeros((), BF))
            faces = dot_t(tall, dot(spread, tall).astype(BF))
            operator = (own + faces).astype(BF)
        part = dot(operator, group_block) + dot(surface, column_block)
        with jax.named_scope("result"):
            blocks = exchange(part.astype(BF).reshape(cols, n, ne), "col")
        summed = jnp.sum(blocks.astype(F32), axis=0)
        residual = excitation - current - summed
        current = current + damping * residual
    return (current, residual)


def solution(mesh):
    in_specs = (
        P("row", "col"),
        P(("row", "col"), None),
        P(("row", "col"), None, None),
        P(("row", "col"), None, None),
        P(("row", "col"), None),
    )
    out_specs = (P(("row", "col"), None), P(("row", "col"), None))
    return jax.shard_map(local, mesh=mesh, in_specs=in_specs, out_specs=out_specs, check_vma=False)
```

time: 176 us -> 132 us (0.75)
  waiting for transfers between devices: 56.9 us -> 24.5 us
  blocking collectives: 64.9 us -> 38.3 us
  starting transfers between devices: 10.7 us -> 32.2 us
  between operations: 14.2 us -> 0.78 us
  matrix products: 20.4 us -> 29.9 us
  local copies, waits for them, and re-layouts: 6.58 us -> 2.73 us
    all_to_all x4 -> x3, blocking collectives: 64.9 us -> 38.3 us  [exchange(): return lax.all_to_all(blocks, axis, split_axis=0, concat_axis=0, tiled=True)]
    all_gather x2 -> x0, waiting for transfers between devices: 24.3 us -> none  [picked(): lax.all_gather(shard, axis)]
    all_to_all x2 -> x4, starting transfers between devices: 10.7 us -> 25.5 us  [exchange(): return lax.all_to_all(blocks, axis, split_axis=0, concat_axis=0, tiled=True)]
    all_to_all x2 -> x4, waiting for transfers between devices: 32.6 us -> 21 us  [exchange(): return lax.all_to_all(blocks, axis, split_axis=0, concat_axis=0, tiled=True)]
    dot_general x8 -> x6, matrix products: 20.4 us -> 29.9 us  [the longest x2 18.4 us: dot_t(): lax.dot_general(a, b, (((0,), (0,)), ((), ())), preferred_element_type=F32)]
    ppermute x0 -> x2, starting transfers between devices: none -> 6.77 us  [local(): piece = lax.ppermute(rounded, ('row', 'col'), turned(rows, cols))]
    ppermute x0 -> x2, waiting for transfers between devices: none -> 3.52 us  [local(): piece = lax.ppermute(rounded, ('row', 'col'), turned(rows, cols))]
    squeeze x2 -> x0, local copies, waits for them, and re-layouts: 2.13 us -> none  [picked(): lax.dynamic_index_in_dim(lax.all_gather(shard, axis), root, 0, keepdims=F...]
  transfers between devices with their start and end apart: 4 -> 6, of which waited for: 4 -> 3; matrix products, arithmetic and copies ran while one was open for 9% -> 18% of each run, Pallas kernels for 0% -> 0%
where the time goes in v1:
time: 132 us; the launch traced here: 131 us
  blocking collectives  38.3 us (29%)
  starting transfers between devices  32.2 us (24%)
  matrix products  29.9 us (23%)
  waiting for transfers between devices  24.5 us (19%)
  local copies, waits for them, and re-layouts  2.73 us (2%)
  other arithmetic  2.53 us (2%)
    all_to_all x3, blocking collectives, exchange(): return lax.all_to_all(blocks, axis, split_axis=0, concat_axis=0, tiled=True)  38.3 us
    all_to_all x4, starting transfers between devices, exchange(): return lax.all_to_all(blocks, axis, split_axis=0, concat_axis=0, tiled=True)  25.5 us
    all_to_all x4, waiting for transfers between devices, exchange(): return lax.all_to_all(blocks, axis, split_axis=0, concat_axis=0, tiled=True)  21 us
    dot_general x2, matrix products, dot_t(): lax.dot_general(a, b, (((0,), (0,)), ((), ())), preferred_element_type=F32)  18.4 us
    dot_general x4, matrix products, dot(): return jnp.dot(a, b, preferred_element_type=F32)  11.6 us
    ppermute x2, starting transfers between devices, local(): piece = lax.ppermute(rounded, ('row', 'col'), turned(rows, cols))  6.77 us
    ppermute x2, waiting for transfers between devices, local(): piece = lax.ppermute(rounded, ('row', 'col'), turned(rows, cols))  3.52 us
  transfers between devices with their start and end apart: 6, of which 3 were waited for; matrix products, arithmetic and copies ran while one was open for 18% of the time, Pallas kernels for 0%

profile of v1, /device:TPU:1, one launch (start us, length us, event | category | flops | bytes accessed | tf_op | source)
XLA Modules:
  0.0 131.0 jit_solution(188472255898583784)
XLA Ops:
  0.6 0.0 copy-start
  0.6 1.0 convert_element_type.40
  1.6 0.7 fusion.29
  2.3 0.1 convert_reduce_fusion.2
  2.5 13.9 %all_to_all.35 = bf16[8,144,128]{2,1,0:T(8,128)(2,1)S(1)} all-to-all(bf16[8,144,128]{2,1,0:T(8,128)(2,1)S(1)} %broadcast_in_dim.33), channel_id=1, replica_groups=mesh['row'=16,'col'=8] {'col'}, dimensions={0} | all-to-all | bytes 589824 | tf_op jit(solution)/shard_map/group/all_to_all | solution.py:25
  16.4 4.8 %all-to-all-start.1 = ((bf16[8,128,1024]{2,1,0:T(8,128)(2,1)}), bf16[8,128,1024]{2,1,0:T(8,128)(2,1)}, u32[]{:S(2)}, u32[]{:S(2)}) async-start(bf16[8,128,1024]{2,1,0:T(8,128)(2,1)} %bitcast.53), calls=%async_computation.1 | async-start | bytes 4194304 | tf_op jit(solution)/shard_map/slices/all_to_all | solution.py:25
  21.1 3.2 %collective-permute-start = (bf16[128,128]{1,0:T(8,128)(2,1)S(1)}, bf16[128,128]{1,0:T(8,128)(2,1)S(1)}, u32[]{:S(2)}, u32[]{:S(2)}) collective-permute-start(bf16[128,128]{1,0:T(8,128)(2,1)S(1)} %convert_element_type.40), channel_id=1, source_target_pairs={{0,0},{1,8},{2,16},{3,24},{4,32},{5,40},{6,48},{7,56},{8,64},{9,72... | collective-permute-start | bytes 98312 | tf_op jit(solution)/shard_map/turn/ppermute | solution.py:67
  24.4 8.7 %fusion = f32[1024,1024]{1,0:T(8,128)} fusion(bf16[1,1024,1024]{2,1,0:T(8,128)(2,1)} %param.8, bf16[1,1024,1024]{2,1,0:T(8,128)(2,1)S(1)} %copy-done), kind=kOutput, calls=%fused_computation.3 | convolution fusion | flops 4296015872 | bytes 8388608 | tf_op jit(solution)/shard_map/dot_general | solution.py:21
  33.1 0.1 broadcast_bitcast_fusion
  33.2 0.0 collective-permute-done
  33.2 14.3 %all-to-all-done.1 = bf16[8,128,1024]{2,1,0:T(8,128)(2,1)} async-done(((bf16[8,128,1024]{2,1,0:T(8,128)(2,1)}), bf16[8,128,1024]{2,1,0:T(8,128)(2,1)}, u32[]{:S(2)}, u32[]{:S(2)}) %all-to-all-start.1) | async-done | bytes 2097184 | tf_op jit(solution)/shard_map/slices/all_to_all | solution.py:25
  47.5 0.9 broadcast_in_dim.37
  48.4 6.8 %all-to-all-start.2 = ((bf16[16,128,128]{2,1,0:T(8,128)(2,1)}), bf16[16,128,128]{2,1,0:T(8,128)(2,1)S(1)}, u32[]{:S(2)}, u32[]{:S(2)}) async-start(bf16[16,128,128]{2,1,0:T(8,128)(2,1)} %broadcast_in_dim.37), calls=%async_computation.2 | async-start | bytes 1048576 | tf_op jit(solution)/shard_map/columns/all_to_all | solution.py:25
  55.2 0.0 slice-start
  55.2 9.7 %add_convert_fusion = bf16[1024,1024]{1,0:T(8,128)(2,1)} fusion(f32[1024,1024]{1,0:T(8,128)} %fusion, bf16[1024,1024]{1,0:T(8,128)(2,1)} %bitcast.7, bf16[8,128,1024]{2,1,0:T(8,128)(2,1)} %all-to-all-done.1, s32[8,128]{1,0:T(8,128)S(1)} %add_select_fusion, s32[1024]{0:T(1024)S(1)} %add_select_fusion.1, bf16[1024,8]{0,1:T(8,128)(2,1)S(1)} %broadcast_bitcast_fusion), kind=kOutput, calls=%fused_computation.1 | convolution fusion | flops 4300210176 | bytes 10510336 | tf_op jit(solution)/shard_map/dot_general | solution.py:21
  64.9 2.3 %fusion.34 = f32[1024,128]{1,0:T(8,128)S(1)} fusion(bf16[1024,1024]{1,0:T(8,128)(2,1)} %add_convert_fusion, bf16[1024,128]{1,0:T(8,128)(2,1)S(1)} %bitcast.56), kind=kOutput, calls=%fused_computation.48 | convolution fusion | flops 268435456 | bytes 2883584 | tf_op jit(solution)/shard_map/dot_general | solution.py:17
  67.2 0.0 all-to-all-done.2
  67.2 0.0 copy-start.2
  67.2 3.5 %fusion.18 = bf16[1024,128]{1,0:T(8,128)(2,1)S(1)} fusion(f32[1024,128]{1,0:T(8,128)S(1)} %fusion.34, bf16[1024,2048]{1,0:T(8,128)(2,1)} %param.5, bf16[2048,128]{1,0:T(8,128)(2,1)S(1)} %bitcast.51), kind=kOutput, calls=%fused_computation.15 | convolution fusion | flops 537133056 | bytes 5505024 | tf_op jit(solution)/shard_map/dot_general | solution.py:17
  70.7 11.2 %all_to_all.36 = bf16[8,128,128]{2,1,0:T(8,128)(2,1)S(1)} all-to-all(bf16[8,128,128]{2,1,0:T(8,128)(2,1)S(1)} %bitcast.54), channel_id=1, replica_groups=mesh['row'=16,'col'=8] {'col'}, dimensions={0} | all-to-all | bytes 524288 | tf_op jit(solution)/shard_map/result/all_to_all | solution.py:25
  82.0 0.7 broadcast_in_dim.38
  82.7 4.4 %all-to-all-start.4 = ((bf16[8,128,128]{2,1,0:T(8,128)(2,1)}), bf16[8,128,128]{2,1,0:T(8,128)(2,1)S(1)}, u32[]{:S(2)}, u32[]{:S(2)}) async-start(bf16[8,128,128]{2,1,0:T(8,128)(2,1)} %broadcast_in_dim.38), calls=%async_computation.4 | async-start | bytes 524288 | tf_op jit(solution)/shard_map/group/all_to_all | solution.py:25
  87.1 3.5 %collective-permute-start.1 = (bf16[128,128]{1,0:T(8,128)(2,1)S(1)}, bf16[128,128]{1,0:T(8,128)(2,1)S(1)}, u32[]{:S(2)}, u32[]{:S(2)}) collective-permute-start(bf16[128,128]{1,0:T(8,128)(2,1)S(1)} %fusion.27), channel_id=1, source_target_pairs={{0,0},{1,8},{2,16},{3,24},{4,32},{5,40},{6,48},{7,56},{8,64},{9,72... | collective-permute-start | bytes 98312 | tf_op jit(solution)/shard_map/turn/ppermute | solution.py:67
  90.6 3.5 %collective-permute-done.1 = bf16[128,128]{1,0:T(8,128)(2,1)S(1)} collective-permute-done((bf16[128,128]{1,0:T(8,128)(2,1)S(1)}, bf16[128,128]{1,0:T(8,128)(2,1)S(1)}, u32[]{:S(2)}, u32[]{:S(2)}) %collective-permute-start.1) | collective-permute-done | bytes 32800 | tf_op jit(solution)/shard_map/turn/ppermute | solution.py:67
  94.1 0.0 all-to-all-done.4
  94.1 0.9 broadcast_in_dim.39
  95.0 9.6 %all-to-all-start.5 = ((bf16[16,128,128]{2,1,0:T(8,128)(2,1)}), bf16[16,128,128]{2,1,0:T(8,128)(2,1)S(1)}, u32[]{:S(2)}, u32[]{:S(2)}) async-start(bf16[16,128,128]{2,1,0:T(8,128)(2,1)} %broadcast_in_dim.39), calls=%async_computation.5 | async-start | bytes 1048576 | tf_op jit(solution)/shard_map/columns/all_to_all | solution.py:25
  104.6 2.3 %fusion.35 = f32[1024,128]{1,0:T(8,128)S(1)} fusion(bf16[1024,1024]{1,0:T(8,128)(2,1)} %add_convert_fusion, bf16[1024,128]{1,0:T(8,128)(2,1)S(1)} %bitcast.57), kind=kOutput, calls=%fused_computation.49 | convolution fusion | flops 268435456 | bytes 2883584 | tf_op jit(solution)/shard_map/dot_general | solution.py:17
  106.9 6.7 %all-to-all-done.5 = bf16[16,128,128]{2,1,0:T(8,128)(2,1)S(1)} async-done(((bf16[16,128,128]{2,1,0:T(8,128)(2,1)}), bf16[16,128,128]{2,1,0:T(8,128)(2,1)S(1)}, u32[]{:S(2)}, u32[]{:S(2)}) %all-to-all-start.5) | async-done | bytes 524320 | tf_op jit(solution)/shard_map/columns/all_to_all | solution.py:25
  113.6 3.4 %fusion.17 = bf16[1024,128]{1,0:T(8,128)(2,1)S(1)} fusion(f32[1024,128]{1,0:T(8,128)S(1)} %fusion.35, bf16[1024,2048]{1,0:T(8,128)(2,1)} %param.5, bf16[2048,128]{1,0:T(8,128)(2,1)S(1)} %bitcast.52), kind=kOutput, calls=%fused_computation.14 | convolution fusion | flops 537133056 | bytes 5505024 | tf_op jit(solution)/shard_map/dot_general | solution.py:17
  117.1 13.2 %all_to_all.37 = bf16[8,128,128]{2,1,0:T(8,128)(2,1)S(1)} all-to-all(bf16[8,128,128]{2,1,0:T(8,128)(2,1)S(1)} %bitcast.55), channel_id=1, replica_groups=mesh['row'=16,'col'=8] {'col'}, dimensions={0} | all-to-all | bytes 524288 | tf_op jit(solution)/shard_map/result/all_to_all | solution.py:25
  130.4 0.7 multiply_add_fusion
  (16 shorter events, 0.2 us)
Async XLA Ops:
  0.6 23.8 %copy-start = (bf16[1,1024,1024]{2,1,0:T(8,128)(2,1)S(1)}, bf16[1,1024,1024]{2,1,0:T(8,128)(2,1)}, u32[]{:S(2)}) copy-start(bf16[1,1024,1024]{2,1,0:T(8,128)(2,1)} %param.7) | copy-start | bytes 6291460
  16.4 16.8 %copy-start.1 = (bf16[8,144,128]{2,1,0:T(8,128)(2,1)}, bf16[8,144,128]{2,1,0:T(8,128)(2,1)S(1)}, u32[]{:S(2)}) copy-start(bf16[8,144,128]{2,1,0:T(8,128)(2,1)S(1)} %all_to_all.35) | copy-start | bytes 884740
  16.4 31.1 %all-to-all-start.1 = ((bf16[8,128,1024]{2,1,0:T(8,128)(2,1)}), bf16[8,128,1024]{2,1,0:T(8,128)(2,1)}, u32[]{:S(2)}, u32[]{:S(2)}) async-start(bf16[8,128,1024]{2,1,0:T(8,128)(2,1)} %bitcast.53), calls=%async_computation.1 | async-start | bytes 4194304 | tf_op jit(solution)/shard_map/slices/all_to_all | solution.py:25
  21.1 12.0 %collective-permute-start = (bf16[128,128]{1,0:T(8,128)(2,1)S(1)}, bf16[128,128]{1,0:T(8,128)(2,1)S(1)}, u32[]{:S(2)}, u32[]{:S(2)}) collective-permute-start(bf16[128,128]{1,0:T(8,128)(2,1)S(1)} %convert_element_type.40), channel_id=1, source_target_pairs={{0,0},{1,8},{2,16},{3,24},{4,32},{5,40},{6,48},{7,56},{8,64},{9,72... | collective-permute-start | bytes 98312 | tf_op jit(solution)/shard_map/turn/ppermute | solution.py:67
  48.4 18.8 %all-to-all-start.2 = ((bf16[16,128,128]{2,1,0:T(8,128)(2,1)}), bf16[16,128,128]{2,1,0:T(8,128)(2,1)S(1)}, u32[]{:S(2)}, u32[]{:S(2)}) async-start(bf16[16,128,128]{2,1,0:T(8,128)(2,1)} %broadcast_in_dim.37), calls=%async_computation.2 | async-start | bytes 1048576 | tf_op jit(solution)/shard_map/columns/all_to_all | solution.py:25
  55.2 9.7 %slice-start = ((bf16[8,144,128]{2,1,0:T(8,128)(2,1)}), bf16[8,128,128]{2,1,0:T(8,128)(2,1)S(1)}, s32[]{:S(2)}) async-start(bf16[8,144,128]{2,1,0:T(8,128)(2,1)} %copy-done.1), calls=%async_computation.7 | async-start | bytes 524288 | tf_op jit(solution)/shard_map/group/slice | solution.py:73
  67.2 14.7 %copy-start.2 = (f32[128,128]{1,0:T(8,128)S(1)}, f32[128,128]{1,0:T(8,128)}, u32[]{:S(2)}) copy-start(f32[128,128]{1,0:T(8,128)} %param.6) | copy-start | bytes 196612
  82.7 11.4 %all-to-all-start.4 = ((bf16[8,128,128]{2,1,0:T(8,128)(2,1)}), bf16[8,128,128]{2,1,0:T(8,128)(2,1)S(1)}, u32[]{:S(2)}, u32[]{:S(2)}) async-start(bf16[8,128,128]{2,1,0:T(8,128)(2,1)} %broadcast_in_dim.38), calls=%async_computation.4 | async-start | bytes 524288 | tf_op jit(solution)/shard_map/group/all_to_all | solution.py:25
  87.1 7.1 %collective-permute-start.1 = (bf16[128,128]{1,0:T(8,128)(2,1)S(1)}, bf16[128,128]{1,0:T(8,128)(2,1)S(1)}, u32[]{:S(2)}, u32[]{:S(2)}) collective-permute-start(bf16[128,128]{1,0:T(8,128)(2,1)S(1)} %fusion.27), channel_id=1, source_target_pairs={{0,0},{1,8},{2,16},{3,24},{4,32},{5,40},{6,48},{7,56},{8,64},{9,72... | collective-permute-start | bytes 98312 | tf_op jit(solution)/shard_map/turn/ppermute | solution.py:67
  95.0 18.6 %all-to-all-start.5 = ((bf16[16,128,128]{2,1,0:T(8,128)(2,1)}), bf16[16,128,128]{2,1,0:T(8,128)(2,1)S(1)}, u32[]{:S(2)}, u32[]{:S(2)}) async-start(bf16[16,128,128]{2,1,0:T(8,128)(2,1)} %broadcast_in_dim.39), calls=%async_computation.5 | async-start | bytes 1048576 | tf_op jit(solution)/shard_map/columns/all_to_all | solution.py:25

commit v2 on v1

v2 whole, which is shorter than its diff:
```python
import jax
import jax.numpy as jnp
from jax import lax
from jax.experimental import pallas as pl
from jax.experimental.pallas import tpu as pltpu
from jax.sharding import PartitionSpec as P


ITERS = 2
NADJ = 6

damping = 0.25
face_weight = 0.25

BF = jnp.bfloat16
F32 = jnp.float32


def dot(a, b):
    return jnp.dot(a, b, preferred_element_type=F32)


def dot_t(a, b):
    return lax.dot_general(a, b, (((0,), (0,)), ((), ())), preferred_element_type=F32)


def exchange(blocks, axis):
    return lax.all_to_all(blocks, axis, split_axis=0, concat_axis=0, tiled=True)


def copy_for_each(shard, axis):
    return exchange(jnp.broadcast_to(shard, (lax.axis_size(axis), *shard.shape)), axis)


def turned(rows, cols):
    per_col = rows // cols
    return [
        (r * cols + c, ((r % per_col) * cols + c) * cols + r // per_col)
        for r in range(rows)
        for c in range(cols)
    ]


def volume_kernel(interp_ref, dtn_ref, group_ref, out_ref):
    traces = dot(interp_ref[...], group_ref[...]).astype(BF)
    response = dot(dtn_ref[...], traces).astype(BF)
    out_ref[...] = dot_t(interp_ref[...], response)


def faces_kernel(*refs):
    mix_ref, prior_ref, group_ref = refs[:3]
    slice_refs = refs[3:-1]
    out_ref = refs[-1]
    peers = len(slice_refs)
    group = group_ref[...]
    traces = [dot(ref[...], group).astype(BF).astype(F32) for ref in slice_refs]
    total = prior_ref[...]
    for s in range(peers):
        mixed = mix_ref[s, 0] * traces[0]
        for p in range(1, peers):
            mixed = mixed + mix_ref[s, p] * traces[p]
        total = total + dot_t(slice_refs[s][...], mixed.astype(BF))
    out_ref[...] = total.astype(out_ref.dtype)


def surface_kernel(prior_ref, surface_ref, column_ref, out_ref):
    out_ref[...] = (prior_ref[...] + dot(surface_ref[...], column_ref[...])).astype(out_ref.dtype)


def vmem():
    return pl.BlockSpec(memory_space=pltpu.VMEM)


def volume(interp, dtn, group_block):
    shape = jax.ShapeDtypeStruct(group_block.shape, F32)
    return pl.pallas_call(
        volume_kernel, out_shape=shape, in_specs=[vmem()] * 3, out_specs=vmem(), name="volume"
    )(interp, dtn, group_block)


def applied(prior, surface, column_block, dtype):
    shape = jax.ShapeDtypeStruct(prior.shape, dtype)
    return pl.pallas_call(
        surface_kernel, out_shape=shape, in_specs=[vmem()] * 3, out_specs=vmem(), name="applied"
    )(prior, surface, column_block)


def faces(mix, prior, group_block, slices, dtype):
    shape = jax.ShapeDtypeStruct(group_block.shape, dtype)
    return pl.pallas_call(
        faces_kernel,
        out_shape=shape,
        in_specs=[pl.BlockSpec(memory_space=pltpu.SMEM)] + [vmem()] * (2 + len(slices)),
        out_specs=vmem(),
        name="faces",
    )(mix, prior, group_block, *slices)


def steps(surface, excitation, dtn_blocks, interp_blocks, adjacency):
    cols = lax.axis_size("col")
    rows = lax.axis_size("row")
    col = lax.axis_index("col")
    dtn = dtn_blocks[0]
    interp = interp_blocks[0]
    m, _ = interp.shape
    ms = m // cols
    n, ne = excitation.shape

    slices = []
    for k in range(cols):
        block = lax.dynamic_slice_in_dim(interp, ((col + k) & (cols - 1)) * ms, ms, 0)
        if k:
            block = lax.ppermute(block, "col", [(i, (i + k) % cols) for i in range(cols)])
        slices.append(block)

    adjacent = adjacency[0] % cols
    owners = jnp.arange(ne, dtype=jnp.int32)
    counts = jnp.sum((adjacent[None, :] == owners[:, None]).astype(F32), axis=1)
    me = (owners == col).astype(F32)
    weights = (1.0 + face_weight * NADJ) * me - face_weight * counts
    extra = jnp.broadcast_to(weights.astype(BF)[None, :], (16, ne))

    current = excitation
    residual = excitation
    mix = None
    for sweep in range(ITERS):
        rounded = current.astype(BF)
        piece = lax.ppermute(rounded, ("row", "col"), turned(rows, cols))
        column_block = copy_for_each(piece, "row").reshape(rows * n, ne)
        if sweep == 0:
            got = copy_for_each(jnp.concatenate([rounded, extra], axis=0), "col")
            group_block = got[:, :n].reshape(cols * n, ne)
            order = (col - jnp.arange(cols, dtype=jnp.int32)) & (cols - 1)
            pick = (order[:, None] == jnp.arange(cols, dtype=jnp.int32)[None, :]).astype(F32)
            mix = pick @ got[:, n, :cols].astype(F32) @ pick.T
        else:
            group_block = copy_for_each(rounded, "col").reshape(cols * n, ne)
        own = volume(interp, dtn, group_block)
        if sweep == 0:
            wide = applied(own, surface, column_block, F32)
            part = faces(mix, wide, group_block, slices, BF)
        else:
            wide = faces(mix, own, group_block, slices, F32)
            part = applied(wide, surface, column_block, BF)
        blocks = exchange(part.reshape(cols, n, ne), "col")
        summed = jnp.sum(blocks.astype(F32), axis=0)
        residual = excitation - current - summed
        current = current + damping * residual
    return (current, residual)


def solution(mesh):
    in_specs = (
        P("row", "col"),
        P(("row", "col"), None),
        P(("row", "col"), None, None),
        P(("row", "col"), None, None),
        P(("row", "col"), None),
    )
    out_specs = (P(("row", "col"), None), P(("row", "col"), None))
    return jax.shard_map(steps, mesh=mesh, in_specs=in_specs, out_specs=out_specs, check_vma=False)
```

time: 132 us -> 127 us (0.962)
  matrix products: 29.9 us -> 0.89 us
  Pallas kernels: 0 us -> 28.4 us
  starting transfers between devices: 32.2 us -> 47.4 us
  blocking collectives: 38.3 us -> 24.6 us
  waiting for transfers between devices: 24.5 us -> 12.5 us
  local copies, waits for them, and re-layouts: 2.73 us -> 8.92 us
    dot_general x6 -> x1, matrix products: 29.9 us -> 0.89 us  [steps(): mix = pick @ got[:, n, :cols].astype(F32) @ pick.T]
    pallas_call x0 -> x6, Pallas kernels: none -> 28.4 us  [the longest x2 11.6 us: volume(): pl.pallas_call(volume_kernel, out_shape=shape, in_specs=[vmem()] * 3, out...]
    all_to_all x4, waiting for transfers between devices: 21 us -> 0.01 us  [exchange(): return lax.all_to_all(blocks, axis, split_axis=0, concat_axis=0, tiled=True)]
    all_to_all x3 -> x2, blocking collectives: 38.3 us -> 24.6 us  [exchange(): return lax.all_to_all(blocks, axis, split_axis=0, concat_axis=0, tiled=True)]
    ppermute x2 -> x9, starting transfers between devices: 6.77 us -> 17.2 us  [the longest x7 11.3 us: steps(): lax.ppermute(block, 'col', [(i, (i + k) % cols) for i in range(cols)])]
    ppermute x2 -> x9, waiting for transfers between devices: 3.52 us -> 12.5 us  [the longest x2 7.85 us: steps(): piece = lax.ppermute(rounded, ('row', 'col'), turned(rows, cols))]
    all_to_all x4, starting transfers between devices: 25.5 us -> 30.2 us  [exchange(): return lax.all_to_all(blocks, axis, split_axis=0, concat_axis=0, tiled=True)]
    dynamic_slice x0 -> x1, local copies, waits for them, and re-layouts: none -> 2.6 us  [steps(): block = lax.dynamic_slice_in_dim(interp, (col + k & cols - 1) * ms, ms, 0)]
  transfers between devices with their start and end apart: 6 -> 13, of which waited for: 3 -> 4; matrix products, arithmetic and copies ran while one was open for 18% -> 4% of each run, Pallas kernels for 0% -> 16%
where the time goes in v2:
time: 127 us; the launch traced here: 126 us
  starting transfers between devices  47.4 us (37%)
  Pallas kernels  28.4 us (22%)
  blocking collectives  24.6 us (19%)
  waiting for transfers between devices  12.5 us (10%)
  local copies, waits for them, and re-layouts  8.92 us (7%)
  other arithmetic  2.37 us (2%)
    all_to_all x4, starting transfers between devices, exchange(): return lax.all_to_all(blocks, axis, split_axis=0, concat_axis=0, tiled=True)  30.2 us
    all_to_all x2, blocking collectives, exchange(): return lax.all_to_all(blocks, axis, split_axis=0, concat_axis=0, tiled=True)  24.6 us
    pallas_call x2, Pallas kernels, volume(): pl.pallas_call(volume_kernel, out_shape=shape, in_specs=[vmem()] * 3, out...  11.6 us
    ppermute x7, starting transfers between devices, steps(): lax.ppermute(block, 'col', [(i, (i + k) % cols) for i in range(cols)])  11.3 us
    pallas_call x2, Pallas kernels, applied(): pl.pallas_call(surface_kernel, out_shape=shape, in_specs=[vmem()] * 3, ou...  8.94 us
    pallas_call x2, Pallas kernels, faces(): pl.pallas_call(faces_kernel, out_shape=shape, in_specs=[pl.BlockSpec(memo...  7.89 us
    ppermute x2, waiting for transfers between devices, steps(): piece = lax.ppermute(rounded, ('row', 'col'), turned(rows, cols))  7.85 us
    ppermute x2, starting transfers between devices, steps(): piece = lax.ppermute(rounded, ('row', 'col'), turned(rows, cols))  5.88 us
  transfers between devices with their start and end apart: 13, of which 4 were waited for; matrix products, arithmetic and copies ran while one was open for 4% of the time, Pallas kernels for 16%

profile of v2, /device:TPU:1, one launch (start us, length us, event | category | flops | bytes accessed | tf_op | source)
XLA Modules:
  0.0 125.9 jit_solution(3758373253670051621)
XLA Ops:
  1.4 0.8 convert_element_type.25
  2.3 0.7 broadcast_in_dim.11
  3.0 6.8 %all-to-all-start = ((bf16[8,144,128]{2,1,0:T(8,128)(2,1)}), bf16[8,144,128]{2,1,0:T(8,128)(2,1)S(1)}, u32[]{:S(2)}, u32[]{:S(2)}) async-start(bf16[8,144,128]{2,1,0:T(8,128)(2,1)} %broadcast_in_dim.11), calls=%async_computation | async-start | bytes 589824 | tf_op jit(solution)/shard_map/all_to_all | solution.py:28
  9.8 2.6 %dynamic-slice_bitcast_fusion = (bf16[128,1024]{1,0:T(8,128)(2,1)S(1)}, bf16[128,1024]{1,0:T(8,128)(2,1)S(1)}, bf16[128,1024]{1,0:T(8,128)(2,1)}, bf16[128,1024]...) fusion(bf16[1,1024,1024]{2,1,0:T(8,128)(2,1)} %param.8, ...), kind=kLoop, calls=%fused_computation.4 | loop fusion | bytes 4194336 | tf_op jit(solution)/shard_map/dynamic_slice | solution.py:111
  12.4 1.6 %collective-permute-start.1 = (bf16[128,1024]{1,0:T(8,128)(2,1)S(1)}, bf16[128,1024]{1,0:T(8,128)(2,1)S(1)}, u32[]{:S(2)}, u32[]{:S(2)}) collective-permute-start(bf16[128,1024]{1,0:T(8,128)(2,1)S(1)} %get-tuple-element.9), channel_id=1, source_target_pairs={{0,1},{1,2},{2,3},{3,4},{4,5},{5,6},{6,7},{7,0},{8,9},{9,10},{10,1... | collective-permute-start | bytes 786440 | tf_op jit(solution)/shard_map/ppermute | solution.py:113
  14.0 1.2 collective-permute-start.2
  15.2 2.4 %collective-permute-start = (bf16[128,128]{1,0:T(8,128)(2,1)S(1)}, bf16[128,128]{1,0:T(8,128)(2,1)S(1)}, u32[]{:S(2)}, u32[]{:S(2)}) collective-permute-start(bf16[128,128]{1,0:T(8,128)(2,1)S(1)} %convert_element_type.25), channel_id=1, source_target_pairs={{0,0},{1,8},{2,16},{3,24},{4,32},{5,40},{6,48},{7,56},{8,64},{9,72... | collective-permute-start | bytes 98312 | tf_op jit(solution)/shard_map/ppermute | solution.py:128
  17.6 4.3 %collective-permute-done = bf16[128,128]{1,0:T(8,128)(2,1)S(1)} collective-permute-done((bf16[128,128]{1,0:T(8,128)(2,1)S(1)}, bf16[128,128]{1,0:T(8,128)(2,1)S(1)}, u32[]{:S(2)}, u32[]{:S(2)}) %collective-permute-start) | collective-permute-done | bytes 32800 | tf_op jit(solution)/shard_map/ppermute | solution.py:128
  22.0 0.9 broadcast_in_dim.24
  22.9 9.6 %all-to-all-start.1 = ((bf16[16,128,128]{2,1,0:T(8,128)(2,1)}), bf16[16,128,128]{2,1,0:T(8,128)(2,1)S(1)}, u32[]{:S(2)}, u32[]{:S(2)}) async-start(bf16[16,128,128]{2,1,0:T(8,128)(2,1)} %broadcast_in_dim.24), calls=%async_computation.1 | async-start | bytes 1048576 | tf_op jit(solution)/shard_map/all_to_all | solution.py:28
  32.4 2.3 %collective-permute-start.3 = (bf16[128,1024]{1,0:T(8,128)(2,1)}, bf16[128,1024]{1,0:T(8,128)(2,1)S(1)}, u32[]{:S(2)}, u32[]{:S(2)}) collective-permute-start(bf16[128,1024]{1,0:T(8,128)(2,1)} %get-tuple-element.7), channel_id=1, source_target_pairs={{0,3},{1,4},{2,5},{3,6},{4,7},{5,0},{6,1},{7,2},{8,11},{9,12},{10,... | collective-permute-start | bytes 786440 | tf_op jit(solution)/shard_map/ppermute | solution.py:113
  34.8 1.5 %collective-permute-start.4 = (bf16[128,1024]{1,0:T(8,128)(2,1)}, bf16[128,1024]{1,0:T(8,128)(2,1)S(1)}, u32[]{:S(2)}, u32[]{:S(2)}) collective-permute-start(bf16[128,1024]{1,0:T(8,128)(2,1)} %get-tuple-element.6), channel_id=1, source_target_pairs={{0,4},{1,5},{2,6},{3,7},{4,0},{5,1},{6,2},{7,3},{8,12},{9,13},{10,... | collective-permute-start | bytes 786440 | tf_op jit(solution)/shard_map/ppermute | solution.py:113
  36.2 1.5 %collective-permute-start.5 = (bf16[128,1024]{1,0:T(8,128)(2,1)S(1)}, bf16[128,1024]{1,0:T(8,128)(2,1)S(1)}, u32[]{:S(2)}, u32[]{:S(2)}) collective-permute-start(bf16[128,1024]{1,0:T(8,128)(2,1)S(1)} %get-tuple-element.5), channel_id=1, source_target_pairs={{0,5},{1,6},{2,7},{3,0},{4,1},{5,2},{6,3},{7,4},{8,13},{9,14},{10,... | collective-permute-start | bytes 786440 | tf_op jit(solution)/shard_map/ppermute | solution.py:113
  37.7 3.3 %collective-permute-start.7 = (bf16[128,1024]{1,0:T(8,128)(2,1)S(1)}, bf16[128,1024]{1,0:T(8,128)(2,1)S(1)}, u32[]{:S(2)}, u32[]{:S(2)}) collective-permute-start(bf16[128,1024]{1,0:T(8,128)(2,1)S(1)} %get-tuple-element.4), channel_id=1, source_target_pairs={{0,7},{1,0},{2,1},{3,2},{4,3},{5,4},{6,5},{7,6},{8,15},{9,8},{10,9... | collective-permute-start | bytes 786440 | tf_op jit(solution)/shard_map/ppermute | solution.py:113
  41.7 5.8 %volume.2.prior_ref = f32[1024,128]{1,0:T(8,128)} custom-call(bf16[1024,1024]{1,0:T(8,128)(2,1)} %bitcast.30, bf16[1024,1024]{1,0:T(8,128)(2,1)} %bitcast.32, bf16[1024,128]{1,0:T(8,128)(2,1)} %bitcast.34), custom_call_target="tpu_custom_call" | custom-call | tf_op jit(solution)/shard_map/volume/pallas_call | solution.py:76
  47.5 0.9 fusion.refs_0_
  48.4 0.8 copy-done.1
  49.2 4.5 %applied.2.refs_1_ = f32[1024,128]{1,0:T(8,128)} custom-call(f32[1024,128]{1,0:T(8,128)} %volume.2.prior_ref, bf16[1024,2048]{1,0:T(8,128)(2,1)} %surface_ref.3, bf16[2048,128]{1,0:T(8,128)(2,1)} %bitcast.38), custom_call_target="tpu_custom_call" | custom-call | tf_op jit(solution)/shard_map/applied/pallas_call | solution.py:83
  53.8 3.8 %collective-permute-done.6.refs_9_ = bf16[128,1024]{1,0:T(8,128)(2,1)S(1)} collective-permute-done((bf16[128,1024]{1,0:T(8,128)(2,1)S(1)}, bf16[128,1024]{1,0:T(8,128)(2,1)S(1)}, u32[]{:S(2)}, u32[]{:S(2)}) %collective-permute-start.6) | collective-permute-done | bytes 262176 | tf_op jit(solution)/shard_map/ppermute | solution.py:113
  57.6 0.9 collective-permute-done.7.refs_10_
  59.2 3.9 %faces.2 = bf16[1024,128]{1,0:T(8,128)(2,1)} custom-call(f32[8,8]{1,0:T(8,128)} %fusion.refs_0_, f32[1024,128]{1,0:T(8,128)} %applied.2.refs_1_, bf16[1024,128]{1,0:T(8,128)(2,1)} %bitcast.35, bf16[128,1024]{1,0:T(8,128)(2,1)} %get-tuple-element.10.refs_3_, bf16[128,1024]{1,0:T(8,128)(2,1)} %copy-done.3, bf16[128,1024]{1,0:T(8,128)(2,1)} %copy-done.4, ...), custom_call_target="tpu_custom_call" | custom-call | tf_op jit(solution)/shard_map/faces/pallas_call | solution.py:90
  63.1 11.9 %all_to_all.30 = bf16[8,128,128]{2,1,0:T(8,128)(2,1)S(1)} all-to-all(bf16[8,128,128]{2,1,0:T(8,128)(2,1)} %bitcast.40), channel_id=1, replica_groups=mesh['row'=16,'col'=8] {'col'}, dimensions={0} | all-to-all | bytes 524288 | tf_op jit(solution)/shard_map/all_to_all | solution.py:28
  75.7 4.4 %all-to-all-start.3 = ((bf16[8,128,128]{2,1,0:T(8,128)(2,1)}), bf16[8,128,128]{2,1,0:T(8,128)(2,1)S(1)}, u32[]{:S(2)}, u32[]{:S(2)}) async-start(bf16[8,128,128]{2,1,0:T(8,128)(2,1)} %broadcast_in_dim.25), calls=%async_computation.3 | async-start | bytes 524288 | tf_op jit(solution)/shard_map/all_to_all | solution.py:28
  80.1 3.5 %collective-permute-start.8 = (bf16[128,128]{1,0:T(8,128)(2,1)S(1)}, bf16[128,128]{1,0:T(8,128)(2,1)S(1)}, u32[]{:S(2)}, u32[]{:S(2)}) collective-permute-start(bf16[128,128]{1,0:T(8,128)(2,1)S(1)} %fusion.5), channel_id=1, source_target_pairs={{0,0},{1,8},{2,16},{3,24},{4,32},{5,40},{6,48},{7,56},{8,64},{9,72... | collective-permute-start | bytes 98312 | tf_op jit(solution)/shard_map/ppermute | solution.py:128
  83.6 3.5 %collective-permute-done.8 = bf16[128,128]{1,0:T(8,128)(2,1)S(1)} collective-permute-done((bf16[128,128]{1,0:T(8,128)(2,1)S(1)}, bf16[128,128]{1,0:T(8,128)(2,1)S(1)}, u32[]{:S(2)}, u32[]{:S(2)}) %collective-permute-start.8) | collective-permute-done | bytes 32800 | tf_op jit(solution)/shard_map/ppermute | solution.py:128
  87.1 0.9 broadcast_in_dim.26
  88.0 9.4 %all-to-all-start.4 = ((bf16[16,128,128]{2,1,0:T(8,128)(2,1)}), bf16[16,128,128]{2,1,0:T(8,128)(2,1)S(1)}, u32[]{:S(2)}, u32[]{:S(2)}) async-start(bf16[16,128,128]{2,1,0:T(8,128)(2,1)} %broadcast_in_dim.26), calls=%async_computation.4 | async-start | bytes 1048576 | tf_op jit(solution)/shard_map/all_to_all | solution.py:28
  97.5 5.8 %volume.3.refs_1_ = f32[1024,128]{1,0:T(8,128)} custom-call(bf16[1024,1024]{1,0:T(8,128)(2,1)} %bitcast.31, bf16[1024,1024]{1,0:T(8,128)(2,1)} %bitcast.33, bf16[1024,128]{1,0:T(8,128)(2,1)} %bitcast.36), custom_call_target="tpu_custom_call" | custom-call | tf_op jit(solution)/shard_map/volume/pallas_call | solution.py:76
  103.3 4.0 %faces.3.prior_ref = f32[1024,128]{1,0:T(8,128)} custom-call(f32[8,8]{1,0:T(8,128)} %fusion.refs_0_, f32[1024,128]{1,0:T(8,128)} %volume.3.refs_1_, bf16[1024,128]{1,0:T(8,128)(2,1)} %bitcast.37, bf16[128,1024]{1,0:T(8,128)(2,1)} %get-tuple-element.10.refs_3_, bf16[128,1024]{1,0:T(8,128)(2,1)} %copy-done.3, bf16[128,1024]{1,0:T(8,128)(2,1)} %copy-done.4, ...), custom_call_target="tpu_custom_call" | custom-call | tf_op jit(solution)/shard_map/faces/pallas_call | solution.py:90
  107.3 0.8 copy-done.2
  108.1 4.4 %applied.3 = bf16[1024,128]{1,0:T(8,128)(2,1)} custom-call(f32[1024,128]{1,0:T(8,128)} %faces.3.prior_ref, bf16[1024,2048]{1,0:T(8,128)(2,1)} %surface_ref.3, bf16[2048,128]{1,0:T(8,128)(2,1)} %bitcast.39), custom_call_target="tpu_custom_call" | custom-call | tf_op jit(solution)/shard_map/applied/pallas_call | solution.py:83
  112.5 12.7 %all_to_all.31 = bf16[8,128,128]{2,1,0:T(8,128)(2,1)S(1)} all-to-all(bf16[8,128,128]{2,1,0:T(8,128)(2,1)} %bitcast.41), channel_id=1, replica_groups=mesh['row'=16,'col'=8] {'col'}, dimensions={0} | all-to-all | bytes 524288 | tf_op jit(solution)/shard_map/all_to_all | solution.py:28
  (43 shorter events, 3.7 us)
Async XLA Ops:
  3.0 19.0 %all-to-all-start = ((bf16[8,144,128]{2,1,0:T(8,128)(2,1)}), bf16[8,144,128]{2,1,0:T(8,128)(2,1)S(1)}, u32[]{:S(2)}, u32[]{:S(2)}) async-start(bf16[8,144,128]{2,1,0:T(8,128)(2,1)} %broadcast_in_dim.11), calls=%async_computation | async-start | bytes 589824 | tf_op jit(solution)/shard_map/all_to_all | solution.py:28
  12.4 25.3 %collective-permute-start.1 = (bf16[128,1024]{1,0:T(8,128)(2,1)S(1)}, bf16[128,1024]{1,0:T(8,128)(2,1)S(1)}, u32[]{:S(2)}, u32[]{:S(2)}) collective-permute-start(bf16[128,1024]{1,0:T(8,128)(2,1)S(1)} %get-tuple-element.9), channel_id=1, source_target_pairs={{0,1},{1,2},{2,3},{3,4},{4,5},{5,6},{6,7},{7,0},{8,9},{9,10},{10,1... | collective-permute-start | bytes 786440 | tf_op jit(solution)/shard_map/ppermute | solution.py:113
  14.0 23.7 %collective-permute-start.2 = (bf16[128,1024]{1,0:T(8,128)(2,1)S(1)}, bf16[128,1024]{1,0:T(8,128)(2,1)S(1)}, u32[]{:S(2)}, u32[]{:S(2)}) collective-permute-start(bf16[128,1024]{1,0:T(8,128)(2,1)S(1)} %get-tuple-element.8), channel_id=1, source_target_pairs={{0,2},{1,3},{2,4},{3,5},{4,6},{5,7},{6,0},{7,1},{8,10},{9,11},{10,... | collective-permute-start | bytes 786440 | tf_op jit(solution)/shard_map/ppermute | solution.py:113
  15.2 6.7 %collective-permute-start = (bf16[128,128]{1,0:T(8,128)(2,1)S(1)}, bf16[128,128]{1,0:T(8,128)(2,1)S(1)}, u32[]{:S(2)}, u32[]{:S(2)}) collective-permute-start(bf16[128,128]{1,0:T(8,128)(2,1)S(1)} %convert_element_type.25), channel_id=1, source_target_pairs={{0,0},{1,8},{2,16},{3,24},{4,32},{5,40},{6,48},{7,56},{8,64},{9,72... | collective-permute-start | bytes 98312 | tf_op jit(solution)/shard_map/ppermute | solution.py:128
  22.9 25.6 %all-to-all-start.1 = ((bf16[16,128,128]{2,1,0:T(8,128)(2,1)}), bf16[16,128,128]{2,1,0:T(8,128)(2,1)S(1)}, u32[]{:S(2)}, u32[]{:S(2)}) async-start(bf16[16,128,128]{2,1,0:T(8,128)(2,1)} %broadcast_in_dim.24), calls=%async_computation.1 | async-start | bytes 1048576 | tf_op jit(solution)/shard_map/all_to_all | solution.py:28
  32.4 21.3 %collective-permute-start.3 = (bf16[128,1024]{1,0:T(8,128)(2,1)}, bf16[128,1024]{1,0:T(8,128)(2,1)S(1)}, u32[]{:S(2)}, u32[]{:S(2)}) collective-permute-start(bf16[128,1024]{1,0:T(8,128)(2,1)} %get-tuple-element.7), channel_id=1, source_target_pairs={{0,3},{1,4},{2,5},{3,6},{4,7},{5,0},{6,1},{7,2},{8,11},{9,12},{10,... | collective-permute-start | bytes 786440 | tf_op jit(solution)/shard_map/ppermute | solution.py:113
  34.8 19.0 %collective-permute-start.4 = (bf16[128,1024]{1,0:T(8,128)(2,1)}, bf16[128,1024]{1,0:T(8,128)(2,1)S(1)}, u32[]{:S(2)}, u32[]{:S(2)}) collective-permute-start(bf16[128,1024]{1,0:T(8,128)(2,1)} %get-tuple-element.6), channel_id=1, source_target_pairs={{0,4},{1,5},{2,6},{3,7},{4,0},{5,1},{6,2},{7,3},{8,12},{9,13},{10,... | collective-permute-start | bytes 786440 | tf_op jit(solution)/shard_map/ppermute | solution.py:113
  36.2 17.5 %collective-permute-start.5 = (bf16[128,1024]{1,0:T(8,128)(2,1)S(1)}, bf16[128,1024]{1,0:T(8,128)(2,1)S(1)}, u32[]{:S(2)}, u32[]{:S(2)}) collective-permute-start(bf16[128,1024]{1,0:T(8,128)(2,1)S(1)} %get-tuple-element.5), channel_id=1, source_target_pairs={{0,5},{1,6},{2,7},{3,0},{4,1},{5,2},{6,3},{7,4},{8,13},{9,14},{10,... | collective-permute-start | bytes 786440 | tf_op jit(solution)/shard_map/ppermute | solution.py:113
  37.7 9.8 %copy-start.3 = (bf16[128,1024]{1,0:T(8,128)(2,1)}, bf16[128,1024]{1,0:T(8,128)(2,1)S(1)}, u32[]{:S(2)}) copy-start(bf16[128,1024]{1,0:T(8,128)(2,1)S(1)} %collective-permute-done.1.refs_4_) | copy-start | bytes 786436
  37.7 19.9 %collective-permute-start.6 = (bf16[128,1024]{1,0:T(8,128)(2,1)S(1)}, bf16[128,1024]{1,0:T(8,128)(2,1)S(1)}, u32[]{:S(2)}, u32[]{:S(2)}) collective-permute-start(bf16[128,1024]{1,0:T(8,128)(2,1)S(1)} %get-tuple-element.11), channel_id=1, source_target_pairs={{0,6},{1,7},{2,0},{3,1},{4,2},{5,3},{6,4},{7,5},{8,14},{9,15},{10,... | collective-permute-start | bytes 786440 | tf_op jit(solution)/shard_map/ppermute | solution.py:113
  37.7 9.8 %copy-start.4 = (bf16[128,1024]{1,0:T(8,128)(2,1)}, bf16[128,1024]{1,0:T(8,128)(2,1)S(1)}, u32[]{:S(2)}) copy-start(bf16[128,1024]{1,0:T(8,128)(2,1)S(1)} %collective-permute-done.2.refs_5_) | copy-start | bytes 786436
  37.7 20.7 %collective-permute-start.7 = (bf16[128,1024]{1,0:T(8,128)(2,1)S(1)}, bf16[128,1024]{1,0:T(8,128)(2,1)S(1)}, u32[]{:S(2)}, u32[]{:S(2)}) collective-permute-start(bf16[128,1024]{1,0:T(8,128)(2,1)S(1)} %get-tuple-element.4), channel_id=1, source_target_pairs={{0,7},{1,0},{2,1},{3,2},{4,3},{5,4},{6,5},{7,6},{8,15},{9,8},{10,9... | collective-permute-start | bytes 786440 | tf_op jit(solution)/shard_map/ppermute | solution.py:113
  48.4 0.8 copy-start.1
  53.7 21.2 %copy-start.10 = (f32[128,128]{1,0:T(8,128)S(1)}, f32[128,128]{1,0:T(8,128)}, u32[]{:S(2)}) copy-start(f32[128,128]{1,0:T(8,128)} %param.6) | copy-start | bytes 196612
  53.7 4.7 %copy-start.5 = (bf16[128,1024]{1,0:T(8,128)(2,1)}, bf16[128,1024]{1,0:T(8,128)(2,1)S(1)}, u32[]{:S(2)}) copy-start(bf16[128,1024]{1,0:T(8,128)(2,1)S(1)} %collective-permute-done.3.refs_6_) | copy-start | bytes 786436
  53.7 4.7 %copy-start.6 = (bf16[128,1024]{1,0:T(8,128)(2,1)}, bf16[128,1024]{1,0:T(8,128)(2,1)S(1)}, u32[]{:S(2)}) copy-start(bf16[128,1024]{1,0:T(8,128)(2,1)S(1)} %collective-permute-done.4.refs_7_) | copy-start | bytes 786436
  53.8 4.7 %copy-start.7 = (bf16[128,1024]{1,0:T(8,128)(2,1)}, bf16[128,1024]{1,0:T(8,128)(2,1)S(1)}, u32[]{:S(2)}) copy-start(bf16[128,1024]{1,0:T(8,128)(2,1)S(1)} %collective-permute-done.5.refs_8_) | copy-start | bytes 786436
  57.6 0.9 copy-start.8
  58.5 0.7 copy-start.9
  75.7 11.4 %all-to-all-start.3 = ((bf16[8,128,128]{2,1,0:T(8,128)(2,1)}), bf16[8,128,128]{2,1,0:T(8,128)(2,1)S(1)}, u32[]{:S(2)}, u32[]{:S(2)}) async-start(bf16[8,128,128]{2,1,0:T(8,128)(2,1)} %broadcast_in_dim.25), calls=%async_computation.3 | async-start | bytes 524288 | tf_op jit(solution)/shard_map/all_to_all | solution.py:28
  80.1 7.0 %collective-permute-start.8 = (bf16[128,128]{1,0:T(8,128)(2,1)S(1)}, bf16[128,128]{1,0:T(8,128)(2,1)S(1)}, u32[]{:S(2)}, u32[]{:S(2)}) collective-permute-start(bf16[128,128]{1,0:T(8,128)(2,1)S(1)} %fusion.5), channel_id=1, source_target_pairs={{0,0},{1,8},{2,16},{3,24},{4,32},{5,40},{6,48},{7,56},{8,64},{9,72... | collective-permute-start | bytes 98312 | tf_op jit(solution)/shard_map/ppermute | solution.py:128
  87.1 10.4 %copy-start = (bf16[8,128,128]{2,1,0:T(8,128)(2,1)}, bf16[8,128,128]{2,1,0:T(8,128)(2,1)S(1)}, u32[]{:S(2)}) copy-start(bf16[8,128,128]{2,1,0:T(8,128)(2,1)S(1)} %all-to-all-done.3) | copy-start | bytes 786436
  88.0 19.3 %all-to-all-start.4 = ((bf16[16,128,128]{2,1,0:T(8,128)(2,1)}), bf16[16,128,128]{2,1,0:T(8,128)(2,1)S(1)}, u32[]{:S(2)}, u32[]{:S(2)}) async-start(bf16[16,128,128]{2,1,0:T(8,128)(2,1)} %broadcast_in_dim.26), calls=%async_computation.4 | async-start | bytes 1048576 | tf_op jit(solution)/shard_map/all_to_all | solution.py:28
  107.3 0.8 copy-start.2

commit v3 on v2

--- a/solution.py
+++ b/solution.py
@@ -14,6 +14,8 @@
 
 BF = jnp.bfloat16
 F32 = jnp.float32
+
+PARAMS = pltpu.CompilerParams(vmem_limit_bytes=16 * 2**20)
 
 
 def dot(a, b):
@@ -74,14 +76,14 @@
 def volume(interp, dtn, group_block):
     shape = jax.ShapeDtypeStruct(group_block.shape, F32)
     return pl.pallas_call(
-        volume_kernel, out_shape=shape, in_specs=[vmem()] * 3, out_specs=vmem(), name="volume"
+        volume_kernel, out_shape=shape, in_specs=[vmem()] * 3, out_specs=vmem(), compiler_params=PARAMS, name="volume"
     )(interp, dtn, group_block)
 
 
 def applied(prior, surface, column_block, dtype):
     shape = jax.ShapeDtypeStruct(prior.shape, dtype)
     return pl.pallas_call(
-        surface_kernel, out_shape=shape, in_specs=[vmem()] * 3, out_specs=vmem(), name="applied"
+        surface_kernel, out_shape=shape, in_specs=[vmem()] * 3, out_specs=vmem(), compiler_params=PARAMS, name="applied"
     )(prior, surface, column_block)
 
 
@@ -92,6 +94,7 @@
         out_shape=shape,
         in_specs=[pl.BlockSpec(memory_space=pltpu.SMEM)] + [vmem()] * (2 + len(slices)),
         out_specs=vmem(),
+        compiler_params=PARAMS,
         name="faces",
     )(mix, prior, group_block, *slices)
 

time: 127 us -> 123 us (0.969)
  Pallas kernels: 28.4 us -> 14.7 us
  local copies, waits for them, and re-layouts: 8.92 us -> 15 us
  waiting for transfers between devices: 12.5 us -> 16.8 us
    pallas_call x2, Pallas kernels: 11.6 us -> 5.55 us  [volume(): pl.pallas_call(volume_kernel, out_shape=shape, in_specs=[vmem()] * 3, out...]
    unnamed x22 -> x20, local copies, waits for them, and re-layouts: 2.31 us -> 8.26 us
    pallas_call x2, Pallas kernels: 8.94 us -> 3.6 us  [applied(): pl.pallas_call(surface_kernel, out_shape=shape, in_specs=[vmem()] * 3, ou...]
    ppermute x7, waiting for transfers between devices: 4.69 us -> 7.08 us  [steps(): lax.ppermute(block, 'col', [(i, (i + k) % cols) for i in range(cols)])]
    pallas_call x2, Pallas kernels: 7.89 us -> 5.53 us  [faces(): pl.pallas_call(faces_kernel, out_shape=shape, in_specs=[pl.BlockSpec(memo...]
    all_to_all x4, waiting for transfers between devices: 0.01 us -> 1.84 us  [exchange(): return lax.all_to_all(blocks, axis, split_axis=0, concat_axis=0, tiled=True)]
  transfers between devices with their start and end apart: 13 -> 13, of which waited for: 4 -> 6; matrix products, arithmetic and copies ran while one was open for 4% -> 4% of each run, Pallas kernels for 16% -> 9%
where the time goes in v3:
time: 123 us; the launch traced here: 122 us
  starting transfers between devices  47.4 us (39%)
  blocking collectives  24.8 us (20%)
  waiting for transfers between devices  16.8 us (14%)
  local copies, waits for them, and re-layouts  15 us (12%)
  Pallas kernels  14.7 us (12%)
  other arithmetic  2.37 us (2%)
    all_to_all x4, starting transfers between devices, exchange(): return lax.all_to_all(blocks, axis, split_axis=0, concat_axis=0, tiled=True)  30.2 us
    all_to_all x2, blocking collectives, exchange(): return lax.all_to_all(blocks, axis, split_axis=0, concat_axis=0, tiled=True)  24.8 us
    ppermute x7, starting transfers between devices, steps(): lax.ppermute(block, 'col', [(i, (i + k) % cols) for i in range(cols)])  11.4 us
    unnamed x20, local copies, waits for them, and re-layouts  8.26 us
    ppermute x2, waiting for transfers between devices, steps(): piece = lax.ppermute(rounded, ('row', 'col'), turned(rows, cols))  7.89 us
    ppermute x7, waiting for transfers between devices, steps(): lax.ppermute(block, 'col', [(i, (i + k) % cols) for i in range(cols)])  7.08 us
    ppermute x2, starting transfers between devices, steps(): piece = lax.ppermute(rounded, ('row', 'col'), turned(rows, cols))  5.84 us
    pallas_call x2, Pallas kernels, volume(): pl.pallas_call(volume_kernel, out_shape=shape, in_specs=[vmem()] * 3, out...  5.55 us
  transfers between devices with their start and end apart: 13, of which 6 were waited for; matrix products, arithmetic and copies ran while one was open for 4% of the time, Pallas kernels for 9%

profile of v3, /device:TPU:1, one launch (start us, length us, event | category | flops | bytes accessed | tf_op | source)
XLA Modules:
  0.0 122.1 jit_solution(17643851440099660153)
XLA Ops:
  3.0 6.8 %all-to-all-start = ((bf16[8,144,128]{2,1,0:T(8,128)(2,1)}), bf16[8,144,128]{2,1,0:T(8,128)(2,1)S(1)}, u32[]{:S(2)}, u32[]{:S(2)}) async-start(bf16[8,144,128]{2,1,0:T(8,128)(2,1)} %broadcast_in_dim.11), calls=%async_computation | async-start | bytes 589824 | tf_op jit(solution)/shard_map/all_to_all | solution.py:30
  9.8 2.7 %dynamic-slice_bitcast_fusion = (bf16[128,1024]{1,0:T(8,128)(2,1)}, bf16[128,1024]{1,0:T(8,128)(2,1)}, bf16[128,1024]{1,0:T(8,128)(2,1)}, bf16[128,1024]{1,0:T(8...) fusion(bf16[1,1024,1024]{2,1,0:T(8,128)(2,1)} %param.8, ...), kind=kLoop, calls=%fused_computation.4 | loop fusion | bytes 4194336 | tf_op jit(solution)/shard_map/dynamic_slice | solution.py:114
  12.5 1.6 %collective-permute-start.1 = (bf16[128,1024]{1,0:T(8,128)(2,1)}, bf16[128,1024]{1,0:T(8,128)(2,1)S(1)}, u32[]{:S(2)}, u32[]{:S(2)}) collective-permute-start(bf16[128,1024]{1,0:T(8,128)(2,1)} %get-tuple-element.9), channel_id=1, source_target_pairs={{0,1},{1,2},{2,3},{3,4},{4,5},{5,6},{6,7},{7,0},{8,9},{9,10},{10,1... | collective-permute-start | bytes 786440 | tf_op jit(solution)/shard_map/ppermute | solution.py:116
  14.1 1.2 collective-permute-start.2
  15.3 2.4 %collective-permute-start = (bf16[128,128]{1,0:T(8,128)(2,1)S(1)}, bf16[128,128]{1,0:T(8,128)(2,1)S(1)}, u32[]{:S(2)}, u32[]{:S(2)}) collective-permute-start(bf16[128,128]{1,0:T(8,128)(2,1)S(1)} %convert_element_type.25), channel_id=1, source_target_pairs={{0,0},{1,8},{2,16},{3,24},{4,32},{5,40},{6,48},{7,56},{8,64},{9,72... | collective-permute-start | bytes 98312 | tf_op jit(solution)/shard_map/ppermute | solution.py:131
  17.7 4.3 %collective-permute-done = bf16[128,128]{1,0:T(8,128)(2,1)S(1)} collective-permute-done((bf16[128,128]{1,0:T(8,128)(2,1)S(1)}, bf16[128,128]{1,0:T(8,128)(2,1)S(1)}, u32[]{:S(2)}, u32[]{:S(2)}) %collective-permute-start) | collective-permute-done | bytes 32800 | tf_op jit(solution)/shard_map/ppermute | solution.py:131
  22.0 0.9 broadcast_in_dim.24
  22.9 9.6 %all-to-all-start.1 = ((bf16[16,128,128]{2,1,0:T(8,128)(2,1)}), bf16[16,128,128]{2,1,0:T(8,128)(2,1)}, u32[]{:S(2)}, u32[]{:S(2)}) async-start(bf16[16,128,128]{2,1,0:T(8,128)(2,1)} %broadcast_in_dim.24), calls=%async_computation.1 | async-start | bytes 1048576 | tf_op jit(solution)/shard_map/all_to_all | solution.py:30
  32.6 2.6 %collective-permute-start.3 = (bf16[128,1024]{1,0:T(8,128)(2,1)}, bf16[128,1024]{1,0:T(8,128)(2,1)}, u32[]{:S(2)}, u32[]{:S(2)}) collective-permute-start(bf16[128,1024]{1,0:T(8,128)(2,1)} %get-tuple-element.7), channel_id=1, source_target_pairs={{0,3},{1,4},{2,5},{3,6},{4,7},{5,0},{6,1},{7,2},{8,11},{9,12},{10,... | collective-permute-start | bytes 786440 | tf_op jit(solution)/shard_map/ppermute | solution.py:116
  35.1 1.3 %collective-permute-start.4 = (bf16[128,1024]{1,0:T(8,128)(2,1)}, bf16[128,1024]{1,0:T(8,128)(2,1)}, u32[]{:S(2)}, u32[]{:S(2)}) collective-permute-start(bf16[128,1024]{1,0:T(8,128)(2,1)} %get-tuple-element.6), channel_id=1, source_target_pairs={{0,4},{1,5},{2,6},{3,7},{4,0},{5,1},{6,2},{7,3},{8,12},{9,13},{10,... | collective-permute-start | bytes 786440 | tf_op jit(solution)/shard_map/ppermute | solution.py:116
  36.4 1.5 %collective-permute-start.5 = (bf16[128,1024]{1,0:T(8,128)(2,1)}, bf16[128,1024]{1,0:T(8,128)(2,1)}, u32[]{:S(2)}, u32[]{:S(2)}) collective-permute-start(bf16[128,1024]{1,0:T(8,128)(2,1)} %get-tuple-element.5), channel_id=1, source_target_pairs={{0,5},{1,6},{2,7},{3,0},{4,1},{5,2},{6,3},{7,4},{8,13},{9,14},{10,... | collective-permute-start | bytes 786440 | tf_op jit(solution)/shard_map/ppermute | solution.py:116
  38.5 3.3 %collective-permute-start.7 = (bf16[128,1024]{1,0:T(8,128)(2,1)}, bf16[128,1024]{1,0:T(8,128)(2,1)}, u32[]{:S(2)}, u32[]{:S(2)}) collective-permute-start(bf16[128,1024]{1,0:T(8,128)(2,1)} %get-tuple-element.4), channel_id=1, source_target_pairs={{0,7},{1,0},{2,1},{3,2},{4,3},{5,4},{6,5},{7,6},{8,15},{9,8},{10,9... | collective-permute-start | bytes 786440 | tf_op jit(solution)/shard_map/ppermute | solution.py:116
  41.9 1.6 %copy-done.3 = bf16[1,1024,1024]{2,1,0:T(8,128)(2,1)S(1)} copy-done((bf16[1,1024,1024]{2,1,0:T(8,128)(2,1)S(1)}, bf16[1,1024,1024]{2,1,0:T(8,128)(2,1)}, u32[]{:S(2)}) %copy-start.3) | copy-done | bytes 2097176
  43.4 2.8 %volume.2.prior_ref = f32[1024,128]{1,0:T(8,128)S(1)} custom-call(bf16[1024,1024]{1,0:T(8,128)(2,1)S(1)} %bitcast.30, bf16[1024,1024]{1,0:T(8,128)(2,1)S(1)} %bitcast.32, bf16[1024,128]{1,0:T(8,128)(2,1)S(1)} %bitcast.34), custom_call_target="tpu_custom_call" | custom-call | tf_op jit(solution)/shard_map/volume/pallas_call | solution.py:78
  47.3 2.2 %copy-done.1 = bf16[1024,2048]{1,0:T(8,128)(2,1)S(1)} copy-done((bf16[1024,2048]{1,0:T(8,128)(2,1)S(1)}, bf16[1024,2048]{1,0:T(8,128)(2,1)}, u32[]{:S(2)}) %copy-start.1) | copy-done | bytes 4194328
  49.5 2.3 %applied.2.refs_1_ = f32[1024,128]{1,0:T(8,128)S(1)} custom-call(f32[1024,128]{1,0:T(8,128)S(1)} %volume.2.prior_ref, bf16[1024,2048]{1,0:T(8,128)(2,1)S(1)} %copy-done.1, bf16[2048,128]{1,0:T(8,128)(2,1)} %bitcast.5.column_ref), custom_call_target="tpu_custom_call" | custom-call | tf_op jit(solution)/shard_map/applied/pallas_call | solution.py:85
  52.4 5.6 %collective-permute-done.6.refs_9_ = bf16[128,1024]{1,0:T(8,128)(2,1)} collective-permute-done((bf16[128,1024]{1,0:T(8,128)(2,1)}, bf16[128,1024]{1,0:T(8,128)(2,1)}, u32[]{:S(2)}, u32[]{:S(2)}) %collective-permute-start.6) | collective-permute-done | bytes 262176 | tf_op jit(solution)/shard_map/ppermute | solution.py:116
  58.0 0.9 collective-permute-done.7.refs_10_
  58.9 2.8 %faces.2 = bf16[1024,128]{1,0:T(8,128)(2,1)S(1)} custom-call(f32[8,8]{1,0:T(8,128)S(1)} %fusion.refs_0_, f32[1024,128]{1,0:T(8,128)S(1)} %applied.2.refs_1_, bf16[1024,128]{1,0:T(8,128)(2,1)S(1)} %bitcast.35, bf16[128,1024]{1,0:T(8,128)(2,1)S(1)} %get-tuple-element.10.refs_3_, bf16[128,1024]{1,0:T(8,128)(2,1)S(1)} %collective-permute-done.1.refs_4_, ...), custom_call_target="tpu_custom_call" | custom-call | tf_op jit(solution)/shard_map/faces/pallas_call | solution.py:92
  61.7 11.4 %all_to_all.30 = bf16[8,128,128]{2,1,0:T(8,128)(2,1)S(1)} all-to-all(bf16[8,128,128]{2,1,0:T(8,128)(2,1)S(1)} %bitcast.39), channel_id=1, replica_groups=mesh['row'=16,'col'=8] {'col'}, dimensions={0} | all-to-all | bytes 524288 | tf_op jit(solution)/shard_map/all_to_all | solution.py:30
  73.9 4.4 %all-to-all-start.3 = ((bf16[8,128,128]{2,1,0:T(8,128)(2,1)}), bf16[8,128,128]{2,1,0:T(8,128)(2,1)S(1)}, u32[]{:S(2)}, u32[]{:S(2)}) async-start(bf16[8,128,128]{2,1,0:T(8,128)(2,1)} %broadcast_in_dim.25), calls=%async_computation.3 | async-start | bytes 524288 | tf_op jit(solution)/shard_map/all_to_all | solution.py:30
  78.3 3.4 %collective-permute-start.8 = (bf16[128,128]{1,0:T(8,128)(2,1)S(1)}, bf16[128,128]{1,0:T(8,128)(2,1)S(1)}, u32[]{:S(2)}, u32[]{:S(2)}) collective-permute-start(bf16[128,128]{1,0:T(8,128)(2,1)S(1)} %fusion.5), channel_id=1, source_target_pairs={{0,0},{1,8},{2,16},{3,24},{4,32},{5,40},{6,48},{7,56},{8,64},{9,72... | collective-permute-start | bytes 98312 | tf_op jit(solution)/shard_map/ppermute | solution.py:131
  81.7 3.6 %collective-permute-done.8 = bf16[128,128]{1,0:T(8,128)(2,1)S(1)} collective-permute-done((bf16[128,128]{1,0:T(8,128)(2,1)S(1)}, bf16[128,128]{1,0:T(8,128)(2,1)S(1)}, u32[]{:S(2)}, u32[]{:S(2)}) %collective-permute-start.8) | collective-permute-done | bytes 32800 | tf_op jit(solution)/shard_map/ppermute | solution.py:131
  85.3 0.9 broadcast_in_dim.26
  86.2 9.4 %all-to-all-start.4 = ((bf16[16,128,128]{2,1,0:T(8,128)(2,1)}), bf16[16,128,128]{2,1,0:T(8,128)(2,1)S(1)}, u32[]{:S(2)}, u32[]{:S(2)}) async-start(bf16[16,128,128]{2,1,0:T(8,128)(2,1)} %broadcast_in_dim.26), calls=%async_computation.4 | async-start | bytes 1048576 | tf_op jit(solution)/shard_map/all_to_all | solution.py:30
  95.6 1.6 %copy-done.4 = bf16[1,1024,1024]{2,1,0:T(8,128)(2,1)S(1)} copy-done((bf16[1,1024,1024]{2,1,0:T(8,128)(2,1)S(1)}, bf16[1,1024,1024]{2,1,0:T(8,128)(2,1)}, u32[]{:S(2)}) %copy-start.4) | copy-done | bytes 2097176
  97.2 2.8 %volume.3.refs_1_ = f32[1024,128]{1,0:T(8,128)S(1)} custom-call(bf16[1024,1024]{1,0:T(8,128)(2,1)S(1)} %bitcast.31, bf16[1024,1024]{1,0:T(8,128)(2,1)S(1)} %bitcast.33, bf16[1024,128]{1,0:T(8,128)(2,1)S(1)} %bitcast.36), custom_call_target="tpu_custom_call" | custom-call | tf_op jit(solution)/shard_map/volume/pallas_call | solution.py:78
  100.0 2.8 %faces.3.prior_ref = f32[1024,128]{1,0:T(8,128)S(1)} custom-call(f32[8,8]{1,0:T(8,128)S(1)} %fusion.refs_0_, f32[1024,128]{1,0:T(8,128)S(1)} %volume.3.refs_1_, bf16[1024,128]{1,0:T(8,128)(2,1)S(1)} %bitcast.37, bf16[128,1024]{1,0:T(8,128)(2,1)S(1)} %get-tuple-element.10.refs_3_, bf16[128,1024]{1,0:T(8,128)(2,1)S(1)} %collective-permute-done.1.refs_4_, ...), custom_call_target="tpu_custom_call" | custom-call | tf_op jit(solution)/shard_map/faces/pallas_call | solution.py:92
  102.8 1.8 %all-to-all-done.4 = bf16[16,128,128]{2,1,0:T(8,128)(2,1)S(1)} async-done(((bf16[16,128,128]{2,1,0:T(8,128)(2,1)}), bf16[16,128,128]{2,1,0:T(8,128)(2,1)S(1)}, u32[]{:S(2)}, u32[]{:S(2)}) %all-to-all-start.4) | async-done | bytes 524320 | tf_op jit(solution)/shard_map/all_to_all | solution.py:30
  104.6 2.2 %copy-done.2 = bf16[1024,2048]{1,0:T(8,128)(2,1)S(1)} copy-done((bf16[1024,2048]{1,0:T(8,128)(2,1)S(1)}, bf16[1024,2048]{1,0:T(8,128)(2,1)}, u32[]{:S(2)}) %copy-start.2) | copy-done | bytes 4194328
  106.8 1.3 %applied.3 = bf16[1024,128]{1,0:T(8,128)(2,1)S(1)} custom-call(f32[1024,128]{1,0:T(8,128)S(1)} %faces.3.prior_ref, bf16[1024,2048]{1,0:T(8,128)(2,1)S(1)} %copy-done.2, bf16[2048,128]{1,0:T(8,128)(2,1)S(1)} %bitcast.38), custom_call_target="tpu_custom_call" | custom-call | tf_op jit(solution)/shard_map/applied/pallas_call | solution.py:85
  108.1 13.4 %all_to_all.31 = bf16[8,128,128]{2,1,0:T(8,128)(2,1)S(1)} all-to-all(bf16[8,128,128]{2,1,0:T(8,128)(2,1)S(1)} %bitcast.40), channel_id=1, replica_groups=mesh['row'=16,'col'=8] {'col'}, dimensions={0} | all-to-all | bytes 524288 | tf_op jit(solution)/shard_map/all_to_all | solution.py:30
  (41 shorter events, 6.2 us)
Async XLA Ops:
  3.0 19.0 %all-to-all-start = ((bf16[8,144,128]{2,1,0:T(8,128)(2,1)}), bf16[8,144,128]{2,1,0:T(8,128)(2,1)S(1)}, u32[]{:S(2)}, u32[]{:S(2)}) async-start(bf16[8,144,128]{2,1,0:T(8,128)(2,1)} %broadcast_in_dim.11), calls=%async_computation | async-start | bytes 589824 | tf_op jit(solution)/shard_map/all_to_all | solution.py:30
  12.5 29.4 %copy-start = (bf16[1,1024,1024]{2,1,0:T(8,128)(2,1)S(1)}, bf16[1,1024,1024]{2,1,0:T(8,128)(2,1)}, u32[]{:S(2)}) copy-start(bf16[1,1024,1024]{2,1,0:T(8,128)(2,1)} %param.8) | copy-start | bytes 6291460
  12.5 25.3 %collective-permute-start.1 = (bf16[128,1024]{1,0:T(8,128)(2,1)}, bf16[128,1024]{1,0:T(8,128)(2,1)S(1)}, u32[]{:S(2)}, u32[]{:S(2)}) collective-permute-start(bf16[128,1024]{1,0:T(8,128)(2,1)} %get-tuple-element.9), channel_id=1, source_target_pairs={{0,1},{1,2},{2,3},{3,4},{4,5},{5,6},{6,7},{7,0},{8,9},{9,10},{10,1... | collective-permute-start | bytes 786440 | tf_op jit(solution)/shard_map/ppermute | solution.py:116
  14.1 23.7 %collective-permute-start.2 = (bf16[128,1024]{1,0:T(8,128)(2,1)S(1)}, bf16[128,1024]{1,0:T(8,128)(2,1)S(1)}, u32[]{:S(2)}, u32[]{:S(2)}) collective-permute-start(bf16[128,1024]{1,0:T(8,128)(2,1)S(1)} %get-tuple-element.8), channel_id=1, source_target_pairs={{0,2},{1,3},{2,4},{3,5},{4,6},{5,7},{6,0},{7,1},{8,10},{9,11},{10,... | collective-permute-start | bytes 786440 | tf_op jit(solution)/shard_map/ppermute | solution.py:116
  15.3 6.7 %collective-permute-start = (bf16[128,128]{1,0:T(8,128)(2,1)S(1)}, bf16[128,128]{1,0:T(8,128)(2,1)S(1)}, u32[]{:S(2)}, u32[]{:S(2)}) collective-permute-start(bf16[128,128]{1,0:T(8,128)(2,1)S(1)} %convert_element_type.25), channel_id=1, source_target_pairs={{0,0},{1,8},{2,16},{3,24},{4,32},{5,40},{6,48},{7,56},{8,64},{9,72... | collective-permute-start | bytes 98312 | tf_op jit(solution)/shard_map/ppermute | solution.py:131
  22.0 19.8 %copy-start.8 = (bf16[8,144,128]{2,1,0:T(8,128)(2,1)}, bf16[8,144,128]{2,1,0:T(8,128)(2,1)S(1)}, u32[]{:S(2)}) copy-start(bf16[8,144,128]{2,1,0:T(8,128)(2,1)S(1)} %all-to-all-done) | copy-start | bytes 884740
  22.9 24.3 %all-to-all-start.1 = ((bf16[16,128,128]{2,1,0:T(8,128)(2,1)}), bf16[16,128,128]{2,1,0:T(8,128)(2,1)}, u32[]{:S(2)}, u32[]{:S(2)}) async-start(bf16[16,128,128]{2,1,0:T(8,128)(2,1)} %broadcast_in_dim.24), calls=%async_computation.1 | async-start | bytes 1048576 | tf_op jit(solution)/shard_map/all_to_all | solution.py:30
  32.6 19.3 %collective-permute-start.3 = (bf16[128,1024]{1,0:T(8,128)(2,1)}, bf16[128,1024]{1,0:T(8,128)(2,1)}, u32[]{:S(2)}, u32[]{:S(2)}) collective-permute-start(bf16[128,1024]{1,0:T(8,128)(2,1)} %get-tuple-element.7), channel_id=1, source_target_pairs={{0,3},{1,4},{2,5},{3,6},{4,7},{5,0},{6,1},{7,2},{8,11},{9,12},{10,... | collective-permute-start | bytes 786440 | tf_op jit(solution)/shard_map/ppermute | solution.py:116
  35.1 16.7 %collective-permute-start.4 = (bf16[128,1024]{1,0:T(8,128)(2,1)}, bf16[128,1024]{1,0:T(8,128)(2,1)}, u32[]{:S(2)}, u32[]{:S(2)}) collective-permute-start(bf16[128,1024]{1,0:T(8,128)(2,1)} %get-tuple-element.6), channel_id=1, source_target_pairs={{0,4},{1,5},{2,6},{3,7},{4,0},{5,1},{6,2},{7,3},{8,12},{9,13},{10,... | collective-permute-start | bytes 786440 | tf_op jit(solution)/shard_map/ppermute | solution.py:116
  36.4 16.1 %collective-permute-start.5 = (bf16[128,1024]{1,0:T(8,128)(2,1)}, bf16[128,1024]{1,0:T(8,128)(2,1)}, u32[]{:S(2)}, u32[]{:S(2)}) collective-permute-start(bf16[128,1024]{1,0:T(8,128)(2,1)} %get-tuple-element.5), channel_id=1, source_target_pairs={{0,5},{1,6},{2,7},{3,0},{4,1},{5,2},{6,3},{7,4},{8,13},{9,14},{10,... | collective-permute-start | bytes 786440 | tf_op jit(solution)/shard_map/ppermute | solution.py:116
  37.8 20.2 %collective-permute-start.6 = (bf16[128,1024]{1,0:T(8,128)(2,1)}, bf16[128,1024]{1,0:T(8,128)(2,1)}, u32[]{:S(2)}, u32[]{:S(2)}) collective-permute-start(bf16[128,1024]{1,0:T(8,128)(2,1)} %get-tuple-element.11), channel_id=1, source_target_pairs={{0,6},{1,7},{2,0},{3,1},{4,2},{5,3},{6,4},{7,5},{8,14},{9,15},{10,... | collective-permute-start | bytes 786440 | tf_op jit(solution)/shard_map/ppermute | solution.py:116
  37.8 0.7 copy-start.5
  38.5 20.4 %collective-permute-start.7 = (bf16[128,1024]{1,0:T(8,128)(2,1)}, bf16[128,1024]{1,0:T(8,128)(2,1)}, u32[]{:S(2)}, u32[]{:S(2)}) collective-permute-start(bf16[128,1024]{1,0:T(8,128)(2,1)} %get-tuple-element.4), channel_id=1, source_target_pairs={{0,7},{1,0},{2,1},{3,2},{4,3},{5,4},{6,5},{7,6},{8,15},{9,8},{10,9... | collective-permute-start | bytes 786440 | tf_op jit(solution)/shard_map/ppermute | solution.py:116
  41.9 1.6 %copy-start.3 = (bf16[1,1024,1024]{2,1,0:T(8,128)(2,1)S(1)}, bf16[1,1024,1024]{2,1,0:T(8,128)(2,1)}, u32[]{:S(2)}) copy-start(bf16[1,1024,1024]{2,1,0:T(8,128)(2,1)} %param.7) | copy-start | bytes 6291460
  47.3 2.2 %copy-start.1 = (bf16[1024,2048]{1,0:T(8,128)(2,1)S(1)}, bf16[1024,2048]{1,0:T(8,128)(2,1)}, u32[]{:S(2)}) copy-start(bf16[1024,2048]{1,0:T(8,128)(2,1)} %surface_ref.3) | copy-start | bytes 12582916
  49.5 9.5 %copy-start.6 = (bf16[128,1024]{1,0:T(8,128)(2,1)S(1)}, bf16[128,1024]{1,0:T(8,128)(2,1)}, u32[]{:S(2)}) copy-start(bf16[128,1024]{1,0:T(8,128)(2,1)} %copy-done.5) | copy-start | bytes 786436
  51.8 21.4 %copy-start.9 = (f32[128,128]{1,0:T(8,128)S(1)}, f32[128,128]{1,0:T(8,128)}, u32[]{:S(2)}) copy-start(f32[128,128]{1,0:T(8,128)} %param.6) | copy-start | bytes 196612
  73.9 11.4 %all-to-all-start.3 = ((bf16[8,128,128]{2,1,0:T(8,128)(2,1)}), bf16[8,128,128]{2,1,0:T(8,128)(2,1)S(1)}, u32[]{:S(2)}, u32[]{:S(2)}) async-start(bf16[8,128,128]{2,1,0:T(8,128)(2,1)} %broadcast_in_dim.25), calls=%async_computation.3 | async-start | bytes 524288 | tf_op jit(solution)/shard_map/all_to_all | solution.py:30
  78.3 7.0 %collective-permute-start.8 = (bf16[128,128]{1,0:T(8,128)(2,1)S(1)}, bf16[128,128]{1,0:T(8,128)(2,1)S(1)}, u32[]{:S(2)}, u32[]{:S(2)}) collective-permute-start(bf16[128,128]{1,0:T(8,128)(2,1)S(1)} %fusion.5), channel_id=1, source_target_pairs={{0,0},{1,8},{2,16},{3,24},{4,32},{5,40},{6,48},{7,56},{8,64},{9,72... | collective-permute-start | bytes 98312 | tf_op jit(solution)/shard_map/ppermute | solution.py:131
  86.2 18.4 %all-to-all-start.4 = ((bf16[16,128,128]{2,1,0:T(8,128)(2,1)}), bf16[16,128,128]{2,1,0:T(8,128)(2,1)S(1)}, u32[]{:S(2)}, u32[]{:S(2)}) async-start(bf16[16,128,128]{2,1,0:T(8,128)(2,1)} %broadcast_in_dim.26), calls=%async_computation.4 | async-start | bytes 1048576 | tf_op jit(solution)/shard_map/all_to_all | solution.py:30
  95.6 1.6 %copy-start.4 = (bf16[1,1024,1024]{2,1,0:T(8,128)(2,1)S(1)}, bf16[1,1024,1024]{2,1,0:T(8,128)(2,1)}, u32[]{:S(2)}) copy-start(bf16[1,1024,1024]{2,1,0:T(8,128)(2,1)} %param.7) | copy-start | bytes 6291460
  97.2 2.8 %copy-start.7 = (bf16[128,1024]{1,0:T(8,128)(2,1)S(1)}, bf16[128,1024]{1,0:T(8,128)(2,1)}, u32[]{:S(2)}) copy-start(bf16[128,1024]{1,0:T(8,128)(2,1)} %copy-done.5) | copy-start | bytes 786436
  104.6 2.2 %copy-start.2 = (bf16[1024,2048]{1,0:T(8,128)(2,1)S(1)}, bf16[1024,2048]{1,0:T(8,128)(2,1)}, u32[]{:S(2)}) copy-start(bf16[1024,2048]{1,0:T(8,128)(2,1)} %surface_ref.3) | copy-start | bytes 12582916

commit v4 on v3

v4 whole, which is shorter than its diff:
```python
import jax
import jax.numpy as jnp
from jax import lax
from jax.experimental import pallas as pl
from jax.experimental.pallas import tpu as pltpu
from jax.sharding import PartitionSpec as P


ITERS = 2
NADJ = 6

damping = 0.25
face_weight = 0.25

BF = jnp.bfloat16
F32 = jnp.float32

PARAMS = pltpu.CompilerParams(vmem_limit_bytes=16 * 2**20)


def dot(a, b):
    return jnp.dot(a, b, preferred_element_type=F32)


def dot_t(a, b):
    return lax.dot_general(a, b, (((0,), (0,)), ((), ())), preferred_element_type=F32)


def exchange(blocks, axis):
    return lax.all_to_all(blocks, axis, split_axis=0, concat_axis=0, tiled=True)


def copy_for_each(shard, axis):
    return exchange(jnp.broadcast_to(shard, (lax.axis_size(axis), *shard.shape)), axis)


def turned(rows, cols):
    per_col = rows // cols
    return [
        (r * cols + c, ((r % per_col) * cols + c) * cols + r // per_col)
        for r in range(rows)
        for c in range(cols)
    ]


def rotated(col, k, peers):
    return (col + k) & (peers - 1)


def grouped(got_ref, n):
    got = got_ref[:, :n]
    return got.reshape(got.shape[0] * n, got.shape[2])


def volume_kernel(interp_ref, dtn_ref, got_ref, *refs):
    peers = got_ref.shape[0]
    traces = dot(interp_ref[...], grouped(got_ref, interp_ref.shape[1] // peers)).astype(BF)
    response = dot(dtn_ref[...], traces).astype(BF)
    total = dot_t(interp_ref[...], response)
    if len(refs) == 2:
        total = total + refs[0][...]
    refs[-1][...] = total


def faces_kernel(col_ref, mix_ref, got_ref, *refs):
    peers = got_ref.shape[0]
    slice_refs, prior_refs = refs[:peers], refs[peers:-2]
    out_ref, traces_ref = refs[-2:]
    n = slice_refs[0].shape[1] // peers
    group = grouped(got_ref, n)
    for k in range(peers):
        traces_ref[rotated(col_ref[0], -k, peers)] = dot(slice_refs[k][...], group)
    total = prior_refs[0][...] if prior_refs else None
    for k in range(peers):
        s = rotated(col_ref[0], -k, peers)
        row = mix_ref[s, n : n + 16, :].astype(F32)[:1]
        mixed = None
        for p in range(peers):
            term = row[:, p : p + 1] * traces_ref[p]
            mixed = term if mixed is None else mixed + term
        term = dot_t(slice_refs[k][...], mixed.astype(BF))
        total = term if total is None else total + term
    out_ref[...] = total.astype(out_ref.dtype)


def surface_kernel(prior_ref, surface_ref, column_ref, out_ref):
    out_ref[...] = (prior_ref[...] + dot(surface_ref[...], column_ref[...])).astype(out_ref.dtype)


def vmem():
    return pl.BlockSpec(memory_space=pltpu.VMEM)


def cost(products, m, k, ne):
    return pl.CostEstimate(
        flops=2 * products * m * k * ne, bytes_accessed=2 * products * m * k, transcendentals=0
    )


def volume(interp, dtn, got, *prior):
    m, rb = interp.shape
    ne = got.shape[-1]
    return pl.pallas_call(
        volume_kernel,
        out_shape=jax.ShapeDtypeStruct((rb, ne), F32),
        in_specs=[vmem()] * (3 + len(prior)),
        out_specs=vmem(),
        compiler_params=PARAMS,
        cost_estimate=cost(3, m, rb, ne),
        name="volume",
    )(interp, dtn, got, *prior)


def applied(prior, surface, column_block, dtype):
    m, k = surface.shape
    return pl.pallas_call(
        surface_kernel,
        out_shape=jax.ShapeDtypeStruct(prior.shape, dtype),
        in_specs=[vmem()] * 3,
        out_specs=vmem(),
        compiler_params=PARAMS,
        cost_estimate=cost(1, m, k, prior.shape[1]),
        name="applied",
    )(prior, surface, column_block)


def faces(place, mix, got, slices, dtype, *prior):
    (ms, rb), ne = slices[0].shape, got.shape[-1]
    peers = len(slices)
    return pl.pallas_call(
        faces_kernel,
        out_shape=jax.ShapeDtypeStruct((rb, ne), dtype),
        in_specs=[pl.BlockSpec(memory_space=pltpu.SMEM)] + [vmem()] * (2 + peers + len(prior)),
        out_specs=vmem(),
        scratch_shapes=[pltpu.VMEM((peers, ms, ne), F32)],
        compiler_params=PARAMS,
        cost_estimate=cost(2, peers * ms, rb, ne),
        name="faces",
    )(place, mix, got, *slices, *prior)


def steps(surface, excitation, dtn_blocks, interp_blocks, adjacency):
    cols = lax.axis_size("col")
    rows = lax.axis_size("row")
    col = lax.axis_index("col")
    place = col.astype(jnp.int32)[None]
    dtn = dtn_blocks[0]
    interp = interp_blocks[0]
    ms = interp.shape[0] // cols
    n, ne = excitation.shape

    slices = []
    for k in range(cols):
        block = lax.dynamic_slice_in_dim(interp, rotated(col, k, cols) * ms, ms, 0)
        if k:
            block = lax.ppermute(block, "col", [(i, (i + k) % cols) for i in range(cols)])
        slices.append(block)

    adjacent = adjacency[0] & (cols - 1)
    owners = jnp.arange(ne, dtype=jnp.int32)
    counts = jnp.sum((adjacent[None, :] == owners[:, None]).astype(F32), axis=1)
    me = (owners == col).astype(F32)
    weights = (1.0 + face_weight * NADJ) * me - face_weight * counts
    extra = jnp.broadcast_to(weights.astype(BF)[None, :], (16, ne))

    current = excitation
    residual = excitation
    mix = None
    for sweep in range(ITERS):
        rounded = current.astype(BF)
        piece = lax.ppermute(rounded, ("row", "col"), turned(rows, cols))
        column_block = copy_for_each(piece, "row").reshape(rows * n, ne)
        sent = jnp.concatenate([rounded, extra], axis=0) if sweep == 0 else rounded
        got = copy_for_each(sent, "col")
        mix = got if mix is None else mix
        if sweep == 0:
            own = volume(interp, dtn, got)
            wide = applied(own, surface, column_block, F32)
            part = faces(place, mix, got, slices, BF, wide)
        else:
            wide = faces(place, mix, got, slices, F32)
            own = volume(interp, dtn, got, wide)
            part = applied(own, surface, column_block, BF)
        parts = exchange(part.reshape(cols, n, ne), "col")
        summed = jnp.sum(parts.astype(F32), axis=0)
        residual = excitation - current - summed
        current = current + damping * residual
    return (current, residual)


def solution(mesh):
    in_specs = (
        P("row", "col"),
        P(("row", "col"), None),
        P(("row", "col"), None, None),
        P(("row", "col"), None, None),
        P(("row", "col"), None),
    )
    out_specs = (P(("row", "col"), None), P(("row", "col"), None))
    return jax.shard_map(steps, mesh=mesh, in_specs=in_specs, out_specs=out_specs, check_vma=False)
```

time: 123 us -> 122 us (level)
  local copies, waits for them, and re-layouts: 15 us -> 11.4 us
  starting transfers between devices: 47.4 us -> 50.3 us
    ppermute x7, starting transfers between devices: 11.4 us -> 14.2 us  [steps(): lax.ppermute(block, 'col', [(i, (i + k) % cols) for i in range(cols)])]
    dynamic_slice x1, local copies, waits for them, and re-layouts: 2.68 us -> 1.11 us  [steps(): block = lax.dynamic_slice_in_dim(interp, rotated(col, k, cols) * ms, ms, 0)]
    unnamed x20 -> x24, local copies, waits for them, and re-layouts: 8.26 us -> 7.02 us
  transfers between devices with their start and end apart: 13 -> 13, of which waited for: 6 -> 8; matrix products, arithmetic and copies ran while one was open for 4% -> 1% of each run, Pallas kernels for 9% -> 9%
where the time goes in v4:
time: 122 us; the launch traced here: 121 us
  starting transfers between devices  50.3 us (41%)
  blocking collectives  25.4 us (21%)
  waiting for transfers between devices  15.7 us (13%)
  Pallas kernels  14.9 us (12%)
  local copies, waits for them, and re-layouts  11.4 us (9%)
  other arithmetic  2.51 us (2%)
    all_to_all x4, starting transfers between devices, exchange(): return lax.all_to_all(blocks, axis, split_axis=0, concat_axis=0, tiled=True)  29.9 us
    all_to_all x2, blocking collectives, exchange(): return lax.all_to_all(blocks, axis, split_axis=0, concat_axis=0, tiled=True)  25.4 us
    ppermute x7, starting transfers between devices, steps(): lax.ppermute(block, 'col', [(i, (i + k) % cols) for i in range(cols)])  14.2 us
    ppermute x2, waiting for transfers between devices, steps(): piece = lax.ppermute(rounded, ('row', 'col'), turned(rows, cols))  7.43 us
    unnamed x24, local copies, waits for them, and re-layouts  7.02 us
    ppermute x7, waiting for transfers between devices, steps(): lax.ppermute(block, 'col', [(i, (i + k) % cols) for i in range(cols)])  6.89 us
    ppermute x2, starting transfers between devices, steps(): piece = lax.ppermute(rounded, ('row', 'col'), turned(rows, cols))  6.29 us
    pallas_call x2, Pallas kernels, faces(): pl.pallas_call(faces_kernel, out_shape=jax.ShapeDtypeStruct((rb, ne), dty...  5.72 us
  transfers between devices with their start and end apart: 13, of which 8 were waited for; matrix products, arithmetic and copies ran while one was open for 1% of the time, Pallas kernels for 9%

profile of v4, /device:TPU:1, one launch (start us, length us, event | category | flops | bytes accessed | tf_op | source)
XLA Modules:
  0.0 121.1 jit_solution(7822733656612273318)
XLA Ops:
  3.2 6.8 %all-to-all-start = ((bf16[8,144,128]{2,1,0:T(8,128)(2,1)}), bf16[8,144,128]{2,1,0:T(8,128)(2,1)S(1)}, u32[]{:S(2)}, u32[]{:S(2)}) async-start(bf16[8,144,128]{2,1,0:T(8,128)(2,1)} %broadcast_in_dim.25), calls=%async_computation | async-start | bytes 589824 | tf_op jit(solution)/shard_map/all_to_all | solution.py:30
  10.0 3.1 %collective-permute-start.7 = (bf16[128,128]{1,0:T(8,128)(2,1)S(1)}, bf16[128,128]{1,0:T(8,128)(2,1)S(1)}, u32[]{:S(2)}, u32[]{:S(2)}) collective-permute-start(bf16[128,128]{1,0:T(8,128)(2,1)S(1)} %convert_element_type.23), channel_id=1, source_target_pairs={{0,0},{1,8},{2,16},{3,24},{4,32},{5,40},{6,48},{7,56},{8,64},{9,72... | collective-permute-start | bytes 98312 | tf_op jit(solution)/shard_map/ppermute | solution.py:171
  13.1 3.6 %collective-permute-done.7 = bf16[128,128]{1,0:T(8,128)(2,1)S(1)} collective-permute-done((bf16[128,128]{1,0:T(8,128)(2,1)S(1)}, bf16[128,128]{1,0:T(8,128)(2,1)S(1)}, u32[]{:S(2)}, u32[]{:S(2)}) %collective-permute-start.7) | collective-permute-done | bytes 32800 | tf_op jit(solution)/shard_map/ppermute | solution.py:171
  16.7 0.9 broadcast_in_dim.26
  17.6 9.5 %all-to-all-start.1 = ((bf16[16,128,128]{2,1,0:T(8,128)(2,1)}), bf16[16,128,128]{2,1,0:T(8,128)(2,1)}, u32[]{:S(2)}, u32[]{:S(2)}) async-start(bf16[16,128,128]{2,1,0:T(8,128)(2,1)} %broadcast_in_dim.26), calls=%async_computation.1 | async-start | bytes 1048576 | tf_op jit(solution)/shard_map/all_to_all | solution.py:30
  27.2 1.1 dynamic-slice_bitcast_fusion
  28.3 1.5 %collective-permute-start.6 = (bf16[128,1024]{1,0:T(8,128)(2,1)S(1)}, bf16[128,1024]{1,0:T(8,128)(2,1)S(1)}, u32[]{:S(2)}, u32[]{:S(2)}) collective-permute-start(bf16[128,1024]{1,0:T(8,128)(2,1)S(1)} %get-tuple-element.4), channel_id=1, source_target_pairs={{0,7},{1,0},{2,1},{3,2},{4,3},{5,4},{6,5},{7,6},{8,15},{9,8},{10,9... | collective-permute-start | bytes 786440 | tf_op jit(solution)/shard_map/ppermute | solution.py:156
  29.8 2.3 %collective-permute-start.5 = (bf16[128,1024]{1,0:T(8,128)(2,1)S(1)}, bf16[128,1024]{1,0:T(8,128)(2,1)S(1)}, u32[]{:S(2)}, u32[]{:S(2)}) collective-permute-start(bf16[128,1024]{1,0:T(8,128)(2,1)S(1)} %get-tuple-element.5), channel_id=1, source_target_pairs={{0,6},{1,7},{2,0},{3,1},{4,2},{5,3},{6,4},{7,5},{8,14},{9,15},{10,... | collective-permute-start | bytes 786440 | tf_op jit(solution)/shard_map/ppermute | solution.py:156
  32.8 1.4 %collective-permute-start.3 = (bf16[128,1024]{1,0:T(8,128)(2,1)}, bf16[128,1024]{1,0:T(8,128)(2,1)}, u32[]{:S(2)}, u32[]{:S(2)}) collective-permute-start(bf16[128,1024]{1,0:T(8,128)(2,1)} %get-tuple-element.7), channel_id=1, source_target_pairs={{0,4},{1,5},{2,6},{3,7},{4,0},{5,1},{6,2},{7,3},{8,12},{9,13},{10,... | collective-permute-start | bytes 786440 | tf_op jit(solution)/shard_map/ppermute | solution.py:156
  34.3 3.2 %collective-permute-start.2 = (bf16[128,1024]{1,0:T(8,128)(2,1)}, bf16[128,1024]{1,0:T(8,128)(2,1)}, u32[]{:S(2)}, u32[]{:S(2)}) collective-permute-start(bf16[128,1024]{1,0:T(8,128)(2,1)} %get-tuple-element.8), channel_id=1, source_target_pairs={{0,3},{1,4},{2,5},{3,6},{4,7},{5,0},{6,1},{7,2},{8,11},{9,12},{10,... | collective-permute-start | bytes 786440 | tf_op jit(solution)/shard_map/ppermute | solution.py:156
  37.4 1.8 %collective-permute-done.6.refs_7_ = bf16[128,1024]{1,0:T(8,128)(2,1)S(1)} collective-permute-done((bf16[128,1024]{1,0:T(8,128)(2,1)S(1)}, bf16[128,1024]{1,0:T(8,128)(2,1)S(1)}, u32[]{:S(2)}, u32[]{:S(2)}) %collective-permute-start.6) | collective-permute-done | bytes 262176 | tf_op jit(solution)/shard_map/ppermute | solution.py:156
  40.0 5.0 %collective-permute-start = (bf16[128,1024]{1,0:T(8,128)(2,1)}, bf16[128,1024]{1,0:T(8,128)(2,1)}, u32[]{:S(2)}, u32[]{:S(2)}) collective-permute-start(bf16[128,1024]{1,0:T(8,128)(2,1)} %get-tuple-element.10), channel_id=1, source_target_pairs={{0,1},{1,2},{2,3},{3,4},{4,5},{5,6},{6,7},{7,0},{8,9},{9,10},{10,1... | collective-permute-start | bytes 786440 | tf_op jit(solution)/shard_map/ppermute | solution.py:156
  45.0 2.8 %volume.2.prior_ref = f32[1024,128]{1,0:T(8,128)S(1)} custom-call(bf16[1024,1024]{1,0:T(8,128)(2,1)S(1)} %bitcast.25, bf16[1024,1024]{1,0:T(8,128)(2,1)S(1)} %bitcast.27, bf16[8,144,128]{2,1,0:T(8,128)(2,1)S(1)} %all-to-all-done.got_ref.mix_ref), custom_call_target="tpu_custom_call" | custom-call | flops 805306368 | bytes 6291456 | tf_op jit(solution)/shard_map/volume/pallas_call | solution.py:103
  47.8 2.2 %copy-done.1 = bf16[1024,2048]{1,0:T(8,128)(2,1)S(1)} copy-done((bf16[1024,2048]{1,0:T(8,128)(2,1)S(1)}, bf16[1024,2048]{1,0:T(8,128)(2,1)}, u32[]{:S(2)}) %copy-start.1) | copy-done | bytes 4194328
  50.0 2.3 %applied.2.refs_8_ = f32[1024,128]{1,0:T(8,128)S(1)} custom-call(f32[1024,128]{1,0:T(8,128)S(1)} %volume.2.prior_ref, bf16[1024,2048]{1,0:T(8,128)(2,1)S(1)} %copy-done.1, bf16[2048,128]{1,0:T(8,128)(2,1)} %bitcast.12.column_ref), custom_call_target="tpu_custom_call" | custom-call | flops 536870912 | bytes 4194304 | tf_op jit(solution)/shard_map/applied/pallas_call | solution.py:116
  52.4 1.3 %collective-permute-done.2.refs_3_ = bf16[128,1024]{1,0:T(8,128)(2,1)} collective-permute-done((bf16[128,1024]{1,0:T(8,128)(2,1)}, bf16[128,1024]{1,0:T(8,128)(2,1)}, u32[]{:S(2)}, u32[]{:S(2)}) %collective-permute-start.2) | collective-permute-done | bytes 262176 | tf_op jit(solution)/shard_map/ppermute | solution.py:156
  54.2 3.3 %collective-permute-done.refs_1_ = bf16[128,1024]{1,0:T(8,128)(2,1)} collective-permute-done((bf16[128,1024]{1,0:T(8,128)(2,1)}, bf16[128,1024]{1,0:T(8,128)(2,1)}, u32[]{:S(2)}, u32[]{:S(2)}) %collective-permute-start) | collective-permute-done | bytes 262176 | tf_op jit(solution)/shard_map/ppermute | solution.py:156
  57.4 2.8 %faces.2 = bf16[1024,128]{1,0:T(8,128)(2,1)S(1)} custom-call(s32[1]{0:T(128)} %bitcast.col_ref, bf16[8,144,128]{2,1,0:T(8,128)(2,1)S(1)} %all-to-all-done.got_ref.mix_ref, bf16[8,144,128]{2,1,0:T(8,128)(2,1)S(1)} %all-to-all-done.got_ref.mix_ref, bf16[128,1024]{1,0:T(8,128)(2,1)S(1)} %get-tuple-element.11.refs_0_, ...), custom_call_target="tpu_custom_call" | custom-call | flops 536870912 | bytes 4194304 | tf_op jit(solution)/shard_map/faces/pallas_call | solution.py:130
  60.2 12.1 %all_to_all.30 = bf16[8,128,128]{2,1,0:T(8,128)(2,1)S(1)} all-to-all(bf16[8,128,128]{2,1,0:T(8,128)(2,1)S(1)} %bitcast.30), channel_id=1, replica_groups=mesh['row'=16,'col'=8] {'col'}, dimensions={0} | all-to-all | bytes 524288 | tf_op jit(solution)/shard_map/all_to_all | solution.py:30
  73.1 4.4 %all-to-all-start.3 = ((bf16[8,128,128]{2,1,0:T(8,128)(2,1)}), bf16[8,128,128]{2,1,0:T(8,128)(2,1)S(1)}, u32[]{:S(2)}, u32[]{:S(2)}) async-start(bf16[8,128,128]{2,1,0:T(8,128)(2,1)} %broadcast_in_dim.27), calls=%async_computation.3 | async-start | bytes 524288 | tf_op jit(solution)/shard_map/all_to_all | solution.py:30
  77.5 3.2 %collective-permute-start.8 = (bf16[128,128]{1,0:T(8,128)(2,1)S(1)}, bf16[128,128]{1,0:T(8,128)(2,1)S(1)}, u32[]{:S(2)}, u32[]{:S(2)}) collective-permute-start(bf16[128,128]{1,0:T(8,128)(2,1)S(1)} %fusion), channel_id=1, source_target_pairs={{0,0},{1,8},{2,16},{3,24},{4,32},{5,40},{6,48},{7,56},{8,64},{9,72... | collective-permute-start | bytes 98312 | tf_op jit(solution)/shard_map/ppermute | solution.py:171
  80.7 3.8 %collective-permute-done.8 = bf16[128,128]{1,0:T(8,128)(2,1)S(1)} collective-permute-done((bf16[128,128]{1,0:T(8,128)(2,1)S(1)}, bf16[128,128]{1,0:T(8,128)(2,1)S(1)}, u32[]{:S(2)}, u32[]{:S(2)}) %collective-permute-start.8) | collective-permute-done | bytes 32800 | tf_op jit(solution)/shard_map/ppermute | solution.py:171
  84.5 0.9 broadcast_in_dim.28
  85.4 9.2 %all-to-all-start.4 = ((bf16[16,128,128]{2,1,0:T(8,128)(2,1)}), bf16[16,128,128]{2,1,0:T(8,128)(2,1)S(1)}, u32[]{:S(2)}, u32[]{:S(2)}) async-start(bf16[16,128,128]{2,1,0:T(8,128)(2,1)} %broadcast_in_dim.28), calls=%async_computation.4 | async-start | bytes 1048576 | tf_op jit(solution)/shard_map/all_to_all | solution.py:30
  94.6 0.9 copy-done.6
  95.6 0.9 copy-done.9
  96.5 2.9 %faces.3.refs_0_ = f32[1024,128]{1,0:T(8,128)S(1)} custom-call(s32[1]{0:T(128)} %bitcast.col_ref, bf16[8,144,128]{2,1,0:T(8,128)(2,1)S(1)} %all-to-all-done.got_ref.mix_ref, bf16[8,128,128]{2,1,0:T(8,128)(2,1)S(1)} %all-to-all-done.3.got_ref, bf16[128,1024]{1,0:T(8,128)(2,1)S(1)} %get-tuple-element.11.refs_0_, ...), custom_call_target="tpu_custom_call" | custom-call | flops 536870912 | bytes 4194304 | tf_op jit(solution)/shard_map/faces/pallas_call | solution.py:130
  99.5 2.8 %volume.3.prior_ref = f32[1024,128]{1,0:T(8,128)S(1)} custom-call(bf16[1024,1024]{1,0:T(8,128)(2,1)S(1)} %bitcast.26, bf16[1024,1024]{1,0:T(8,128)(2,1)S(1)} %bitcast.28, bf16[8,128,128]{2,1,0:T(8,128)(2,1)S(1)} %all-to-all-done.3.got_ref, f32[1024,128]{1,0:T(8,128)S(1)} %faces.3.refs_0_), custom_call_target="tpu_custom_call" | custom-call | flops 805306368 | bytes 6291456 | tf_op jit(solution)/shard_map/volume/pallas_call | solution.py:103
  102.2 1.4 %all-to-all-done.4 = bf16[16,128,128]{2,1,0:T(8,128)(2,1)S(1)} async-done(((bf16[16,128,128]{2,1,0:T(8,128)(2,1)}), bf16[16,128,128]{2,1,0:T(8,128)(2,1)S(1)}, u32[]{:S(2)}, u32[]{:S(2)}) %all-to-all-start.4) | async-done | bytes 524320 | tf_op jit(solution)/shard_map/all_to_all | solution.py:30
  103.6 2.2 %copy-done.2 = bf16[1024,2048]{1,0:T(8,128)(2,1)S(1)} copy-done((bf16[1024,2048]{1,0:T(8,128)(2,1)S(1)}, bf16[1024,2048]{1,0:T(8,128)(2,1)}, u32[]{:S(2)}) %copy-start.2) | copy-done | bytes 4194328
  105.8 1.3 %applied.3 = bf16[1024,128]{1,0:T(8,128)(2,1)S(1)} custom-call(f32[1024,128]{1,0:T(8,128)S(1)} %volume.3.prior_ref, bf16[1024,2048]{1,0:T(8,128)(2,1)S(1)} %copy-done.2, bf16[2048,128]{1,0:T(8,128)(2,1)S(1)} %bitcast.29), custom_call_target="tpu_custom_call" | custom-call | flops 536870912 | bytes 4194304 | tf_op jit(solution)/shard_map/applied/pallas_call | solution.py:116
  107.1 13.3 %all_to_all.31 = bf16[8,128,128]{2,1,0:T(8,128)(2,1)S(1)} all-to-all(bf16[8,128,128]{2,1,0:T(8,128)(2,1)S(1)} %bitcast.31), channel_id=1, replica_groups=mesh['row'=16,'col'=8] {'col'}, dimensions={0} | all-to-all | bytes 524288 | tf_op jit(solution)/shard_map/all_to_all | solution.py:30
  (41 shorter events, 6.1 us)
Async XLA Ops:
  0.6 26.5 %copy-start = (bf16[1,1024,1024]{2,1,0:T(8,128)(2,1)S(1)}, bf16[1,1024,1024]{2,1,0:T(8,128)(2,1)}, u32[]{:S(2)}) copy-start(bf16[1,1024,1024]{2,1,0:T(8,128)(2,1)} %param.8) | copy-start | bytes 6291460
  3.2 13.6 %all-to-all-start = ((bf16[8,144,128]{2,1,0:T(8,128)(2,1)}), bf16[8,144,128]{2,1,0:T(8,128)(2,1)S(1)}, u32[]{:S(2)}, u32[]{:S(2)}) async-start(bf16[8,144,128]{2,1,0:T(8,128)(2,1)} %broadcast_in_dim.25), calls=%async_computation | async-start | bytes 589824 | tf_op jit(solution)/shard_map/all_to_all | solution.py:30
  10.0 6.7 %collective-permute-start.7 = (bf16[128,128]{1,0:T(8,128)(2,1)S(1)}, bf16[128,128]{1,0:T(8,128)(2,1)S(1)}, u32[]{:S(2)}, u32[]{:S(2)}) collective-permute-start(bf16[128,128]{1,0:T(8,128)(2,1)S(1)} %convert_element_type.23), channel_id=1, source_target_pairs={{0,0},{1,8},{2,16},{3,24},{4,32},{5,40},{6,48},{7,56},{8,64},{9,72... | collective-permute-start | bytes 98312 | tf_op jit(solution)/shard_map/ppermute | solution.py:171
  17.6 30.2 %all-to-all-start.1 = ((bf16[16,128,128]{2,1,0:T(8,128)(2,1)}), bf16[16,128,128]{2,1,0:T(8,128)(2,1)}, u32[]{:S(2)}, u32[]{:S(2)}) async-start(bf16[16,128,128]{2,1,0:T(8,128)(2,1)} %broadcast_in_dim.26), calls=%async_computation.1 | async-start | bytes 1048576 | tf_op jit(solution)/shard_map/all_to_all | solution.py:30
  27.2 17.9 %copy-start.3 = (bf16[1,1024,1024]{2,1,0:T(8,128)(2,1)S(1)}, bf16[1,1024,1024]{2,1,0:T(8,128)(2,1)}, u32[]{:S(2)}) copy-start(bf16[1,1024,1024]{2,1,0:T(8,128)(2,1)} %param.7) | copy-start | bytes 6291460
  28.3 11.0 %collective-permute-start.6 = (bf16[128,1024]{1,0:T(8,128)(2,1)S(1)}, bf16[128,1024]{1,0:T(8,128)(2,1)S(1)}, u32[]{:S(2)}, u32[]{:S(2)}) collective-permute-start(bf16[128,1024]{1,0:T(8,128)(2,1)S(1)} %get-tuple-element.4), channel_id=1, source_target_pairs={{0,7},{1,0},{2,1},{3,2},{4,3},{5,4},{6,5},{7,6},{8,15},{9,8},{10,9... | collective-permute-start | bytes 786440 | tf_op jit(solution)/shard_map/ppermute | solution.py:156
  29.8 9.5 %collective-permute-start.5 = (bf16[128,1024]{1,0:T(8,128)(2,1)S(1)}, bf16[128,1024]{1,0:T(8,128)(2,1)S(1)}, u32[]{:S(2)}, u32[]{:S(2)}) collective-permute-start(bf16[128,1024]{1,0:T(8,128)(2,1)S(1)} %get-tuple-element.5), channel_id=1, source_target_pairs={{0,6},{1,7},{2,0},{3,1},{4,2},{5,3},{6,4},{7,5},{8,14},{9,15},{10,... | collective-permute-start | bytes 786440 | tf_op jit(solution)/shard_map/ppermute | solution.py:156
  32.1 20.2 %collective-permute-start.4 = (bf16[128,1024]{1,0:T(8,128)(2,1)}, bf16[128,1024]{1,0:T(8,128)(2,1)}, u32[]{:S(2)}, u32[]{:S(2)}) collective-permute-start(bf16[128,1024]{1,0:T(8,128)(2,1)} %get-tuple-element.6), channel_id=1, source_target_pairs={{0,5},{1,6},{2,7},{3,0},{4,1},{5,2},{6,3},{7,4},{8,13},{9,14},{10,... | collective-permute-start | bytes 786440 | tf_op jit(solution)/shard_map/ppermute | solution.py:156
  32.8 19.5 %collective-permute-start.3 = (bf16[128,1024]{1,0:T(8,128)(2,1)}, bf16[128,1024]{1,0:T(8,128)(2,1)}, u32[]{:S(2)}, u32[]{:S(2)}) collective-permute-start(bf16[128,1024]{1,0:T(8,128)(2,1)} %get-tuple-element.7), channel_id=1, source_target_pairs={{0,4},{1,5},{2,6},{3,7},{4,0},{5,1},{6,2},{7,3},{8,12},{9,13},{10,... | collective-permute-start | bytes 786440 | tf_op jit(solution)/shard_map/ppermute | solution.py:156
  34.3 19.4 %collective-permute-start.2 = (bf16[128,1024]{1,0:T(8,128)(2,1)}, bf16[128,1024]{1,0:T(8,128)(2,1)}, u32[]{:S(2)}, u32[]{:S(2)}) collective-permute-start(bf16[128,1024]{1,0:T(8,128)(2,1)} %get-tuple-element.8), channel_id=1, source_target_pairs={{0,3},{1,4},{2,5},{3,6},{4,7},{5,0},{6,1},{7,2},{8,11},{9,12},{10,... | collective-permute-start | bytes 786440 | tf_op jit(solution)/shard_map/ppermute | solution.py:156
  39.3 18.2 %copy-start.5 = (bf16[128,1024]{1,0:T(8,128)(2,1)}, bf16[128,1024]{1,0:T(8,128)(2,1)S(1)}, u32[]{:S(2)}) copy-start(bf16[128,1024]{1,0:T(8,128)(2,1)S(1)} %collective-permute-done.6.refs_7_) | copy-start | bytes 786436
  39.3 14.9 %collective-permute-start.1 = (bf16[128,1024]{1,0:T(8,128)(2,1)}, bf16[128,1024]{1,0:T(8,128)(2,1)}, u32[]{:S(2)}, u32[]{:S(2)}) collective-permute-start(bf16[128,1024]{1,0:T(8,128)(2,1)} %get-tuple-element.9), channel_id=1, source_target_pairs={{0,2},{1,3},{2,4},{3,5},{4,6},{5,7},{6,0},{7,1},{8,10},{9,11},{10,... | collective-permute-start | bytes 786440 | tf_op jit(solution)/shard_map/ppermute | solution.py:156
  39.3 0.7 copy-start.7
  40.0 17.4 %collective-permute-start = (bf16[128,1024]{1,0:T(8,128)(2,1)}, bf16[128,1024]{1,0:T(8,128)(2,1)}, u32[]{:S(2)}, u32[]{:S(2)}) collective-permute-start(bf16[128,1024]{1,0:T(8,128)(2,1)} %get-tuple-element.10), channel_id=1, source_target_pairs={{0,1},{1,2},{2,3},{3,4},{4,5},{5,6},{6,7},{7,0},{8,9},{9,10},{10,1... | collective-permute-start | bytes 786440 | tf_op jit(solution)/shard_map/ppermute | solution.py:156
  47.8 2.2 %copy-start.1 = (bf16[1024,2048]{1,0:T(8,128)(2,1)S(1)}, bf16[1024,2048]{1,0:T(8,128)(2,1)}, u32[]{:S(2)}) copy-start(bf16[1024,2048]{1,0:T(8,128)(2,1)} %surface_ref.3) | copy-start | bytes 12582916
  50.0 7.4 %copy-start.8 = (bf16[128,1024]{1,0:T(8,128)(2,1)S(1)}, bf16[128,1024]{1,0:T(8,128)(2,1)}, u32[]{:S(2)}) copy-start(bf16[128,1024]{1,0:T(8,128)(2,1)} %copy-done.7) | copy-start | bytes 786436
  57.4 14.9 %copy-start.10 = (f32[128,128]{1,0:T(8,128)S(1)}, f32[128,128]{1,0:T(8,128)}, u32[]{:S(2)}) copy-start(f32[128,128]{1,0:T(8,128)} %param.6) | copy-start | bytes 196612
  73.1 11.4 %all-to-all-start.3 = ((bf16[8,128,128]{2,1,0:T(8,128)(2,1)}), bf16[8,128,128]{2,1,0:T(8,128)(2,1)S(1)}, u32[]{:S(2)}, u32[]{:S(2)}) async-start(bf16[8,128,128]{2,1,0:T(8,128)(2,1)} %broadcast_in_dim.27), calls=%async_computation.3 | async-start | bytes 524288 | tf_op jit(solution)/shard_map/all_to_all | solution.py:30
  77.5 7.0 %collective-permute-start.8 = (bf16[128,128]{1,0:T(8,128)(2,1)S(1)}, bf16[128,128]{1,0:T(8,128)(2,1)S(1)}, u32[]{:S(2)}, u32[]{:S(2)}) collective-permute-start(bf16[128,128]{1,0:T(8,128)(2,1)S(1)} %fusion), channel_id=1, source_target_pairs={{0,0},{1,8},{2,16},{3,24},{4,32},{5,40},{6,48},{7,56},{8,64},{9,72... | collective-permute-start | bytes 98312 | tf_op jit(solution)/shard_map/ppermute | solution.py:171
  85.4 18.2 %all-to-all-start.4 = ((bf16[16,128,128]{2,1,0:T(8,128)(2,1)}), bf16[16,128,128]{2,1,0:T(8,128)(2,1)S(1)}, u32[]{:S(2)}, u32[]{:S(2)}) async-start(bf16[16,128,128]{2,1,0:T(8,128)(2,1)} %broadcast_in_dim.28), calls=%async_computation.4 | async-start | bytes 1048576 | tf_op jit(solution)/shard_map/all_to_all | solution.py:30
  94.6 1.0 copy-start.6
  95.6 0.9 copy-start.9
  96.5 2.9 %copy-start.4 = (bf16[1,1024,1024]{2,1,0:T(8,128)(2,1)S(1)}, bf16[1,1024,1024]{2,1,0:T(8,128)(2,1)}, u32[]{:S(2)}) copy-start(bf16[1,1024,1024]{2,1,0:T(8,128)(2,1)} %param.7) | copy-start | bytes 6291460
  103.6 2.2 %copy-start.2 = (bf16[1024,2048]{1,0:T(8,128)(2,1)S(1)}, bf16[1024,2048]{1,0:T(8,128)(2,1)}, u32[]{:S(2)}) copy-start(bf16[1024,2048]{1,0:T(8,128)(2,1)} %surface_ref.3) | copy-start | bytes 12582916
  105.8 14.6 %copy-start.11 = (f32[128,128]{1,0:T(8,128)S(1)}, f32[128,128]{1,0:T(8,128)}, u32[]{:S(2)}) copy-start(f32[128,128]{1,0:T(8,128)} %param.6) | copy-start | bytes 196612

commit v5 on v4

--- a/solution.py
+++ b/solution.py
@@ -1,3 +1,5 @@
+import functools
+
 import jax
 import jax.numpy as jnp
 from jax import lax
@@ -47,14 +49,24 @@
     return (col + k) & (peers - 1)
 
 
-def grouped(got_ref, n):
-    got = got_ref[:, :n]
-    return got.reshape(got.shape[0] * n, got.shape[2])
-
-
-def volume_kernel(interp_ref, dtn_ref, got_ref, *refs):
-    peers = got_ref.shape[0]
-    traces = dot(interp_ref[...], grouped(got_ref, interp_ref.shape[1] // peers)).astype(BF)
+def owner(col, distance, j, peers):
+    return rotated(col, -2 * distance, peers) ^ j
+
+
+def assemble_kernel(outs, col_ref, *refs):
+    pair_refs, group_ref = refs[:-outs], refs[-outs]
+    peers = 2 * len(pair_refs)
+    n = group_ref.shape[0] // peers
+    for d, pair_ref in enumerate(pair_refs):
+        for j in range(2):
+            s = owner(col_ref[0], d, j, peers)
+            group_ref[pl.ds(pl.multiple_of(s * n, n), n), :] = pair_ref[j, :n, :]
+            if outs == 2:
+                refs[-1][s] = pair_ref[j, n:, :].astype(F32)
+
+
+def volume_kernel(interp_ref, dtn_ref, group_ref, *refs):
+    traces = dot(interp_ref[...], group_ref[...]).astype(BF)
     response = dot(dtn_ref[...], traces).astype(BF)
     total = dot_t(interp_ref[...], response)
     if len(refs) == 2:
@@ -62,18 +74,16 @@
     refs[-1][...] = total
 
 
-def faces_kernel(col_ref, mix_ref, got_ref, *refs):
-    peers = got_ref.shape[0]
+def faces_kernel(col_ref, mix_ref, group_ref, *refs):
+    peers = mix_ref.shape[0]
     slice_refs, prior_refs = refs[:peers], refs[peers:-2]
     out_ref, traces_ref = refs[-2:]
-    n = slice_refs[0].shape[1] // peers
-    group = grouped(got_ref, n)
+    group = group_ref[...]
     for k in range(peers):
         traces_ref[rotated(col_ref[0], -k, peers)] = dot(slice_refs[k][...], group)
     total = prior_refs[0][...] if prior_refs else None
     for k in range(peers):
-        s = rotated(col_ref[0], -k, peers)
-        row = mix_ref[s, n : n + 16, :].astype(F32)[:1]
+        row = mix_ref[rotated(col_ref[0], -k, peers)][:1]
         mixed = None
         for p in range(peers):
             term = row[:, p : p + 1] * traces_ref[p]
@@ -97,9 +107,28 @@
     )
 
 
-def volume(interp, dtn, got, *prior):
+def smem():
+    return pl.BlockSpec(memory_space=pltpu.SMEM)
+
+
+def assemble(place, pairs, n):
+    peers, (_, high, ne) = 2 * len(pairs), pairs[0].shape
+    shapes = [jax.ShapeDtypeStruct((peers * n, ne), BF)]
+    if high > n:
+        shapes.append(jax.ShapeDtypeStruct((peers, high - n, ne), F32))
+    return pl.pallas_call(
+        functools.partial(assemble_kernel, len(shapes)),
+        out_shape=shapes,
+        in_specs=[smem()] + [vmem()] * len(pairs),
+        out_specs=[vmem()] * len(shapes),
+        compiler_params=PARAMS,
+        name="assemble",
+    )(place, *pairs)
+
+
+def volume(interp, dtn, group, *prior):
     m, rb = interp.shape
-    ne = got.shape[-1]
+    ne = group.shape[-1]
     return pl.pallas_call(
         volume_kernel,
         out_shape=jax.ShapeDtypeStruct((rb, ne), F32),
@@ -108,7 +137,7 @@
         compiler_params=PARAMS,
         cost_estimate=cost(3, m, rb, ne),
         name="volume",
-    )(interp, dtn, got, *prior)
+    )(interp, dtn, group, *prior)
 
 
 def applied(prior, surface, column_block, dtype):
@@ -124,19 +153,29 @@
     )(prior, surface, column_block)
 
 
-def faces(place, mix, got, slices, dtype, *prior):
-    (ms, rb), ne = slices[0].shape, got.shape[-1]
+def faces(place, mix, group, slices, dtype, *prior):
+    (ms, rb), ne = slices[0].shape, group.shape[-1]
     peers = len(slices)
     return pl.pallas_call(
         faces_kernel,
         out_shape=jax.ShapeDtypeStruct((rb, ne), dtype),
-        in_specs=[pl.BlockSpec(memory_space=pltpu.SMEM)] + [vmem()] * (2 + peers + len(prior)),
+        in_specs=[smem()] + [vmem()] * (2 + peers + len(prior)),
         out_specs=vmem(),
         scratch_shapes=[pltpu.VMEM((peers, ms, ne), F32)],
         compiler_params=PARAMS,
         cost_estimate=cost(2, peers * ms, rb, ne),
         name="faces",
-    )(place, mix, got, *slices, *prior)
+    )(place, mix, group, *slices, *prior)
+
+
+def gathered(shard, cols):
+    other = lax.ppermute(shard, "col", [(i, i ^ 1) for i in range(cols)])
+    pair = jnp.stack([shard, other])
+    pairs = [pair]
+    for d in range(1, cols // 2):
+        path = [(i, (i + 2 * d) % cols) for i in range(cols)]
+        pairs.append(lax.ppermute(pair, "col", path))
+    return pairs
 
 
 def steps(surface, excitation, dtn_blocks, interp_blocks, adjacency):
@@ -171,15 +210,16 @@
         piece = lax.ppermute(rounded, ("row", "col"), turned(rows, cols))
         column_block = copy_for_each(piece, "row").reshape(rows * n, ne)
         sent = jnp.concatenate([rounded, extra], axis=0) if sweep == 0 else rounded
-        got = copy_for_each(sent, "col")
-        mix = got if mix is None else mix
+        pairs = gathered(sent, cols)
+        group, *rows_got = assemble(place, pairs, n)
         if sweep == 0:
-            own = volume(interp, dtn, got)
+            mix = rows_got[0]
+            own = volume(interp, dtn, group)
             wide = applied(own, surface, column_block, F32)
-            part = faces(place, mix, got, slices, BF, wide)
+            part = faces(place, mix, group, slices, BF, wide)
         else:
-            wide = faces(place, mix, got, slices, F32)
-            own = volume(interp, dtn, got, wide)
+            wide = faces(place, mix, group, slices, F32)
+            own = volume(interp, dtn, group, wide)
             part = applied(own, surface, column_block, BF)
         parts = exchange(part.reshape(cols, n, ne), "col")
         summed = jnp.sum(parts.astype(F32), axis=0)

time: 122 us -> 120 us (0.984)
  waiting for transfers between devices: 15.7 us -> 19.7 us
  starting transfers between devices: 50.3 us -> 46.9 us
  blocking collectives: 25.4 us -> 23.7 us
    all_to_all x4 -> x2, starting transfers between devices: 29.9 us -> 14 us  [exchange(): return lax.all_to_all(blocks, axis, split_axis=0, concat_axis=0, tiled=True)]
    ppermute x0 -> x8, starting transfers between devices: none -> 10.9 us  [the longest x6 6.1 us: gathered(): pairs.append(lax.ppermute(pair, 'col', path))]
    ppermute x0 -> x8, waiting for transfers between devices: none -> 8.64 us  [the longest x6 6.71 us: gathered(): pairs.append(lax.ppermute(pair, 'col', path))]
    ppermute x2, waiting for transfers between devices: 7.43 us -> 3.1 us  [steps(): piece = lax.ppermute(rounded, ('row', 'col'), turned(rows, cols))]
    ppermute x2, starting transfers between devices: 6.29 us -> 9.05 us  [steps(): piece = lax.ppermute(rounded, ('row', 'col'), turned(rows, cols))]
    all_to_all x2, blocking collectives: 25.4 us -> 23.7 us  [exchange(): return lax.all_to_all(blocks, axis, split_axis=0, concat_axis=0, tiled=True)]
    dynamic_slice x1, local copies, waits for them, and re-layouts: 1.11 us -> 2.77 us  [steps(): block = lax.dynamic_slice_in_dim(interp, rotated(col, k, cols) * ms, ms, 0)]
    broadcast_in_dim x4 -> x2, local copies, waits for them, and re-layouts: 3.28 us -> 1.82 us  [copy_for_each(): jnp.broadcast_to(shard, (lax.axis_size(axis), *shard.shape))]
  transfers between devices with their start and end apart: 13 -> 19, of which waited for: 8 -> 11; matrix products, arithmetic and copies ran while one was open for 1% -> 4% of each run, Pallas kernels for 9% -> 8%
where the time goes in v5:
time: 120 us; the launch traced here: 119 us
  starting transfers between devices  46.9 us (39%)
  blocking collectives  23.7 us (20%)
  waiting for transfers between devices  19.7 us (16%)
  Pallas kernels  13.7 us (11%)
  local copies, waits for them, and re-layouts  12 us (10%)
  other arithmetic  2.49 us (2%)
    all_to_all x2, blocking collectives, exchange(): return lax.all_to_all(blocks, axis, split_axis=0, concat_axis=0, tiled=True)  23.7 us
    all_to_all x2, starting transfers between devices, exchange(): return lax.all_to_all(blocks, axis, split_axis=0, concat_axis=0, tiled=True)  14 us
    ppermute x7, starting transfers between devices, steps(): lax.ppermute(block, 'col', [(i, (i + k) % cols) for i in range(cols)])  13 us
    ppermute x2, starting transfers between devices, steps(): piece = lax.ppermute(rounded, ('row', 'col'), turned(rows, cols))  9.05 us
    ppermute x7, waiting for transfers between devices, steps(): lax.ppermute(block, 'col', [(i, (i + k) % cols) for i in range(cols)])  7.92 us
    unnamed x34, local copies, waits for them, and re-layouts  7.41 us
    ppermute x6, waiting for transfers between devices, gathered(): pairs.append(lax.ppermute(pair, 'col', path))  6.71 us
    ppermute x6, starting transfers between devices, gathered(): pairs.append(lax.ppermute(pair, 'col', path))  6.1 us
  transfers between devices with their start and end apart: 19, of which 11 were waited for; matrix products, arithmetic and copies ran while one was open for 4% of the time, Pallas kernels for 8%

profile of v5, /device:TPU:1, one launch (start us, length us, event | category | flops | bytes accessed | tf_op | source)
XLA Modules:
  0.0 119.4 jit_solution(6108623441796465562)
XLA Ops:
  1.5 4.6 %collective-permute-start.11 = (bf16[128,128]{1,0:T(8,128)(2,1)S(1)}, bf16[128,128]{1,0:T(8,128)(2,1)S(1)}, u32[]{:S(2)}, u32[]{:S(2)}) collective-permute-start(bf16[128,128]{1,0:T(8,128)(2,1)S(1)} %convert_element_type.23), channel_id=1, source_target_pairs={{0,0},{1,8},{2,16},{3,24},{4,32},{5,40},{6,48},{7,56},{8,64},{9,72... | collective-permute-start | bytes 98312 | tf_op jit(solution)/shard_map/ppermute | solution.py:210
  6.1 2.8 %dynamic-slice_bitcast_fusion = (bf16[128,1024]{1,0:T(8,128)(2,1)}, bf16[128,1024]{1,0:T(8,128)(2,1)}, bf16[128,1024]{1,0:T(8,128)(2,1)}, bf16[128,1024]{1,0:T(8...) fusion(bf16[1,1024,1024]{2,1,0:T(8,128)(2,1)} %param.8, ...), kind=kLoop, calls=%fused_computation.2 | loop fusion | bytes 4194336 | tf_op jit(solution)/shard_map/dynamic_slice | solution.py:193
  8.9 5.3 %collective-permute-start.9 = (bf16[128,1024]{1,0:T(8,128)(2,1)}, bf16[128,1024]{1,0:T(8,128)(2,1)S(1)}, u32[]{:S(2)}, u32[]{:S(2)}) collective-permute-start(bf16[128,1024]{1,0:T(8,128)(2,1)} %get-tuple-element.9), channel_id=1, source_target_pairs={{0,6},{1,7},{2,0},{3,1},{4,2},{5,3},{6,4},{7,5},{8,14},{9,15},{10,... | collective-permute-start | bytes 786440 | tf_op jit(solution)/shard_map/ppermute | solution.py:195
  15.2 5.1 %all-to-all-start = ((bf16[16,128,128]{2,1,0:T(8,128)(2,1)}), bf16[16,128,128]{2,1,0:T(8,128)(2,1)S(1)}, u32[]{:S(2)}, u32[]{:S(2)}) async-start(bf16[16,128,128]{2,1,0:T(8,128)(2,1)} %broadcast_in_dim.19), calls=%async_computation | async-start | bytes 1048576 | tf_op jit(solution)/shard_map/all_to_all | solution.py:32
  20.4 1.5 %collective-permute-start = (bf16[144,128]{1,0:T(8,128)(2,1)S(1)}, bf16[144,128]{1,0:T(8,128)(2,1)S(1)}, u32[]{:S(2)}, u32[]{:S(2)}) collective-permute-start(bf16[144,128]{1,0:T(8,128)(2,1)S(1)} %get-tuple-element.17), channel_id=1, source_target_pairs={{0,1},{1,0},{2,3},{3,2},{4,5},{5,4},{6,7},{7,6},{8,9},{9,8},{10,11... | collective-permute-start | bytes 110600 | tf_op jit(solution)/shard_map/ppermute | solution.py:172
  22.8 3.1 %collective-permute-start.3 = (bf16[2,144,128]{2,1,0:T(8,128)(2,1)S(1)}, bf16[2,144,128]{2,1,0:T(8,128)(2,1)S(1)}, u32[]{:S(2)}, u32[]{:S(2)}) collective-permute-start(bf16[2,144,128]{2,1,0:T(8,128)(2,1)S(1)} %pad_maximum_fusion.refs_0_), channel_id=1, source_target_pairs={{0,6},{1,7},{2,0},{3,1},{4,2},{5,3},{6,4},{7,5},{8,14},{9,15},{10,... | collective-permute-start | bytes 221192 | tf_op jit(solution)/shard_map/ppermute | solution.py:177
  26.8 2.1 %collective-permute-done.3.refs_3_ = bf16[2,144,128]{2,1,0:T(8,128)(2,1)S(1)} collective-permute-done((bf16[2,144,128]{2,1,0:T(8,128)(2,1)S(1)}, bf16[2,144,128]{2,1,0:T(8,128)(2,1)S(1)}, u32[]{:S(2)}, u32[]{:S(2)}) %collective-permute-start.3) | collective-permute-done | bytes 73760 | tf_op jit(solution)/shard_map/ppermute | solution.py:177
  28.9 4.4 %collective-permute-start.8 = (bf16[128,1024]{1,0:T(8,128)(2,1)}, bf16[128,1024]{1,0:T(8,128)(2,1)}, u32[]{:S(2)}, u32[]{:S(2)}) collective-permute-start(bf16[128,1024]{1,0:T(8,128)(2,1)} %get-tuple-element.10), channel_id=1, source_target_pairs={{0,5},{1,6},{2,7},{3,0},{4,1},{5,2},{6,3},{7,4},{8,13},{9,14},{10,... | collective-permute-start | bytes 786440 | tf_op jit(solution)/shard_map/ppermute | solution.py:195
  33.3 2.7 %collective-permute-start.6 = (bf16[128,1024]{1,0:T(8,128)(2,1)}, bf16[128,1024]{1,0:T(8,128)(2,1)}, u32[]{:S(2)}, u32[]{:S(2)}) collective-permute-start(bf16[128,1024]{1,0:T(8,128)(2,1)} %get-tuple-element.12), channel_id=1, source_target_pairs={{0,3},{1,4},{2,5},{3,6},{4,7},{5,0},{6,1},{7,2},{8,11},{9,12},{10,... | collective-permute-start | bytes 786440 | tf_op jit(solution)/shard_map/ppermute | solution.py:195
  37.3 1.6 %copy-done.3 = bf16[1,1024,1024]{2,1,0:T(8,128)(2,1)S(1)} copy-done((bf16[1,1024,1024]{2,1,0:T(8,128)(2,1)S(1)}, bf16[1,1024,1024]{2,1,0:T(8,128)(2,1)}, u32[]{:S(2)}) %copy-start.3) | copy-done | bytes 2097176
  38.9 2.8 %volume.2.prior_ref = f32[1024,128]{1,0:T(8,128)S(1)} custom-call(bf16[1024,1024]{1,0:T(8,128)(2,1)S(1)} %bitcast.30, bf16[1024,1024]{1,0:T(8,128)(2,1)S(1)} %bitcast.32, bf16[1024,128]{1,0:T(8,128)(2,1)S(1)} %get-tuple-element.5.group_ref), custom_call_target="tpu_custom_call" | custom-call | flops 805306368 | bytes 6291456 | tf_op jit(solution)/shard_map/volume/pallas_call | solution.py:132
  42.4 2.2 %copy-done.1 = bf16[1024,2048]{1,0:T(8,128)(2,1)S(1)} copy-done((bf16[1024,2048]{1,0:T(8,128)(2,1)S(1)}, bf16[1024,2048]{1,0:T(8,128)(2,1)}, u32[]{:S(2)}) %copy-start.1) | copy-done | bytes 4194328
  44.6 1.3 %applied.2.refs_8_ = f32[1024,128]{1,0:T(8,128)S(1)} custom-call(f32[1024,128]{1,0:T(8,128)S(1)} %volume.2.prior_ref, bf16[1024,2048]{1,0:T(8,128)(2,1)S(1)} %copy-done.1, bf16[2048,128]{1,0:T(8,128)(2,1)S(1)} %bitcast.34), custom_call_target="tpu_custom_call" | custom-call | flops 536870912 | bytes 4194304 | tf_op jit(solution)/shard_map/applied/pallas_call | solution.py:145
  45.9 2.3 %collective-permute-done.8.refs_5_ = bf16[128,1024]{1,0:T(8,128)(2,1)} collective-permute-done((bf16[128,1024]{1,0:T(8,128)(2,1)}, bf16[128,1024]{1,0:T(8,128)(2,1)}, u32[]{:S(2)}, u32[]{:S(2)}) %collective-permute-start.8) | collective-permute-done | bytes 262176 | tf_op jit(solution)/shard_map/ppermute | solution.py:195
  48.1 3.3 %collective-permute-done.6.refs_3_ = bf16[128,1024]{1,0:T(8,128)(2,1)} collective-permute-done((bf16[128,1024]{1,0:T(8,128)(2,1)}, bf16[128,1024]{1,0:T(8,128)(2,1)}, u32[]{:S(2)}, u32[]{:S(2)}) %collective-permute-start.6) | collective-permute-done | bytes 262176 | tf_op jit(solution)/shard_map/ppermute | solution.py:195
  51.9 1.9 %collective-permute-done.4.refs_1_ = bf16[128,1024]{1,0:T(8,128)(2,1)} collective-permute-done((bf16[128,1024]{1,0:T(8,128)(2,1)}, bf16[128,1024]{1,0:T(8,128)(2,1)}, u32[]{:S(2)}, u32[]{:S(2)}) %collective-permute-start.4) | collective-permute-done | bytes 262176 | tf_op jit(solution)/shard_map/ppermute | solution.py:195
  53.8 2.8 %faces.2 = bf16[1024,128]{1,0:T(8,128)(2,1)S(1)} custom-call(s32[1]{0:T(128)} %bitcast.col_ref, f32[8,16,128]{2,1,0:T(8,128)S(1)} %get-tuple-element.4.mix_ref, bf16[1024,128]{1,0:T(8,128)(2,1)S(1)} %copy-done.12, bf16[128,1024]{1,0:T(8,128)(2,1)S(1)} %get-tuple-element.15.refs_0_, bf16[128,1024]{1,0:T(8,128)(2,1)} %collective-permute-done.4.refs_1_, ...), custom_call_target="tpu_custom_call" | custom-call | flops 536870912 | bytes 4194304 | tf_op jit(solution)/shard_map/faces/pallas_call | solution.py:159
  56.6 13.1 %all_to_all.20 = bf16[8,128,128]{2,1,0:T(8,128)(2,1)S(1)} all-to-all(bf16[8,128,128]{2,1,0:T(8,128)(2,1)S(1)} %bitcast.36), channel_id=1, replica_groups=mesh['row'=16,'col'=8] {'col'}, dimensions={0} | all-to-all | bytes 524288 | tf_op jit(solution)/shard_map/all_to_all | solution.py:32
  69.8 4.5 %collective-permute-start.16 = (bf16[128,128]{1,0:T(8,128)(2,1)S(1)}, bf16[128,128]{1,0:T(8,128)(2,1)S(1)}, u32[]{:S(2)}, u32[]{:S(2)}) collective-permute-start(bf16[128,128]{1,0:T(8,128)(2,1)S(1)} %fusion), channel_id=1, source_target_pairs={{0,0},{1,8},{2,16},{3,24},{4,32},{5,40},{6,48},{7,56},{8,64},{9,72... | collective-permute-start | bytes 98312 | tf_op jit(solution)/shard_map/ppermute | solution.py:210
  74.3 3.1 %collective-permute-done.16 = bf16[128,128]{1,0:T(8,128)(2,1)S(1)} collective-permute-done((bf16[128,128]{1,0:T(8,128)(2,1)S(1)}, bf16[128,128]{1,0:T(8,128)(2,1)S(1)}, u32[]{:S(2)}, u32[]{:S(2)}) %collective-permute-start.16) | collective-permute-done | bytes 32800 | tf_op jit(solution)/shard_map/ppermute | solution.py:210
  78.3 8.9 %all-to-all-start.2 = ((bf16[16,128,128]{2,1,0:T(8,128)(2,1)}), bf16[16,128,128]{2,1,0:T(8,128)(2,1)S(1)}, u32[]{:S(2)}, u32[]{:S(2)}) async-start(bf16[16,128,128]{2,1,0:T(8,128)(2,1)} %broadcast_in_dim.20), calls=%async_computation.2 | async-start | bytes 1048576 | tf_op jit(solution)/shard_map/all_to_all | solution.py:32
  87.2 3.3 %collective-permute-start.12 = (bf16[128,128]{1,0:T(8,128)(2,1)}, bf16[128,128]{1,0:T(8,128)(2,1)S(1)}, u32[]{:S(2)}, u32[]{:S(2)}) collective-permute-start(bf16[128,128]{1,0:T(8,128)(2,1)} %copy-done.15), channel_id=1, source_target_pairs={{0,1},{1,0},{2,3},{3,2},{4,5},{5,4},{6,7},{7,6},{8,9},{9,8},{10,11... | collective-permute-start | bytes 98312 | tf_op jit(solution)/shard_map/ppermute | solution.py:172
  90.4 1.1 collective-permute-done.12
  92.3 2.1 %collective-permute-start.14 = (bf16[2,128,128]{2,1,0:T(8,128)(2,1)S(1)}, bf16[2,128,128]{2,1,0:T(8,128)(2,1)S(1)}, u32[]{:S(2)}, u32[]{:S(2)}) collective-permute-start(bf16[2,128,128]{2,1,0:T(8,128)(2,1)S(1)} %pad_maximum_fusion.1.refs_0_), channel_id=1, source_target_pairs={{0,4},{1,5},{2,6},{3,7},{4,0},{5,1},{6,2},{7,3},{8,12},{9,13},{10,... | collective-permute-start | bytes 196616 | tf_op jit(solution)/shard_map/ppermute | solution.py:177
  94.3 1.3 %collective-permute-done.15.refs_3_ = bf16[2,128,128]{2,1,0:T(8,128)(2,1)S(1)} collective-permute-done((bf16[2,128,128]{2,1,0:T(8,128)(2,1)S(1)}, bf16[2,128,128]{2,1,0:T(8,128)(2,1)S(1)}, u32[]{:S(2)}, u32[]{:S(2)}) %collective-permute-start.15) | collective-permute-done | bytes 65568 | tf_op jit(solution)/shard_map/ppermute | solution.py:177
  95.7 1.6 %collective-permute-done.14.refs_2_ = bf16[2,128,128]{2,1,0:T(8,128)(2,1)S(1)} collective-permute-done((bf16[2,128,128]{2,1,0:T(8,128)(2,1)S(1)}, bf16[2,128,128]{2,1,0:T(8,128)(2,1)S(1)}, u32[]{:S(2)}, u32[]{:S(2)}) %collective-permute-start.14) | collective-permute-done | bytes 65568 | tf_op jit(solution)/shard_map/ppermute | solution.py:177
  97.3 1.7 %collective-permute-done.13.refs_1_ = bf16[2,128,128]{2,1,0:T(8,128)(2,1)S(1)} collective-permute-done((bf16[2,128,128]{2,1,0:T(8,128)(2,1)S(1)}, bf16[2,128,128]{2,1,0:T(8,128)(2,1)S(1)}, u32[]{:S(2)}, u32[]{:S(2)}) %collective-permute-start.13) | collective-permute-done | bytes 65568 | tf_op jit(solution)/shard_map/ppermute | solution.py:177
  99.0 2.8 %faces.3.refs_0_ = f32[1024,128]{1,0:T(8,128)S(1)} custom-call(s32[1]{0:T(128)} %bitcast.col_ref, f32[8,16,128]{2,1,0:T(8,128)S(1)} %get-tuple-element.4.mix_ref, bf16[1024,128]{1,0:T(8,128)(2,1)S(1)} %assemble.3.group_ref, bf16[128,1024]{1,0:T(8,128)(2,1)S(1)} %get-tuple-element.15.refs_0_, bf16[128,1024]{1,0:T(8,128)(2,1)} %collective-permute-done.4.refs_1_, ...), custom_call_target="tpu_custom_call" | custom-call | flops 536870912 | bytes 4194304 | tf_op jit(solution)/shard_map/faces/pallas_call | solution.py:159
  101.8 2.8 %volume.3.prior_ref = f32[1024,128]{1,0:T(8,128)S(1)} custom-call(bf16[1024,1024]{1,0:T(8,128)(2,1)S(1)} %bitcast.31, bf16[1024,1024]{1,0:T(8,128)(2,1)S(1)} %bitcast.33, bf16[1024,128]{1,0:T(8,128)(2,1)S(1)} %assemble.3.group_ref, f32[1024,128]{1,0:T(8,128)S(1)} %faces.3.refs_0_), custom_call_target="tpu_custom_call" | custom-call | flops 805306368 | bytes 6291456 | tf_op jit(solution)/shard_map/volume/pallas_call | solution.py:132
  104.6 2.2 %copy-done.2 = bf16[1024,2048]{1,0:T(8,128)(2,1)S(1)} copy-done((bf16[1024,2048]{1,0:T(8,128)(2,1)S(1)}, bf16[1024,2048]{1,0:T(8,128)(2,1)}, u32[]{:S(2)}) %copy-start.2) | copy-done | bytes 4194328
  106.8 1.3 %applied.3 = bf16[1024,128]{1,0:T(8,128)(2,1)S(1)} custom-call(f32[1024,128]{1,0:T(8,128)S(1)} %volume.3.prior_ref, bf16[1024,2048]{1,0:T(8,128)(2,1)S(1)} %copy-done.2, bf16[2048,128]{1,0:T(8,128)(2,1)S(1)} %bitcast.35), custom_call_target="tpu_custom_call" | custom-call | flops 536870912 | bytes 4194304 | tf_op jit(solution)/shard_map/applied/pallas_call | solution.py:145
  108.1 10.6 %all_to_all.21 = bf16[8,128,128]{2,1,0:T(8,128)(2,1)S(1)} all-to-all(bf16[8,128,128]{2,1,0:T(8,128)(2,1)S(1)} %bitcast.37), channel_id=1, replica_groups=mesh['row'=16,'col'=8] {'col'}, dimensions={0} | all-to-all | bytes 524288 | tf_op jit(solution)/shard_map/all_to_all | solution.py:32
  (65 shorter events, 8.7 us)
Async XLA Ops:
  1.5 12.8 %collective-permute-start.11 = (bf16[128,128]{1,0:T(8,128)(2,1)S(1)}, bf16[128,128]{1,0:T(8,128)(2,1)S(1)}, u32[]{:S(2)}, u32[]{:S(2)}) collective-permute-start(bf16[128,128]{1,0:T(8,128)(2,1)S(1)} %convert_element_type.23), channel_id=1, source_target_pairs={{0,0},{1,8},{2,16},{3,24},{4,32},{5,40},{6,48},{7,56},{8,64},{9,72... | collective-permute-start | bytes 98312 | tf_op jit(solution)/shard_map/ppermute | solution.py:210
  6.1 8.1 %copy-start.16 = (s32[1,6]{1,0:T(1,128)S(1)}, s32[1,6]{1,0:T(1,128)}, u32[]{:S(2)}) copy-start(s32[1,6]{1,0:T(1,128)} %param.9) | copy-start | bytes 76
  8.9 28.5 %copy-start = (bf16[1,1024,1024]{2,1,0:T(8,128)(2,1)S(1)}, bf16[1,1024,1024]{2,1,0:T(8,128)(2,1)}, u32[]{:S(2)}) copy-start(bf16[1,1024,1024]{2,1,0:T(8,128)(2,1)} %param.8) | copy-start | bytes 6291460
  8.9 27.2 %collective-permute-start.10 = (bf16[128,1024]{1,0:T(8,128)(2,1)}, bf16[128,1024]{1,0:T(8,128)(2,1)S(1)}, u32[]{:S(2)}, u32[]{:S(2)}) collective-permute-start(bf16[128,1024]{1,0:T(8,128)(2,1)} %get-tuple-element.8), channel_id=1, source_target_pairs={{0,7},{1,0},{2,1},{3,2},{4,3},{5,4},{6,5},{7,6},{8,15},{9,8},{10,9... | collective-permute-start | bytes 786440 | tf_op jit(solution)/shard_map/ppermute | solution.py:195
  8.9 27.7 %collective-permute-start.9 = (bf16[128,1024]{1,0:T(8,128)(2,1)}, bf16[128,1024]{1,0:T(8,128)(2,1)S(1)}, u32[]{:S(2)}, u32[]{:S(2)}) collective-permute-start(bf16[128,1024]{1,0:T(8,128)(2,1)} %get-tuple-element.9), channel_id=1, source_target_pairs={{0,6},{1,7},{2,0},{3,1},{4,2},{5,3},{6,4},{7,5},{8,14},{9,15},{10,... | collective-permute-start | bytes 786440 | tf_op jit(solution)/shard_map/ppermute | solution.py:195
  15.2 27.2 %all-to-all-start = ((bf16[16,128,128]{2,1,0:T(8,128)(2,1)}), bf16[16,128,128]{2,1,0:T(8,128)(2,1)S(1)}, u32[]{:S(2)}, u32[]{:S(2)}) async-start(bf16[16,128,128]{2,1,0:T(8,128)(2,1)} %broadcast_in_dim.19), calls=%async_computation | async-start | bytes 1048576 | tf_op jit(solution)/shard_map/all_to_all | solution.py:32
  20.4 2.4 %collective-permute-start = (bf16[144,128]{1,0:T(8,128)(2,1)S(1)}, bf16[144,128]{1,0:T(8,128)(2,1)S(1)}, u32[]{:S(2)}, u32[]{:S(2)}) collective-permute-start(bf16[144,128]{1,0:T(8,128)(2,1)S(1)} %get-tuple-element.17), channel_id=1, source_target_pairs={{0,1},{1,0},{2,3},{3,2},{4,5},{5,4},{6,7},{7,6},{8,9},{9,8},{10,11... | collective-permute-start | bytes 110600 | tf_op jit(solution)/shard_map/ppermute | solution.py:172
  22.8 6.1 %collective-permute-start.3 = (bf16[2,144,128]{2,1,0:T(8,128)(2,1)S(1)}, bf16[2,144,128]{2,1,0:T(8,128)(2,1)S(1)}, u32[]{:S(2)}, u32[]{:S(2)}) collective-permute-start(bf16[2,144,128]{2,1,0:T(8,128)(2,1)S(1)} %pad_maximum_fusion.refs_0_), channel_id=1, source_target_pairs={{0,6},{1,7},{2,0},{3,1},{4,2},{5,3},{6,4},{7,5},{8,14},{9,15},{10,... | collective-permute-start | bytes 221192 | tf_op jit(solution)/shard_map/ppermute | solution.py:177
  25.9 7.4 %collective-permute-start.2 = (bf16[2,144,128]{2,1,0:T(8,128)(2,1)S(1)}, bf16[2,144,128]{2,1,0:T(8,128)(2,1)S(1)}, u32[]{:S(2)}, u32[]{:S(2)}) collective-permute-start(bf16[2,144,128]{2,1,0:T(8,128)(2,1)S(1)} %pad_maximum_fusion.refs_0_), channel_id=1, source_target_pairs={{0,4},{1,5},{2,6},{3,7},{4,0},{5,1},{6,2},{7,3},{8,12},{9,13},{10,... | collective-permute-start | bytes 221192 | tf_op jit(solution)/shard_map/ppermute | solution.py:177
  26.8 6.5 %collective-permute-start.1 = (bf16[2,144,128]{2,1,0:T(8,128)(2,1)S(1)}, bf16[2,144,128]{2,1,0:T(8,128)(2,1)S(1)}, u32[]{:S(2)}, u32[]{:S(2)}) collective-permute-start(bf16[2,144,128]{2,1,0:T(8,128)(2,1)S(1)} %pad_maximum_fusion.refs_0_), channel_id=1, source_target_pairs={{0,2},{1,3},{2,4},{3,5},{4,6},{5,7},{6,0},{7,1},{8,10},{9,11},{10,... | collective-permute-start | bytes 221192 | tf_op jit(solution)/shard_map/ppermute | solution.py:177
  28.9 19.2 %collective-permute-start.8 = (bf16[128,1024]{1,0:T(8,128)(2,1)}, bf16[128,1024]{1,0:T(8,128)(2,1)}, u32[]{:S(2)}, u32[]{:S(2)}) collective-permute-start(bf16[128,1024]{1,0:T(8,128)(2,1)} %get-tuple-element.10), channel_id=1, source_target_pairs={{0,5},{1,6},{2,7},{3,0},{4,1},{5,2},{6,3},{7,4},{8,13},{9,14},{10,... | collective-permute-start | bytes 786440 | tf_op jit(solution)/shard_map/ppermute | solution.py:195
  33.3 14.9 %collective-permute-start.7 = (bf16[128,1024]{1,0:T(8,128)(2,1)}, bf16[128,1024]{1,0:T(8,128)(2,1)}, u32[]{:S(2)}, u32[]{:S(2)}) collective-permute-start(bf16[128,1024]{1,0:T(8,128)(2,1)} %get-tuple-element.11), channel_id=1, source_target_pairs={{0,4},{1,5},{2,6},{3,7},{4,0},{5,1},{6,2},{7,3},{8,12},{9,13},{10,... | collective-permute-start | bytes 786440 | tf_op jit(solution)/shard_map/ppermute | solution.py:195
  33.3 18.2 %collective-permute-start.6 = (bf16[128,1024]{1,0:T(8,128)(2,1)}, bf16[128,1024]{1,0:T(8,128)(2,1)}, u32[]{:S(2)}, u32[]{:S(2)}) collective-permute-start(bf16[128,1024]{1,0:T(8,128)(2,1)} %get-tuple-element.12), channel_id=1, source_target_pairs={{0,3},{1,4},{2,5},{3,6},{4,7},{5,0},{6,1},{7,2},{8,11},{9,12},{10,... | collective-permute-start | bytes 786440 | tf_op jit(solution)/shard_map/ppermute | solution.py:195
  36.0 15.9 %collective-permute-start.5 = (bf16[128,1024]{1,0:T(8,128)(2,1)}, bf16[128,1024]{1,0:T(8,128)(2,1)}, u32[]{:S(2)}, u32[]{:S(2)}) collective-permute-start(bf16[128,1024]{1,0:T(8,128)(2,1)} %get-tuple-element.13), channel_id=1, source_target_pairs={{0,2},{1,3},{2,4},{3,5},{4,6},{5,7},{6,0},{7,1},{8,10},{9,11},{10,... | collective-permute-start | bytes 786440 | tf_op jit(solution)/shard_map/ppermute | solution.py:195
  37.3 16.5 %collective-permute-start.4 = (bf16[128,1024]{1,0:T(8,128)(2,1)}, bf16[128,1024]{1,0:T(8,128)(2,1)}, u32[]{:S(2)}, u32[]{:S(2)}) collective-permute-start(bf16[128,1024]{1,0:T(8,128)(2,1)} %get-tuple-element.14), channel_id=1, source_target_pairs={{0,1},{1,2},{2,3},{3,4},{4,5},{5,6},{6,7},{7,0},{8,9},{9,10},{10,1... | collective-permute-start | bytes 786440 | tf_op jit(solution)/shard_map/ppermute | solution.py:195
  42.4 2.2 %copy-start.1 = (bf16[1024,2048]{1,0:T(8,128)(2,1)S(1)}, bf16[1024,2048]{1,0:T(8,128)(2,1)}, u32[]{:S(2)}) copy-start(bf16[1024,2048]{1,0:T(8,128)(2,1)} %surface_ref.3) | copy-start | bytes 12582916
  44.6 9.2 %copy-start.6 = (bf16[128,1024]{1,0:T(8,128)(2,1)S(1)}, bf16[128,1024]{1,0:T(8,128)(2,1)}, u32[]{:S(2)}) copy-start(bf16[128,1024]{1,0:T(8,128)(2,1)} %copy-done.5) | copy-start | bytes 786436
  44.6 9.2 %copy-start.9 = (bf16[128,1024]{1,0:T(8,128)(2,1)S(1)}, bf16[128,1024]{1,0:T(8,128)(2,1)}, u32[]{:S(2)}) copy-start(bf16[128,1024]{1,0:T(8,128)(2,1)} %copy-done.8) | copy-start | bytes 786436
  44.6 9.2 %copy-start.12 = (bf16[1024,128]{1,0:T(8,128)(2,1)S(1)}, bf16[1024,128]{1,0:T(8,128)(2,1)}, u32[]{:S(2)}) copy-start(bf16[1024,128]{1,0:T(8,128)(2,1)} %copy-done.11) | copy-start | bytes 786436
  45.9 23.9 %copy-start.13 = (f32[128,128]{1,0:T(8,128)S(1)}, f32[128,128]{1,0:T(8,128)}, u32[]{:S(2)}) copy-start(f32[128,128]{1,0:T(8,128)} %param.6) | copy-start | bytes 196612
  56.6 42.4 %copy-start.7 = (bf16[128,1024]{1,0:T(8,128)(2,1)S(1)}, bf16[128,1024]{1,0:T(8,128)(2,1)}, u32[]{:S(2)}) copy-start(bf16[128,1024]{1,0:T(8,128)(2,1)} %copy-done.5) | copy-start | bytes 786436
  56.6 42.4 %copy-start.10 = (bf16[128,1024]{1,0:T(8,128)(2,1)S(1)}, bf16[128,1024]{1,0:T(8,128)(2,1)}, u32[]{:S(2)}) copy-start(bf16[128,1024]{1,0:T(8,128)(2,1)} %copy-done.8) | copy-start | bytes 786436
  69.8 8.5 %copy-start.15 = (bf16[128,128]{1,0:T(8,128)(2,1)}, bf16[128,128]{1,0:T(8,128)(2,1)S(1)}, u32[]{:S(2)}) copy-start(bf16[128,128]{1,0:T(8,128)(2,1)S(1)} %fusion) | copy-start | bytes 98308
  69.8 7.6 %collective-permute-start.16 = (bf16[128,128]{1,0:T(8,128)(2,1)S(1)}, bf16[128,128]{1,0:T(8,128)(2,1)S(1)}, u32[]{:S(2)}, u32[]{:S(2)}) collective-permute-start(bf16[128,128]{1,0:T(8,128)(2,1)S(1)} %fusion), channel_id=1, source_target_pairs={{0,0},{1,8},{2,16},{3,24},{4,32},{5,40},{6,48},{7,56},{8,64},{9,72... | collective-permute-start | bytes 98312 | tf_op jit(solution)/shard_map/ppermute | solution.py:210
  78.3 26.4 %all-to-all-start.2 = ((bf16[16,128,128]{2,1,0:T(8,128)(2,1)}), bf16[16,128,128]{2,1,0:T(8,128)(2,1)S(1)}, u32[]{:S(2)}, u32[]{:S(2)}) async-start(bf16[16,128,128]{2,1,0:T(8,128)(2,1)} %broadcast_in_dim.20), calls=%async_computation.2 | async-start | bytes 1048576 | tf_op jit(solution)/shard_map/all_to_all | solution.py:32
  87.1 14.7 %copy-start.4 = (bf16[1,1024,1024]{2,1,0:T(8,128)(2,1)S(1)}, bf16[1,1024,1024]{2,1,0:T(8,128)(2,1)}, u32[]{:S(2)}) copy-start(bf16[1,1024,1024]{2,1,0:T(8,128)(2,1)} %param.7) | copy-start | bytes 6291460
  87.2 4.4 %collective-permute-start.12 = (bf16[128,128]{1,0:T(8,128)(2,1)}, bf16[128,128]{1,0:T(8,128)(2,1)S(1)}, u32[]{:S(2)}, u32[]{:S(2)}) collective-permute-start(bf16[128,128]{1,0:T(8,128)(2,1)} %copy-done.15), channel_id=1, source_target_pairs={{0,1},{1,0},{2,3},{3,2},{4,5},{5,4},{6,7},{7,6},{8,9},{9,8},{10,11... | collective-permute-start | bytes 98312 | tf_op jit(solution)/shard_map/ppermute | solution.py:172
  92.3 3.4 %collective-permute-start.15 = (bf16[2,128,128]{2,1,0:T(8,128)(2,1)S(1)}, bf16[2,128,128]{2,1,0:T(8,128)(2,1)S(1)}, u32[]{:S(2)}, u32[]{:S(2)}) collective-permute-start(bf16[2,128,128]{2,1,0:T(8,128)(2,1)S(1)} %pad_maximum_fusion.1.refs_0_), channel_id=1, source_target_pairs={{0,6},{1,7},{2,0},{3,1},{4,2},{5,3},{6,4},{7,5},{8,14},{9,15},{10,... | collective-permute-start | bytes 196616 | tf_op jit(solution)/shard_map/ppermute | solution.py:177
  92.3 5.0 %collective-permute-start.14 = (bf16[2,128,128]{2,1,0:T(8,128)(2,1)S(1)}, bf16[2,128,128]{2,1,0:T(8,128)(2,1)S(1)}, u32[]{:S(2)}, u32[]{:S(2)}) collective-permute-start(bf16[2,128,128]{2,1,0:T(8,128)(2,1)S(1)} %pad_maximum_fusion.1.refs_0_), channel_id=1, source_target_pairs={{0,4},{1,5},{2,6},{3,7},{4,0},{5,1},{6,2},{7,3},{8,12},{9,13},{10,... | collective-permute-start | bytes 196616 | tf_op jit(solution)/shard_map/ppermute | solution.py:177
  94.3 4.6 %collective-permute-start.13 = (bf16[2,128,128]{2,1,0:T(8,128)(2,1)S(1)}, bf16[2,128,128]{2,1,0:T(8,128)(2,1)S(1)}, u32[]{:S(2)}, u32[]{:S(2)}) collective-permute-start(bf16[2,128,128]{2,1,0:T(8,128)(2,1)S(1)} %pad_maximum_fusion.1.refs_0_), channel_id=1, source_target_pairs={{0,2},{1,3},{2,4},{3,5},{4,6},{5,7},{6,0},{7,1},{8,10},{9,11},{10,... | collective-permute-start | bytes 196616 | tf_op jit(solution)/shard_map/ppermute | solution.py:177
  104.6 2.2 %copy-start.2 = (bf16[1024,2048]{1,0:T(8,128)(2,1)S(1)}, bf16[1024,2048]{1,0:T(8,128)(2,1)}, u32[]{:S(2)}) copy-start(bf16[1024,2048]{1,0:T(8,128)(2,1)} %surface_ref.3) | copy-start | bytes 12582916
  106.8 11.9 %copy-start.14 = (f32[128,128]{1,0:T(8,128)S(1)}, f32[128,128]{1,0:T(8,128)}, u32[]{:S(2)}) copy-start(f32[128,128]{1,0:T(8,128)} %param.6) | copy-start | bytes 196612
  (4 other events, 4.3 us)

commit v6 on v5

--- a/solution.py
+++ b/solution.py
@@ -74,10 +74,10 @@
     refs[-1][...] = total
 
 
-def faces_kernel(col_ref, mix_ref, group_ref, *refs):
+def faces_kernel(has_prior, col_ref, mix_ref, group_ref, *refs):
     peers = mix_ref.shape[0]
-    slice_refs, prior_refs = refs[:peers], refs[peers:-2]
-    out_ref, traces_ref = refs[-2:]
+    slice_refs, prior_refs = refs[:peers], refs[peers : peers + has_prior]
+    out_refs, traces_ref = refs[peers + has_prior : -1], refs[-1]
     group = group_ref[...]
     for k in range(peers):
         traces_ref[rotated(col_ref[0], -k, peers)] = dot(slice_refs[k][...], group)
@@ -90,11 +90,34 @@
             mixed = term if mixed is None else mixed + term
         term = dot_t(slice_refs[k][...], mixed.astype(BF))
         total = term if total is None else total + term
-    out_ref[...] = total.astype(out_ref.dtype)
-
-
-def surface_kernel(prior_ref, surface_ref, column_ref, out_ref):
-    out_ref[...] = (prior_ref[...] + dot(surface_ref[...], column_ref[...])).astype(out_ref.dtype)
+    if len(out_refs) == 1:
+        out_refs[0][...] = total
+    else:
+        divide(col_ref[0], total, traces_ref, *out_refs)
+
+
+def divide(col, total, blocks_ref, keep_ref, give_ref):
+    peers, n, ne = blocks_ref.shape
+    blocks_ref[...] = total.reshape(peers, n, ne)
+    for d in range(peers // 2):
+        keep_ref[d] = blocks_ref[rotated(col, 2 * d, peers)]
+        give_ref[d] = blocks_ref[rotated(col, 2 * d, peers) ^ 1].astype(BF)
+
+
+def surface_kernel(col_ref, prior_ref, surface_ref, column_ref, *refs):
+    total = prior_ref[...] + dot(surface_ref[...], column_ref[...])
+    if len(refs) == 1:
+        refs[0][...] = total
+    else:
+        divide(col_ref[0], total, refs[2], *refs[:2])
+
+
+def divided(peers, shape):
+    n, ne = shape[0] // peers, shape[1]
+    return [
+        jax.ShapeDtypeStruct((peers // 2, n, ne), F32),
+        jax.ShapeDtypeStruct((peers // 2, n, ne), BF),
+    ]
 
 
 def vmem():
@@ -140,27 +163,32 @@
     )(interp, dtn, group, *prior)
 
 
-def applied(prior, surface, column_block, dtype):
-    m, k = surface.shape
+def applied(place, prior, surface, column_block, peers=0):
+    (m, k), ne = surface.shape, prior.shape[1]
+    plain = [jax.ShapeDtypeStruct(prior.shape, F32)]
+    shapes = divided(peers, prior.shape) if peers else plain
     return pl.pallas_call(
         surface_kernel,
-        out_shape=jax.ShapeDtypeStruct(prior.shape, dtype),
-        in_specs=[vmem()] * 3,
-        out_specs=vmem(),
-        compiler_params=PARAMS,
-        cost_estimate=cost(1, m, k, prior.shape[1]),
+        out_shape=shapes,
+        in_specs=[smem()] + [vmem()] * 3,
+        out_specs=[vmem()] * len(shapes),
+        scratch_shapes=[pltpu.VMEM((peers, m // peers, ne), F32)] if peers else [],
+        compiler_params=PARAMS,
+        cost_estimate=cost(1, m, k, ne),
         name="applied",
-    )(prior, surface, column_block)
-
-
-def faces(place, mix, group, slices, dtype, *prior):
+    )(place, prior, surface, column_block)
+
+
+def faces(place, mix, group, slices, *prior):
     (ms, rb), ne = slices[0].shape, group.shape[-1]
     peers = len(slices)
-    return pl.pallas_call(
-        faces_kernel,
-        out_shape=jax.ShapeDtypeStruct((rb, ne), dtype),
+    plain = [jax.ShapeDtypeStruct((rb, ne), F32)]
+    shapes = divided(peers, (rb, ne)) if prior else plain
+    return pl.pallas_call(
+        functools.partial(faces_kernel, len(prior)),
+        out_shape=shapes,
         in_specs=[smem()] + [vmem()] * (2 + peers + len(prior)),
-        out_specs=vmem(),
+        out_specs=[vmem()] * len(shapes),
         scratch_shapes=[pltpu.VMEM((peers, ms, ne), F32)],
         compiler_params=PARAMS,
         cost_estimate=cost(2, peers * ms, rb, ne),
@@ -168,13 +196,29 @@
     )(place, mix, group, *slices, *prior)
 
 
+def swapped(shard, cols):
+    return lax.ppermute(shard, "col", [(i, i ^ 1) for i in range(cols)])
+
+
+def along(shard, d, cols):
+    return lax.ppermute(shard, "col", [(i, (i + 2 * d) % cols) for i in range(cols)])
+
+
+def summed_over(keep, give, cols):
+    taken = swapped(give, cols)
+    sums = keep + taken.astype(F32)
+    total = sums[0]
+    for d in range(1, cols // 2):
+        total = total + along(sums[d].astype(BF), d, cols).astype(F32)
+    return total
+
+
 def gathered(shard, cols):
-    other = lax.ppermute(shard, "col", [(i, i ^ 1) for i in range(cols)])
+    other = swapped(shard, cols)
     pair = jnp.stack([shard, other])
     pairs = [pair]
     for d in range(1, cols // 2):
-        path = [(i, (i + 2 * d) % cols) for i in range(cols)]
-        pairs.append(lax.ppermute(pair, "col", path))
+        pairs.append(along(pair, d, cols))
     return pairs
 
 
@@ -215,14 +259,13 @@
         if sweep == 0:
             mix = rows_got[0]
             own = volume(interp, dtn, group)
-            wide = applied(own, surface, column_block, F32)
-            part = faces(place, mix, group, slices, BF, wide)
+            wide = applied(place, own, surface, column_block)[0]
+            keep, give = faces(place, mix, group, slices, wide)
         else:
-            wide = faces(place, mix, group, slices, F32)
+            wide = faces(place, mix, group, slices)[0]
             own = volume(interp, dtn, group, wide)
-            part = applied(own, surface, column_block, BF)
-        parts = exchange(part.reshape(cols, n, ne), "col")
-        summed = jnp.sum(parts.astype(F32), axis=0)
+            keep, give = applied(place, own, surface, column_block, cols)
+        summed = summed_over(keep, give, cols)
         residual = excitation - current - summed
         current = current + damping * residual
     return (current, residual)

time: 120 us -> 120 us (level); the launches traced: 119 us -> 118 us
  blocking collectives: 23.7 us -> 0 us
  waiting for transfers between devices: 19.7 us -> 30.8 us
  starting transfers between devices: 46.9 us -> 57.2 us
    all_to_all x2 -> x0, blocking collectives: 23.7 us -> none  [exchange(): return lax.all_to_all(blocks, axis, split_axis=0, concat_axis=0, tiled=True)]
    ppermute x8 -> x16, waiting for transfers between devices: 8.64 us -> 19.8 us  [the longest x12 15.9 us: along(): lax.ppermute(shard, 'col', [(i, (i + 2 * d) % cols) for i in range(cols)])]
    ppermute x8 -> x16, starting transfers between devices: 10.9 us -> 21.5 us  [the longest x12 11 us: along(): lax.ppermute(shard, 'col', [(i, (i + 2 * d) % cols) for i in range(cols)])]
    all_to_all x2, starting transfers between devices: 14 us -> 12.6 us  [exchange(): return lax.all_to_all(blocks, axis, split_axis=0, concat_axis=0, tiled=True)]
  transfers between devices with their start and end apart: 19 -> 27, of which waited for: 11 -> 17; matrix products, arithmetic and copies ran while one was open for 4% -> 4% of each run, Pallas kernels for 8% -> 8%
where the time goes in v6:
time: 120 us; the launch traced here: 118 us
  starting transfers between devices  57.2 us (48%)
  waiting for transfers between devices  30.8 us (26%)
  Pallas kernels  13.8 us (12%)
  local copies, waits for them, and re-layouts  12 us (10%)
  other arithmetic  3.15 us (3%)
    ppermute x12, waiting for transfers between devices, along(): lax.ppermute(shard, 'col', [(i, (i + 2 * d) % cols) for i in range(cols)])  15.9 us
    ppermute x7, starting transfers between devices, steps(): lax.ppermute(block, 'col', [(i, (i + k) % cols) for i in range(cols)])  13 us
    all_to_all x2, starting transfers between devices, exchange(): return lax.all_to_all(blocks, axis, split_axis=0, concat_axis=0, tiled=True)  12.6 us
    ppermute x12, starting transfers between devices, along(): lax.ppermute(shard, 'col', [(i, (i + 2 * d) % cols) for i in range(cols)])  11 us
    ppermute x4, starting transfers between devices, swapped(): return lax.ppermute(shard, 'col', [(i, i ^ 1) for i in range(cols)])  10.5 us
    ppermute x2, starting transfers between devices, steps(): piece = lax.ppermute(rounded, ('row', 'col'), turned(rows, cols))  10.1 us
    ppermute x7, waiting for transfers between devices, steps(): lax.ppermute(block, 'col', [(i, (i + k) % cols) for i in range(cols)])  7.88 us
    unnamed x34, local copies, waits for them, and re-layouts  7.43 us
  transfers between devices with their start and end apart: 27, of which 17 were waited for; matrix products, arithmetic and copies ran while one was open for 4% of the time, Pallas kernels for 8%

profile of v6, /device:TPU:1, one launch (start us, length us, event | category | flops | bytes accessed | tf_op | source)
XLA Modules:
  0.0 117.9 jit_solution(18253869964035628978)
XLA Ops:
  1.5 4.6 %collective-permute-start.11 = (bf16[128,128]{1,0:T(8,128)(2,1)S(1)}, bf16[128,128]{1,0:T(8,128)(2,1)S(1)}, u32[]{:S(2)}, u32[]{:S(2)}) collective-permute-start(bf16[128,128]{1,0:T(8,128)(2,1)S(1)} %convert_element_type.65), channel_id=1, source_target_pairs={{0,0},{1,8},{2,16},{3,24},{4,32},{5,40},{6,48},{7,56},{8,64},{9,72... | collective-permute-start | bytes 98312 | tf_op jit(solution)/shard_map/ppermute | solution.py:254
  6.1 2.8 %dynamic-slice_bitcast_fusion = (bf16[128,1024]{1,0:T(8,128)(2,1)}, bf16[128,1024]{1,0:T(8,128)(2,1)}, bf16[128,1024]{1,0:T(8,128)(2,1)}, bf16[128,1024]{1,0:T(8...) fusion(bf16[1,1024,1024]{2,1,0:T(8,128)(2,1)} %param.8, ...), kind=kLoop, calls=%fused_computation.2 | loop fusion | bytes 4194336 | tf_op jit(solution)/shard_map/dynamic_slice | solution.py:237
  8.9 5.3 %collective-permute-start.9 = (bf16[128,1024]{1,0:T(8,128)(2,1)}, bf16[128,1024]{1,0:T(8,128)(2,1)S(1)}, u32[]{:S(2)}, u32[]{:S(2)}) collective-permute-start(bf16[128,1024]{1,0:T(8,128)(2,1)} %get-tuple-element.23), channel_id=1, source_target_pairs={{0,6},{1,7},{2,0},{3,1},{4,2},{5,3},{6,4},{7,5},{8,14},{9,15},{10,... | collective-permute-start | bytes 786440 | tf_op jit(solution)/shard_map/ppermute | solution.py:239
  15.2 5.1 %all-to-all-start = ((bf16[16,128,128]{2,1,0:T(8,128)(2,1)}), bf16[16,128,128]{2,1,0:T(8,128)(2,1)S(1)}, u32[]{:S(2)}, u32[]{:S(2)}) async-start(bf16[16,128,128]{2,1,0:T(8,128)(2,1)} %broadcast_in_dim.19), calls=%async_computation | async-start | bytes 1048576 | tf_op jit(solution)/shard_map/all_to_all | solution.py:32
  20.4 1.5 %collective-permute-start = (bf16[144,128]{1,0:T(8,128)(2,1)S(1)}, bf16[144,128]{1,0:T(8,128)(2,1)S(1)}, u32[]{:S(2)}, u32[]{:S(2)}) collective-permute-start(bf16[144,128]{1,0:T(8,128)(2,1)S(1)} %get-tuple-element.37), channel_id=1, source_target_pairs={{0,1},{1,0},{2,3},{3,2},{4,5},{5,4},{6,7},{7,6},{8,9},{9,8},{10,11... | collective-permute-start | bytes 110600 | tf_op jit(solution)/shard_map/ppermute | solution.py:200
  22.7 3.1 %collective-permute-start.3 = (bf16[2,144,128]{2,1,0:T(8,128)(2,1)S(1)}, bf16[2,144,128]{2,1,0:T(8,128)(2,1)S(1)}, u32[]{:S(2)}, u32[]{:S(2)}) collective-permute-start(bf16[2,144,128]{2,1,0:T(8,128)(2,1)S(1)} %pad_maximum_fusion.refs_0_), channel_id=1, source_target_pairs={{0,6},{1,7},{2,0},{3,1},{4,2},{5,3},{6,4},{7,5},{8,14},{9,15},{10,... | collective-permute-start | bytes 221192 | tf_op jit(solution)/shard_map/ppermute | solution.py:204
  26.8 2.1 %collective-permute-done.3.refs_3_ = bf16[2,144,128]{2,1,0:T(8,128)(2,1)S(1)} collective-permute-done((bf16[2,144,128]{2,1,0:T(8,128)(2,1)S(1)}, bf16[2,144,128]{2,1,0:T(8,128)(2,1)S(1)}, u32[]{:S(2)}, u32[]{:S(2)}) %collective-permute-start.3) | collective-permute-done | bytes 73760 | tf_op jit(solution)/shard_map/ppermute | solution.py:204
  28.9 4.4 %collective-permute-start.8 = (bf16[128,1024]{1,0:T(8,128)(2,1)}, bf16[128,1024]{1,0:T(8,128)(2,1)}, u32[]{:S(2)}, u32[]{:S(2)}) collective-permute-start(bf16[128,1024]{1,0:T(8,128)(2,1)} %get-tuple-element.24), channel_id=1, source_target_pairs={{0,5},{1,6},{2,7},{3,0},{4,1},{5,2},{6,3},{7,4},{8,13},{9,14},{10,... | collective-permute-start | bytes 786440 | tf_op jit(solution)/shard_map/ppermute | solution.py:239
  33.2 2.7 %collective-permute-start.6 = (bf16[128,1024]{1,0:T(8,128)(2,1)}, bf16[128,1024]{1,0:T(8,128)(2,1)}, u32[]{:S(2)}, u32[]{:S(2)}) collective-permute-start(bf16[128,1024]{1,0:T(8,128)(2,1)} %get-tuple-element.26), channel_id=1, source_target_pairs={{0,3},{1,4},{2,5},{3,6},{4,7},{5,0},{6,1},{7,2},{8,11},{9,12},{10,... | collective-permute-start | bytes 786440 | tf_op jit(solution)/shard_map/ppermute | solution.py:239
  37.3 1.6 %copy-done.3 = bf16[1,1024,1024]{2,1,0:T(8,128)(2,1)S(1)} copy-done((bf16[1,1024,1024]{2,1,0:T(8,128)(2,1)S(1)}, bf16[1,1024,1024]{2,1,0:T(8,128)(2,1)}, u32[]{:S(2)}) %copy-start.3) | copy-done | bytes 2097176
  38.9 2.8 %volume.2.prior_ref = f32[1024,128]{1,0:T(8,128)S(1)} custom-call(bf16[1024,1024]{1,0:T(8,128)(2,1)S(1)} %bitcast.66, bf16[1024,1024]{1,0:T(8,128)(2,1)S(1)} %bitcast.68, bf16[1024,128]{1,0:T(8,128)(2,1)S(1)} %get-tuple-element.9.group_ref), custom_call_target="tpu_custom_call" | custom-call | flops 805306368 | bytes 6291456 | tf_op jit(solution)/shard_map/volume/pallas_call | solution.py:155
  42.4 2.2 %copy-done.1 = bf16[1024,2048]{1,0:T(8,128)(2,1)S(1)} copy-done((bf16[1024,2048]{1,0:T(8,128)(2,1)S(1)}, bf16[1024,2048]{1,0:T(8,128)(2,1)}, u32[]{:S(2)}) %copy-start.1) | copy-done | bytes 4194328
  45.9 2.2 %collective-permute-done.8.refs_5_ = bf16[128,1024]{1,0:T(8,128)(2,1)} collective-permute-done((bf16[128,1024]{1,0:T(8,128)(2,1)}, bf16[128,1024]{1,0:T(8,128)(2,1)}, u32[]{:S(2)}, u32[]{:S(2)}) %collective-permute-start.8) | collective-permute-done | bytes 262176 | tf_op jit(solution)/shard_map/ppermute | solution.py:239
  48.1 3.3 %collective-permute-done.6.refs_3_ = bf16[128,1024]{1,0:T(8,128)(2,1)} collective-permute-done((bf16[128,1024]{1,0:T(8,128)(2,1)}, bf16[128,1024]{1,0:T(8,128)(2,1)}, u32[]{:S(2)}, u32[]{:S(2)}) %collective-permute-start.6) | collective-permute-done | bytes 262176 | tf_op jit(solution)/shard_map/ppermute | solution.py:239
  51.9 1.9 %collective-permute-done.4.refs_1_ = bf16[128,1024]{1,0:T(8,128)(2,1)} collective-permute-done((bf16[128,1024]{1,0:T(8,128)(2,1)}, bf16[128,1024]{1,0:T(8,128)(2,1)}, u32[]{:S(2)}, u32[]{:S(2)}) %collective-permute-start.4) | collective-permute-done | bytes 262176 | tf_op jit(solution)/shard_map/ppermute | solution.py:239
  53.8 2.8 %faces.2 = (f32[4,128,128]{2,1,0:T(8,128)S(1)}, bf16[4,128,128]{2,1,0:T(8,128)(2,1)S(1)}) custom-call(s32[1]{0:T(128)} %bitcast.col_ref, f32[8,16,128]{2,1,0:T(8,128)S(1)} %get-tuple-element.8.mix_ref, bf16[1024,128]{1,0:T(8,128)(2,1)S(1)} %copy-done.12, bf16[128,1024]{1,0:T(8,128)(2,1)S(1)} %get-tuple-element.29.refs_0_, ...), custom_call_target="tpu_custom_call" | custom-call | flops 536870912 | bytes 4194304 | tf_op jit(solution)/shard_map/faces/pallas_call | solution.py:187
  56.6 4.1 %collective-permute-start.12 = (bf16[4,128,128]{2,1,0:T(8,128)(2,1)S(1)}, bf16[4,128,128]{2,1,0:T(8,128)(2,1)S(1)}, u32[]{:S(2)}, u32[]{:S(2)}) collective-permute-start(bf16[4,128,128]{2,1,0:T(8,128)(2,1)S(1)} %get-tuple-element.11), channel_id=1, source_target_pairs={{0,1},{1,0},{2,3},{3,2},{4,5},{5,4},{6,7},{7,6},{8,9},{9,8},{10,11... | collective-permute-start | bytes 393224 | tf_op jit(solution)/shard_map/ppermute | solution.py:200
  61.9 2.7 %collective-permute-start.15 = (bf16[128,128]{1,0:T(8,128)(2,1)S(1)}, bf16[128,128]{1,0:T(8,128)(2,1)S(1)}, u32[]{:S(2)}, u32[]{:S(2)}) collective-permute-start(bf16[128,128]{1,0:T(8,128)(2,1)S(1)} %get-tuple-element.34), channel_id=1, source_target_pairs={{0,6},{1,7},{2,0},{3,1},{4,2},{5,3},{6,4},{7,5},{8,14},{9,15},{10,... | collective-permute-start | bytes 98312 | tf_op jit(solution)/shard_map/ppermute | solution.py:204
  65.9 3.0 %collective-permute-done.14 = bf16[128,128]{1,0:T(8,128)(2,1)S(1)} collective-permute-done((bf16[128,128]{1,0:T(8,128)(2,1)S(1)}, bf16[128,128]{1,0:T(8,128)(2,1)S(1)}, u32[]{:S(2)}, u32[]{:S(2)}) %collective-permute-start.14) | collective-permute-done | bytes 32800 | tf_op jit(solution)/shard_map/ppermute | solution.py:204
  69.5 5.5 %collective-permute-start.20 = (bf16[128,128]{1,0:T(8,128)(2,1)S(1)}, bf16[128,128]{1,0:T(8,128)(2,1)S(1)}, u32[]{:S(2)}, u32[]{:S(2)}) collective-permute-start(bf16[128,128]{1,0:T(8,128)(2,1)S(1)} %get-tuple-element.18), channel_id=1, source_target_pairs={{0,0},{1,8},{2,16},{3,24},{4,32},{5,40},{6,48},{7,56},{8,64},{9,72... | collective-permute-start | bytes 98312 | tf_op jit(solution)/shard_map/ppermute | solution.py:254
  75.0 3.1 %collective-permute-done.20 = bf16[128,128]{1,0:T(8,128)(2,1)S(1)} collective-permute-done((bf16[128,128]{1,0:T(8,128)(2,1)S(1)}, bf16[128,128]{1,0:T(8,128)(2,1)S(1)}, u32[]{:S(2)}, u32[]{:S(2)}) %collective-permute-start.20) | collective-permute-done | bytes 32800 | tf_op jit(solution)/shard_map/ppermute | solution.py:254
  79.0 7.5 %all-to-all-start.1 = ((bf16[16,128,128]{2,1,0:T(8,128)(2,1)}), bf16[16,128,128]{2,1,0:T(8,128)(2,1)S(1)}, u32[]{:S(2)}, u32[]{:S(2)}) async-start(bf16[16,128,128]{2,1,0:T(8,128)(2,1)} %broadcast_in_dim.20), calls=%async_computation.1 | async-start | bytes 1048576 | tf_op jit(solution)/shard_map/all_to_all | solution.py:32
  86.5 4.0 %collective-permute-start.16 = (bf16[128,128]{1,0:T(8,128)(2,1)}, bf16[128,128]{1,0:T(8,128)(2,1)S(1)}, u32[]{:S(2)}, u32[]{:S(2)}) collective-permute-start(bf16[128,128]{1,0:T(8,128)(2,1)} %copy-done.15), channel_id=1, source_target_pairs={{0,1},{1,0},{2,3},{3,2},{4,5},{5,4},{6,7},{7,6},{8,9},{9,8},{10,11... | collective-permute-start | bytes 98312 | tf_op jit(solution)/shard_map/ppermute | solution.py:200
  93.8 1.9 %collective-permute-done.19.refs_3_ = bf16[2,128,128]{2,1,0:T(8,128)(2,1)S(1)} collective-permute-done((bf16[2,128,128]{2,1,0:T(8,128)(2,1)S(1)}, bf16[2,128,128]{2,1,0:T(8,128)(2,1)S(1)}, u32[]{:S(2)}, u32[]{:S(2)}) %collective-permute-start.19) | collective-permute-done | bytes 65568 | tf_op jit(solution)/shard_map/ppermute | solution.py:204
  95.7 1.6 %collective-permute-done.18.refs_2_ = bf16[2,128,128]{2,1,0:T(8,128)(2,1)S(1)} collective-permute-done((bf16[2,128,128]{2,1,0:T(8,128)(2,1)S(1)}, bf16[2,128,128]{2,1,0:T(8,128)(2,1)S(1)}, u32[]{:S(2)}, u32[]{:S(2)}) %collective-permute-start.18) | collective-permute-done | bytes 65568 | tf_op jit(solution)/shard_map/ppermute | solution.py:204
  97.3 1.8 %collective-permute-done.17.refs_1_ = bf16[2,128,128]{2,1,0:T(8,128)(2,1)S(1)} collective-permute-done((bf16[2,128,128]{2,1,0:T(8,128)(2,1)S(1)}, bf16[2,128,128]{2,1,0:T(8,128)(2,1)S(1)}, u32[]{:S(2)}, u32[]{:S(2)}) %collective-permute-start.17) | collective-permute-done | bytes 65568 | tf_op jit(solution)/shard_map/ppermute | solution.py:204
  99.1 2.8 %faces.3.refs_0_ = f32[1024,128]{1,0:T(8,128)S(1)} custom-call(s32[1]{0:T(128)} %bitcast.col_ref, f32[8,16,128]{2,1,0:T(8,128)S(1)} %get-tuple-element.8.mix_ref, bf16[1024,128]{1,0:T(8,128)(2,1)S(1)} %assemble.3.group_ref, bf16[128,1024]{1,0:T(8,128)(2,1)S(1)} %get-tuple-element.29.refs_0_, bf16[128,1024]{1,0:T(8,128)(2,1)} %collective-permute-done.4.refs_1_, ...), custom_call_target="tpu_custom_call" | custom-call | flops 536870912 | bytes 4194304 | tf_op jit(solution)/shard_map/faces/pallas_call | solution.py:187
  101.9 2.8 %volume.3.prior_ref = f32[1024,128]{1,0:T(8,128)S(1)} custom-call(bf16[1024,1024]{1,0:T(8,128)(2,1)S(1)} %bitcast.67, bf16[1024,1024]{1,0:T(8,128)(2,1)S(1)} %bitcast.69, bf16[1024,128]{1,0:T(8,128)(2,1)S(1)} %assemble.3.group_ref, f32[1024,128]{1,0:T(8,128)S(1)} %faces.3.refs_0_), custom_call_target="tpu_custom_call" | custom-call | flops 805306368 | bytes 6291456 | tf_op jit(solution)/shard_map/volume/pallas_call | solution.py:155
  104.8 2.2 %copy-done.2 = bf16[1024,2048]{1,0:T(8,128)(2,1)S(1)} copy-done((bf16[1024,2048]{1,0:T(8,128)(2,1)S(1)}, bf16[1024,2048]{1,0:T(8,128)(2,1)}, u32[]{:S(2)}) %copy-start.2) | copy-done | bytes 4194328
  106.9 1.3 %applied.3 = (f32[4,128,128]{2,1,0:T(8,128)S(1)}, bf16[4,128,128]{2,1,0:T(8,128)(2,1)S(1)}) custom-call(s32[1]{0:T(128)} %bitcast.col_ref, f32[1024,128]{1,0:T(8,128)S(1)} %volume.3.prior_ref, bf16[1024,2048]{1,0:T(8,128)(2,1)S(1)} %copy-done.2, bf16[2048,128]{1,0:T(8,128)(2,1)S(1)} %bitcast.71), custom_call_target="tpu_custom_call" | custom-call | flops 536870912 | bytes 4194304 | tf_op jit(solution)/shard_map/applied/pallas_call | solution.py:170
  110.6 2.4 %collective-permute-start.24 = (bf16[128,128]{1,0:T(8,128)(2,1)S(1)}, bf16[128,128]{1,0:T(8,128)(2,1)S(1)}, u32[]{:S(2)}, u32[]{:S(2)}) collective-permute-start(bf16[128,128]{1,0:T(8,128)(2,1)S(1)} %get-tuple-element.31), channel_id=1, source_target_pairs={{0,6},{1,7},{2,0},{3,1},{4,2},{5,3},{6,4},{7,5},{8,14},{9,15},{10,... | collective-permute-start | bytes 98312 | tf_op jit(solution)/shard_map/ppermute | solution.py:204
  114.3 3.0 %collective-permute-done.23 = bf16[128,128]{1,0:T(8,128)(2,1)S(1)} collective-permute-done((bf16[128,128]{1,0:T(8,128)(2,1)S(1)}, bf16[128,128]{1,0:T(8,128)(2,1)S(1)}, u32[]{:S(2)}, u32[]{:S(2)}) %collective-permute-start.23) | collective-permute-done | bytes 32800 | tf_op jit(solution)/shard_map/ppermute | solution.py:204
  (81 shorter events, 19.0 us)
Async XLA Ops:
  1.5 12.8 %collective-permute-start.11 = (bf16[128,128]{1,0:T(8,128)(2,1)S(1)}, bf16[128,128]{1,0:T(8,128)(2,1)S(1)}, u32[]{:S(2)}, u32[]{:S(2)}) collective-permute-start(bf16[128,128]{1,0:T(8,128)(2,1)S(1)} %convert_element_type.65), channel_id=1, source_target_pairs={{0,0},{1,8},{2,16},{3,24},{4,32},{5,40},{6,48},{7,56},{8,64},{9,72... | collective-permute-start | bytes 98312 | tf_op jit(solution)/shard_map/ppermute | solution.py:254
  8.9 28.4 %copy-start = (bf16[1,1024,1024]{2,1,0:T(8,128)(2,1)S(1)}, bf16[1,1024,1024]{2,1,0:T(8,128)(2,1)}, u32[]{:S(2)}) copy-start(bf16[1,1024,1024]{2,1,0:T(8,128)(2,1)} %param.8) | copy-start | bytes 6291460
  8.9 27.1 %collective-permute-start.10 = (bf16[128,1024]{1,0:T(8,128)(2,1)}, bf16[128,1024]{1,0:T(8,128)(2,1)S(1)}, u32[]{:S(2)}, u32[]{:S(2)}) collective-permute-start(bf16[128,1024]{1,0:T(8,128)(2,1)} %get-tuple-element.22), channel_id=1, source_target_pairs={{0,7},{1,0},{2,1},{3,2},{4,3},{5,4},{6,5},{7,6},{8,15},{9,8},{10,9... | collective-permute-start | bytes 786440 | tf_op jit(solution)/shard_map/ppermute | solution.py:239
  8.9 27.7 %collective-permute-start.9 = (bf16[128,1024]{1,0:T(8,128)(2,1)}, bf16[128,1024]{1,0:T(8,128)(2,1)S(1)}, u32[]{:S(2)}, u32[]{:S(2)}) collective-permute-start(bf16[128,1024]{1,0:T(8,128)(2,1)} %get-tuple-element.23), channel_id=1, source_target_pairs={{0,6},{1,7},{2,0},{3,1},{4,2},{5,3},{6,4},{7,5},{8,14},{9,15},{10,... | collective-permute-start | bytes 786440 | tf_op jit(solution)/shard_map/ppermute | solution.py:239
  15.2 27.2 %all-to-all-start = ((bf16[16,128,128]{2,1,0:T(8,128)(2,1)}), bf16[16,128,128]{2,1,0:T(8,128)(2,1)S(1)}, u32[]{:S(2)}, u32[]{:S(2)}) async-start(bf16[16,128,128]{2,1,0:T(8,128)(2,1)} %broadcast_in_dim.19), calls=%async_computation | async-start | bytes 1048576 | tf_op jit(solution)/shard_map/all_to_all | solution.py:32
  20.4 2.3 %collective-permute-start = (bf16[144,128]{1,0:T(8,128)(2,1)S(1)}, bf16[144,128]{1,0:T(8,128)(2,1)S(1)}, u32[]{:S(2)}, u32[]{:S(2)}) collective-permute-start(bf16[144,128]{1,0:T(8,128)(2,1)S(1)} %get-tuple-element.37), channel_id=1, source_target_pairs={{0,1},{1,0},{2,3},{3,2},{4,5},{5,4},{6,7},{7,6},{8,9},{9,8},{10,11... | collective-permute-start | bytes 110600 | tf_op jit(solution)/shard_map/ppermute | solution.py:200
  22.7 6.1 %collective-permute-start.3 = (bf16[2,144,128]{2,1,0:T(8,128)(2,1)S(1)}, bf16[2,144,128]{2,1,0:T(8,128)(2,1)S(1)}, u32[]{:S(2)}, u32[]{:S(2)}) collective-permute-start(bf16[2,144,128]{2,1,0:T(8,128)(2,1)S(1)} %pad_maximum_fusion.refs_0_), channel_id=1, source_target_pairs={{0,6},{1,7},{2,0},{3,1},{4,2},{5,3},{6,4},{7,5},{8,14},{9,15},{10,... | collective-permute-start | bytes 221192 | tf_op jit(solution)/shard_map/ppermute | solution.py:204
  25.9 7.4 %collective-permute-start.2 = (bf16[2,144,128]{2,1,0:T(8,128)(2,1)S(1)}, bf16[2,144,128]{2,1,0:T(8,128)(2,1)S(1)}, u32[]{:S(2)}, u32[]{:S(2)}) collective-permute-start(bf16[2,144,128]{2,1,0:T(8,128)(2,1)S(1)} %pad_maximum_fusion.refs_0_), channel_id=1, source_target_pairs={{0,4},{1,5},{2,6},{3,7},{4,0},{5,1},{6,2},{7,3},{8,12},{9,13},{10,... | collective-permute-start | bytes 221192 | tf_op jit(solution)/shard_map/ppermute | solution.py:204
  26.8 6.5 %collective-permute-start.1 = (bf16[2,144,128]{2,1,0:T(8,128)(2,1)S(1)}, bf16[2,144,128]{2,1,0:T(8,128)(2,1)S(1)}, u32[]{:S(2)}, u32[]{:S(2)}) collective-permute-start(bf16[2,144,128]{2,1,0:T(8,128)(2,1)S(1)} %pad_maximum_fusion.refs_0_), channel_id=1, source_target_pairs={{0,2},{1,3},{2,4},{3,5},{4,6},{5,7},{6,0},{7,1},{8,10},{9,11},{10,... | collective-permute-start | bytes 221192 | tf_op jit(solution)/shard_map/ppermute | solution.py:204
  28.9 19.2 %collective-permute-start.8 = (bf16[128,1024]{1,0:T(8,128)(2,1)}, bf16[128,1024]{1,0:T(8,128)(2,1)}, u32[]{:S(2)}, u32[]{:S(2)}) collective-permute-start(bf16[128,1024]{1,0:T(8,128)(2,1)} %get-tuple-element.24), channel_id=1, source_target_pairs={{0,5},{1,6},{2,7},{3,0},{4,1},{5,2},{6,3},{7,4},{8,13},{9,14},{10,... | collective-permute-start | bytes 786440 | tf_op jit(solution)/shard_map/ppermute | solution.py:239
  33.2 14.9 %collective-permute-start.7 = (bf16[128,1024]{1,0:T(8,128)(2,1)}, bf16[128,1024]{1,0:T(8,128)(2,1)}, u32[]{:S(2)}, u32[]{:S(2)}) collective-permute-start(bf16[128,1024]{1,0:T(8,128)(2,1)} %get-tuple-element.25), channel_id=1, source_target_pairs={{0,4},{1,5},{2,6},{3,7},{4,0},{5,1},{6,2},{7,3},{8,12},{9,13},{10,... | collective-permute-start | bytes 786440 | tf_op jit(solution)/shard_map/ppermute | solution.py:239
  33.2 18.2 %collective-permute-start.6 = (bf16[128,1024]{1,0:T(8,128)(2,1)}, bf16[128,1024]{1,0:T(8,128)(2,1)}, u32[]{:S(2)}, u32[]{:S(2)}) collective-permute-start(bf16[128,1024]{1,0:T(8,128)(2,1)} %get-tuple-element.26), channel_id=1, source_target_pairs={{0,3},{1,4},{2,5},{3,6},{4,7},{5,0},{6,1},{7,2},{8,11},{9,12},{10,... | collective-permute-start | bytes 786440 | tf_op jit(solution)/shard_map/ppermute | solution.py:239
  36.0 15.9 %collective-permute-start.5 = (bf16[128,1024]{1,0:T(8,128)(2,1)}, bf16[128,1024]{1,0:T(8,128)(2,1)}, u32[]{:S(2)}, u32[]{:S(2)}) collective-permute-start(bf16[128,1024]{1,0:T(8,128)(2,1)} %get-tuple-element.27), channel_id=1, source_target_pairs={{0,2},{1,3},{2,4},{3,5},{4,6},{5,7},{6,0},{7,1},{8,10},{9,11},{10,... | collective-permute-start | bytes 786440 | tf_op jit(solution)/shard_map/ppermute | solution.py:239
  37.2 16.5 %collective-permute-start.4 = (bf16[128,1024]{1,0:T(8,128)(2,1)}, bf16[128,1024]{1,0:T(8,128)(2,1)}, u32[]{:S(2)}, u32[]{:S(2)}) collective-permute-start(bf16[128,1024]{1,0:T(8,128)(2,1)} %get-tuple-element.28), channel_id=1, source_target_pairs={{0,1},{1,2},{2,3},{3,4},{4,5},{5,6},{6,7},{7,0},{8,9},{9,10},{10,1... | collective-permute-start | bytes 786440 | tf_op jit(solution)/shard_map/ppermute | solution.py:239
  45.9 23.0 %copy-start.13 = (f32[128,128]{1,0:T(8,128)S(1)}, f32[128,128]{1,0:T(8,128)}, u32[]{:S(2)}) copy-start(f32[128,128]{1,0:T(8,128)} %param.6) | copy-start | bytes 196612
  56.6 42.5 %copy-start.7 = (bf16[128,1024]{1,0:T(8,128)(2,1)S(1)}, bf16[128,1024]{1,0:T(8,128)(2,1)}, u32[]{:S(2)}) copy-start(bf16[128,1024]{1,0:T(8,128)(2,1)} %copy-done.5) | copy-start | bytes 786436
  56.6 42.5 %copy-start.10 = (bf16[128,1024]{1,0:T(8,128)(2,1)S(1)}, bf16[128,1024]{1,0:T(8,128)(2,1)}, u32[]{:S(2)}) copy-start(bf16[128,1024]{1,0:T(8,128)(2,1)} %copy-done.8) | copy-start | bytes 786436
  56.6 5.1 %collective-permute-start.12 = (bf16[4,128,128]{2,1,0:T(8,128)(2,1)S(1)}, bf16[4,128,128]{2,1,0:T(8,128)(2,1)S(1)}, u32[]{:S(2)}, u32[]{:S(2)}) collective-permute-start(bf16[4,128,128]{2,1,0:T(8,128)(2,1)S(1)} %get-tuple-element.11), channel_id=1, source_target_pairs={{0,1},{1,0},{2,3},{3,2},{4,5},{5,4},{6,7},{7,6},{8,9},{9,8},{10,11... | collective-permute-start | bytes 393224 | tf_op jit(solution)/shard_map/ppermute | solution.py:200
  61.8 4.0 %collective-permute-start.13 = (bf16[128,128]{1,0:T(8,128)(2,1)S(1)}, bf16[128,128]{1,0:T(8,128)(2,1)S(1)}, u32[]{:S(2)}, u32[]{:S(2)}) collective-permute-start(bf16[128,128]{1,0:T(8,128)(2,1)S(1)} %get-tuple-element.33), channel_id=1, source_target_pairs={{0,2},{1,3},{2,4},{3,5},{4,6},{5,7},{6,0},{7,1},{8,10},{9,11},{10,... | collective-permute-start | bytes 98312 | tf_op jit(solution)/shard_map/ppermute | solution.py:204
  61.9 4.0 %collective-permute-start.15 = (bf16[128,128]{1,0:T(8,128)(2,1)S(1)}, bf16[128,128]{1,0:T(8,128)(2,1)S(1)}, u32[]{:S(2)}, u32[]{:S(2)}) collective-permute-start(bf16[128,128]{1,0:T(8,128)(2,1)S(1)} %get-tuple-element.34), channel_id=1, source_target_pairs={{0,6},{1,7},{2,0},{3,1},{4,2},{5,3},{6,4},{7,5},{8,14},{9,15},{10,... | collective-permute-start | bytes 98312 | tf_op jit(solution)/shard_map/ppermute | solution.py:204
  64.6 4.3 %collective-permute-start.14 = (bf16[128,128]{1,0:T(8,128)(2,1)S(1)}, bf16[128,128]{1,0:T(8,128)(2,1)S(1)}, u32[]{:S(2)}, u32[]{:S(2)}) collective-permute-start(bf16[128,128]{1,0:T(8,128)(2,1)S(1)} %get-tuple-element.35), channel_id=1, source_target_pairs={{0,4},{1,5},{2,6},{3,7},{4,0},{5,1},{6,2},{7,3},{8,12},{9,13},{10,... | collective-permute-start | bytes 98312 | tf_op jit(solution)/shard_map/ppermute | solution.py:204
  69.5 8.6 %collective-permute-start.20 = (bf16[128,128]{1,0:T(8,128)(2,1)S(1)}, bf16[128,128]{1,0:T(8,128)(2,1)S(1)}, u32[]{:S(2)}, u32[]{:S(2)}) collective-permute-start(bf16[128,128]{1,0:T(8,128)(2,1)S(1)} %get-tuple-element.18), channel_id=1, source_target_pairs={{0,0},{1,8},{2,16},{3,24},{4,32},{5,40},{6,48},{7,56},{8,64},{9,72... | collective-permute-start | bytes 98312 | tf_op jit(solution)/shard_map/ppermute | solution.py:254
  79.0 25.7 %all-to-all-start.1 = ((bf16[16,128,128]{2,1,0:T(8,128)(2,1)}), bf16[16,128,128]{2,1,0:T(8,128)(2,1)S(1)}, u32[]{:S(2)}, u32[]{:S(2)}) async-start(bf16[16,128,128]{2,1,0:T(8,128)(2,1)} %broadcast_in_dim.20), calls=%async_computation.1 | async-start | bytes 1048576 | tf_op jit(solution)/shard_map/all_to_all | solution.py:32
  86.5 15.4 %copy-start.4 = (bf16[1,1024,1024]{2,1,0:T(8,128)(2,1)S(1)}, bf16[1,1024,1024]{2,1,0:T(8,128)(2,1)}, u32[]{:S(2)}) copy-start(bf16[1,1024,1024]{2,1,0:T(8,128)(2,1)} %param.7) | copy-start | bytes 6291460
  86.5 5.0 %collective-permute-start.16 = (bf16[128,128]{1,0:T(8,128)(2,1)}, bf16[128,128]{1,0:T(8,128)(2,1)S(1)}, u32[]{:S(2)}, u32[]{:S(2)}) collective-permute-start(bf16[128,128]{1,0:T(8,128)(2,1)} %copy-done.15), channel_id=1, source_target_pairs={{0,1},{1,0},{2,3},{3,2},{4,5},{5,4},{6,7},{7,6},{8,9},{9,8},{10,11... | collective-permute-start | bytes 98312 | tf_op jit(solution)/shard_map/ppermute | solution.py:200
  92.3 3.4 %collective-permute-start.19 = (bf16[2,128,128]{2,1,0:T(8,128)(2,1)S(1)}, bf16[2,128,128]{2,1,0:T(8,128)(2,1)S(1)}, u32[]{:S(2)}, u32[]{:S(2)}) collective-permute-start(bf16[2,128,128]{2,1,0:T(8,128)(2,1)S(1)} %pad_maximum_fusion.1.refs_0_), channel_id=1, source_target_pairs={{0,6},{1,7},{2,0},{3,1},{4,2},{5,3},{6,4},{7,5},{8,14},{9,15},{10,... | collective-permute-start | bytes 196616 | tf_op jit(solution)/shard_map/ppermute | solution.py:204
  92.3 5.0 %collective-permute-start.18 = (bf16[2,128,128]{2,1,0:T(8,128)(2,1)S(1)}, bf16[2,128,128]{2,1,0:T(8,128)(2,1)S(1)}, u32[]{:S(2)}, u32[]{:S(2)}) collective-permute-start(bf16[2,128,128]{2,1,0:T(8,128)(2,1)S(1)} %pad_maximum_fusion.1.refs_0_), channel_id=1, source_target_pairs={{0,4},{1,5},{2,6},{3,7},{4,0},{5,1},{6,2},{7,3},{8,12},{9,13},{10,... | collective-permute-start | bytes 196616 | tf_op jit(solution)/shard_map/ppermute | solution.py:204
  93.3 5.8 %collective-permute-start.17 = (bf16[2,128,128]{2,1,0:T(8,128)(2,1)S(1)}, bf16[2,128,128]{2,1,0:T(8,128)(2,1)S(1)}, u32[]{:S(2)}, u32[]{:S(2)}) collective-permute-start(bf16[2,128,128]{2,1,0:T(8,128)(2,1)S(1)} %pad_maximum_fusion.1.refs_0_), channel_id=1, source_target_pairs={{0,2},{1,3},{2,4},{3,5},{4,6},{5,7},{6,0},{7,1},{8,10},{9,11},{10,... | collective-permute-start | bytes 196616 | tf_op jit(solution)/shard_map/ppermute | solution.py:204
  108.3 1.9 %collective-permute-start.21 = (bf16[4,128,128]{2,1,0:T(8,128)(2,1)S(1)}, bf16[4,128,128]{2,1,0:T(8,128)(2,1)S(1)}, u32[]{:S(2)}, u32[]{:S(2)}) collective-permute-start(bf16[4,128,128]{2,1,0:T(8,128)(2,1)S(1)} %get-tuple-element.13), channel_id=1, source_target_pairs={{0,1},{1,0},{2,3},{3,2},{4,5},{5,4},{6,7},{7,6},{8,9},{9,8},{10,11... | collective-permute-start | bytes 393224 | tf_op jit(solution)/shard_map/ppermute | solution.py:200
  110.2 4.0 %collective-permute-start.22 = (bf16[128,128]{1,0:T(8,128)(2,1)S(1)}, bf16[128,128]{1,0:T(8,128)(2,1)S(1)}, u32[]{:S(2)}, u32[]{:S(2)}) collective-permute-start(bf16[128,128]{1,0:T(8,128)(2,1)S(1)} %get-tuple-element.30), channel_id=1, source_target_pairs={{0,2},{1,3},{2,4},{3,5},{4,6},{5,7},{6,0},{7,1},{8,10},{9,11},{10,... | collective-permute-start | bytes 98312 | tf_op jit(solution)/shard_map/ppermute | solution.py:204
  110.6 3.7 %collective-permute-start.24 = (bf16[128,128]{1,0:T(8,128)(2,1)S(1)}, bf16[128,128]{1,0:T(8,128)(2,1)S(1)}, u32[]{:S(2)}, u32[]{:S(2)}) collective-permute-start(bf16[128,128]{1,0:T(8,128)(2,1)S(1)} %get-tuple-element.31), channel_id=1, source_target_pairs={{0,6},{1,7},{2,0},{3,1},{4,2},{5,3},{6,4},{7,5},{8,14},{9,15},{10,... | collective-permute-start | bytes 98312 | tf_op jit(solution)/shard_map/ppermute | solution.py:204
  113.0 4.3 %collective-permute-start.23 = (bf16[128,128]{1,0:T(8,128)(2,1)S(1)}, bf16[128,128]{1,0:T(8,128)(2,1)S(1)}, u32[]{:S(2)}, u32[]{:S(2)}) collective-permute-start(bf16[128,128]{1,0:T(8,128)(2,1)S(1)} %get-tuple-element.32), channel_id=1, source_target_pairs={{0,4},{1,5},{2,6},{3,7},{4,0},{5,1},{6,2},{7,3},{8,12},{9,13},{10,... | collective-permute-start | bytes 98312 | tf_op jit(solution)/shard_map/ppermute | solution.py:204
  (12 other events, 64.2 us)

commit v7 on v6

--- a/solution.py
+++ b/solution.py
@@ -53,8 +53,8 @@
     return rotated(col, -2 * distance, peers) ^ j
 
 
-def assemble_kernel(outs, col_ref, *refs):
-    pair_refs, group_ref = refs[:-outs], refs[-outs]
+def assemble_kernel(count, outs, col_ref, *refs):
+    pair_refs, group_ref = refs[:count], refs[-outs]
     peers = 2 * len(pair_refs)
     n = group_ref.shape[0] // peers
     for d, pair_ref in enumerate(pair_refs):
@@ -65,11 +65,11 @@
                 refs[-1][s] = pair_ref[j, n:, :].astype(F32)
 
 
-def volume_kernel(interp_ref, dtn_ref, group_ref, *refs):
+def volume_kernel(has_prior, interp_ref, dtn_ref, group_ref, *refs):
     traces = dot(interp_ref[...], group_ref[...]).astype(BF)
     response = dot(dtn_ref[...], traces).astype(BF)
     total = dot_t(interp_ref[...], response)
-    if len(refs) == 2:
+    if has_prior:
         total = total + refs[0][...]
     refs[-1][...] = total
 
@@ -100,8 +100,8 @@
     peers, n, ne = blocks_ref.shape
     blocks_ref[...] = total.reshape(peers, n, ne)
     for d in range(peers // 2):
-        keep_ref[d] = blocks_ref[rotated(col, 2 * d, peers)]
-        give_ref[d] = blocks_ref[rotated(col, 2 * d, peers) ^ 1].astype(BF)
+        keep_ref[d] = blocks_ref[col ^ (2 * d)]
+        give_ref[d] = blocks_ref[col ^ (2 * d + 1)].astype(BF)
 
 
 def surface_kernel(col_ref, prior_ref, surface_ref, column_ref, *refs):
@@ -112,6 +112,46 @@
         divide(col_ref[0], total, refs[2], *refs[:2])
 
 
+def streamed_kernel(col_ref, prior_ref, surface_ref, column_ref, *refs):
+    keep_ref, give_ref, blocks_ref, parts_ref, sems = refs
+    pieces, high, _ = parts_ref.shape
+    copies = [
+        pltpu.make_async_copy(
+            surface_ref.at[pl.ds(p * high, high)], parts_ref.at[p], sems.at[p]
+        )
+        for p in range(pieces)
+    ]
+    for copy in copies:
+        copy.start()
+    column = column_ref[...]
+    each, n, ne = high // blocks_ref.shape[1], blocks_ref.shape[1], blocks_ref.shape[2]
+    for p, copy in enumerate(copies):
+        copy.wait()
+        total = prior_ref[pl.ds(p * high, high), :] + dot(parts_ref[p], column)
+        blocks_ref[pl.ds(p * each, each)] = total.reshape(each, n, ne)
+    for d in range(blocks_ref.shape[0] // 2):
+        keep_ref[d] = blocks_ref[col_ref[0] ^ (2 * d)]
+        give_ref[d] = blocks_ref[col_ref[0] ^ (2 * d + 1)].astype(BF)
+
+
+def streamed(place, prior, surface, column_block, peers, pieces=4):
+    (m, k), ne = surface.shape, prior.shape[1]
+    shapes = divided(peers, prior.shape)
+    return pl.pallas_call(
+        streamed_kernel,
+        out_shape=shapes,
+        in_specs=[smem(), vmem(), hbm(), vmem()],
+        out_specs=[vmem()] * len(shapes),
+        scratch_shapes=[
+            pltpu.VMEM((peers, m // peers, ne), F32),
+            pltpu.VMEM((pieces, m // pieces, k), BF),
+            pltpu.SemaphoreType.DMA((pieces,)),
+        ],
+        compiler_params=pltpu.CompilerParams(vmem_limit_bytes=60 * 2**20),
+        name="streamed",
+    )(place, prior, surface, column_block)
+
+
 def divided(peers, shape):
     n, ne = shape[0] // peers, shape[1]
     return [
@@ -124,6 +164,10 @@
     return pl.BlockSpec(memory_space=pltpu.VMEM)
 
 
+def hbm():
+    return pl.BlockSpec(memory_space=pl.ANY)
+
+
 def cost(products, m, k, ne):
     return pl.CostEstimate(
         flops=2 * products * m * k * ne, bytes_accessed=2 * products * m * k, transcendentals=0
@@ -134,33 +178,34 @@
     return pl.BlockSpec(memory_space=pltpu.SMEM)
 
 
-def assemble(place, pairs, n):
+def assemble(place, pairs, n, held):
     peers, (_, high, ne) = 2 * len(pairs), pairs[0].shape
     shapes = [jax.ShapeDtypeStruct((peers * n, ne), BF)]
     if high > n:
         shapes.append(jax.ShapeDtypeStruct((peers, high - n, ne), F32))
     return pl.pallas_call(
-        functools.partial(assemble_kernel, len(shapes)),
+        functools.partial(assemble_kernel, len(pairs), len(shapes)),
         out_shape=shapes,
-        in_specs=[smem()] + [vmem()] * len(pairs),
+        in_specs=[smem()] + [vmem()] * len(pairs) + [hbm()] * len(held),
         out_specs=[vmem()] * len(shapes),
         compiler_params=PARAMS,
+        cost_estimate=cost(1, 256, 1024, 1),
         name="assemble",
-    )(place, *pairs)
-
-
-def volume(interp, dtn, group, *prior):
+    )(place, *pairs, *held)
+
+
+def volume(interp, dtn, group, prior=(), held=()):
     m, rb = interp.shape
     ne = group.shape[-1]
     return pl.pallas_call(
-        volume_kernel,
+        functools.partial(volume_kernel, len(prior)),
         out_shape=jax.ShapeDtypeStruct((rb, ne), F32),
-        in_specs=[vmem()] * (3 + len(prior)),
+        in_specs=[vmem()] * (3 + len(prior) + len(held)),
         out_specs=vmem(),
         compiler_params=PARAMS,
         cost_estimate=cost(3, m, rb, ne),
         name="volume",
-    )(interp, dtn, group, *prior)
+    )(interp, dtn, group, *prior, *held)
 
 
 def applied(place, prior, surface, column_block, peers=0):
@@ -196,8 +241,8 @@
     )(place, mix, group, *slices, *prior)
 
 
-def swapped(shard, cols):
-    return lax.ppermute(shard, "col", [(i, i ^ 1) for i in range(cols)])
+def swapped(shard, cols, bits=1):
+    return lax.ppermute(shard, "col", [(i, i ^ bits) for i in range(cols)])
 
 
 def along(shard, d, cols):
@@ -207,10 +252,9 @@
 def summed_over(keep, give, cols):
     taken = swapped(give, cols)
     sums = keep + taken.astype(F32)
-    total = sums[0]
-    for d in range(1, cols // 2):
-        total = total + along(sums[d].astype(BF), d, cols).astype(F32)
-    return total
+    taken = swapped(sums[1:3].astype(BF), cols, 2).astype(F32)
+    last = swapped((sums[3] + taken[1]).astype(BF), cols, 6).astype(F32)
+    return sums[0] + taken[0] + last
 
 
 def gathered(shard, cols):
@@ -255,7 +299,7 @@
         column_block = copy_for_each(piece, "row").reshape(rows * n, ne)
         sent = jnp.concatenate([rounded, extra], axis=0) if sweep == 0 else rounded
         pairs = gathered(sent, cols)
-        group, *rows_got = assemble(place, pairs, n)
+        group, *rows_got = assemble(place, pairs, n, () if sweep else (column_block,))
         if sweep == 0:
             mix = rows_got[0]
             own = volume(interp, dtn, group)
@@ -263,8 +307,8 @@
             keep, give = faces(place, mix, group, slices, wide)
         else:
             wide = faces(place, mix, group, slices)[0]
-            own = volume(interp, dtn, group, wide)
-            keep, give = applied(place, own, surface, column_block, cols)
+            own = volume(interp, dtn, group, (wide,))
+            keep, give = streamed(place, own, surface, column_block, cols)
         summed = summed_over(keep, give, cols)
         residual = excitation - current - summed
         current = current + damping * residual

time: 120 us -> 126 us (1.050)
  waiting for transfers between devices: 30.8 us -> 34.9 us
  Pallas kernels: 13.8 us -> 17.4 us
  starting transfers between devices: 57.2 us -> 54.2 us
    ppermute x4 -> x8, waiting for transfers between devices: 3.91 us -> 16.3 us  [swapped(): return lax.ppermute(shard, 'col', [(i, i ^ bits) for i in range(cols)])]
    ppermute x12 -> x6, waiting for transfers between devices: 15.9 us -> 7.3 us  [along(): lax.ppermute(shard, 'col', [(i, (i + 2 * d) % cols) for i in range(cols)])]
    ppermute x12 -> x6, starting transfers between devices: 11 us -> 5.51 us  [along(): lax.ppermute(shard, 'col', [(i, (i + 2 * d) % cols) for i in range(cols)])]
    pallas_call x4 -> x5, Pallas kernels: 5.6 us -> 10.5 us  [the longest x2 5.55 us: volume(): pl.pallas_call(functools.partial(volume_kernel, len(prior)), out_shape=ja...]
    ppermute x4 -> x8, starting transfers between devices: 10.5 us -> 13 us  [swapped(): return lax.ppermute(shard, 'col', [(i, i ^ bits) for i in range(cols)])]
    pallas_call x2 -> x1, Pallas kernels: 2.58 us -> 1.26 us  [applied(): pl.pallas_call(surface_kernel, out_shape=shapes, in_specs=[smem()] + [vme...]
    unnamed x34 -> x32, local copies, waits for them, and re-layouts: 7.43 us -> 7.79 us
  transfers between devices with their start and end apart: 27 -> 25, of which waited for: 17 -> 17; matrix products, arithmetic and copies ran while one was open for 4% -> 4% of each run, Pallas kernels for 8% -> 8%
where the time goes in v7:
time: 126 us; the launch traced here: 124 us
  starting transfers between devices  54.2 us (43%)
  waiting for transfers between devices  34.9 us (28%)
  Pallas kernels  17.4 us (14%)
  local copies, waits for them, and re-layouts  12.4 us (10%)
  other arithmetic  4.09 us (3%)
    ppermute x8, waiting for transfers between devices, swapped(): return lax.ppermute(shard, 'col', [(i, i ^ bits) for i in range(cols)])  16.3 us
    ppermute x7, starting transfers between devices, steps(): lax.ppermute(block, 'col', [(i, (i + k) % cols) for i in range(cols)])  13 us
    ppermute x8, starting transfers between devices, swapped(): return lax.ppermute(shard, 'col', [(i, i ^ bits) for i in range(cols)])  13 us
    all_to_all x2, starting transfers between devices, exchange(): return lax.all_to_all(blocks, axis, split_axis=0, concat_axis=0, tiled=True)  12 us
    ppermute x2, starting transfers between devices, steps(): piece = lax.ppermute(rounded, ('row', 'col'), turned(rows, cols))  10.6 us
    ppermute x7, waiting for transfers between devices, steps(): lax.ppermute(block, 'col', [(i, (i + k) % cols) for i in range(cols)])  8.22 us
    unnamed x32, local copies, waits for them, and re-layouts  7.79 us
    ppermute x6, waiting for transfers between devices, along(): lax.ppermute(shard, 'col', [(i, (i + 2 * d) % cols) for i in range(cols)])  7.3 us
  transfers between devices with their start and end apart: 25, of which 17 were waited for; matrix products, arithmetic and copies ran while one was open for 4% of the time, Pallas kernels for 8%

profile of v7, /device:TPU:1, one launch (start us, length us, event | category | flops | bytes accessed | tf_op | source)
XLA Modules:
  0.0 123.9 jit_solution(17406094869705452985)
XLA Ops:
  1.5 4.6 %collective-permute-start.4 = (bf16[128,128]{1,0:T(8,128)(2,1)S(1)}, bf16[128,128]{1,0:T(8,128)(2,1)S(1)}, u32[]{:S(2)}, u32[]{:S(2)}) collective-permute-start(bf16[128,128]{1,0:T(8,128)(2,1)S(1)} %convert_element_type.49), channel_id=1, source_target_pairs={{0,0},{1,8},{2,16},{3,24},{4,32},{5,40},{6,48},{7,56},{8,64},{9,72... | collective-permute-start | bytes 98312 | tf_op jit(solution)/shard_map/ppermute | solution.py:298
  6.1 2.8 %dynamic-slice_bitcast_fusion = (bf16[128,1024]{1,0:T(8,128)(2,1)}, bf16[128,1024]{1,0:T(8,128)(2,1)}, bf16[128,1024]{1,0:T(8,128)(2,1)}, bf16[128,1024]{1,0:T(8...) fusion(bf16[1,1024,1024]{2,1,0:T(8,128)(2,1)} %param.8, ...), kind=kLoop, calls=%fused_computation.2 | loop fusion | bytes 4194336 | tf_op jit(solution)/shard_map/dynamic_slice | solution.py:281
  8.9 5.3 %collective-permute-start.10 = (bf16[128,1024]{1,0:T(8,128)(2,1)}, bf16[128,1024]{1,0:T(8,128)(2,1)S(1)}, u32[]{:S(2)}, u32[]{:S(2)}) collective-permute-start(bf16[128,1024]{1,0:T(8,128)(2,1)} %get-tuple-element.19), channel_id=1, source_target_pairs={{0,6},{1,7},{2,0},{3,1},{4,2},{5,3},{6,4},{7,5},{8,14},{9,15},{10,... | collective-permute-start | bytes 786440 | tf_op jit(solution)/shard_map/ppermute | solution.py:283
  15.2 5.1 %all-to-all-start = ((bf16[16,128,128]{2,1,0:T(8,128)(2,1)}), bf16[16,128,128]{2,1,0:T(8,128)(2,1)S(1)}, u32[]{:S(2)}, u32[]{:S(2)}) async-start(bf16[16,128,128]{2,1,0:T(8,128)(2,1)} %broadcast_in_dim.19), calls=%async_computation | async-start | bytes 1048576 | tf_op jit(solution)/shard_map/all_to_all | solution.py:32
  20.4 1.5 %collective-permute-start = (bf16[144,128]{1,0:T(8,128)(2,1)S(1)}, bf16[144,128]{1,0:T(8,128)(2,1)S(1)}, u32[]{:S(2)}, u32[]{:S(2)}) collective-permute-start(bf16[144,128]{1,0:T(8,128)(2,1)S(1)} %get-tuple-element.27), channel_id=1, source_target_pairs={{0,1},{1,0},{2,3},{3,2},{4,5},{5,4},{6,7},{7,6},{8,9},{9,8},{10,11... | collective-permute-start | bytes 110600 | tf_op jit(solution)/shard_map/ppermute | solution.py:245
  22.8 3.1 %collective-permute-start.3 = (bf16[2,144,128]{2,1,0:T(8,128)(2,1)S(1)}, bf16[2,144,128]{2,1,0:T(8,128)(2,1)S(1)}, u32[]{:S(2)}, u32[]{:S(2)}) collective-permute-start(bf16[2,144,128]{2,1,0:T(8,128)(2,1)S(1)} %pad_maximum_fusion.refs_0_), channel_id=1, source_target_pairs={{0,6},{1,7},{2,0},{3,1},{4,2},{5,3},{6,4},{7,5},{8,14},{9,15},{10,... | collective-permute-start | bytes 221192 | tf_op jit(solution)/shard_map/ppermute | solution.py:249
  26.8 2.1 %collective-permute-done.3.refs_3_ = bf16[2,144,128]{2,1,0:T(8,128)(2,1)S(1)} collective-permute-done((bf16[2,144,128]{2,1,0:T(8,128)(2,1)S(1)}, bf16[2,144,128]{2,1,0:T(8,128)(2,1)S(1)}, u32[]{:S(2)}, u32[]{:S(2)}) %collective-permute-start.3) | collective-permute-done | bytes 73760 | tf_op jit(solution)/shard_map/ppermute | solution.py:249
  29.5 4.4 %collective-permute-start.9 = (bf16[128,1024]{1,0:T(8,128)(2,1)}, bf16[128,1024]{1,0:T(8,128)(2,1)}, u32[]{:S(2)}, u32[]{:S(2)}) collective-permute-start(bf16[128,1024]{1,0:T(8,128)(2,1)} %get-tuple-element.20), channel_id=1, source_target_pairs={{0,5},{1,6},{2,7},{3,0},{4,1},{5,2},{6,3},{7,4},{8,13},{9,14},{10,... | collective-permute-start | bytes 786440 | tf_op jit(solution)/shard_map/ppermute | solution.py:283
  35.2 2.1 %collective-permute-start.7 = (bf16[128,1024]{1,0:T(8,128)(2,1)}, bf16[128,1024]{1,0:T(8,128)(2,1)}, u32[]{:S(2)}, u32[]{:S(2)}) collective-permute-start(bf16[128,1024]{1,0:T(8,128)(2,1)} %get-tuple-element.22), channel_id=1, source_target_pairs={{0,3},{1,4},{2,5},{3,6},{4,7},{5,0},{6,1},{7,2},{8,11},{9,12},{10,... | collective-permute-start | bytes 786440 | tf_op jit(solution)/shard_map/ppermute | solution.py:283
  41.2 1.6 %copy-done.2 = bf16[1,1024,1024]{2,1,0:T(8,128)(2,1)S(1)} copy-done((bf16[1,1024,1024]{2,1,0:T(8,128)(2,1)S(1)}, bf16[1,1024,1024]{2,1,0:T(8,128)(2,1)}, u32[]{:S(2)}) %copy-start.2) | copy-done | bytes 2097176
  42.8 2.8 %volume.2.prior_ref = f32[1024,128]{1,0:T(8,128)S(1)} custom-call(bf16[1024,1024]{1,0:T(8,128)(2,1)S(1)} %bitcast.50, bf16[1024,1024]{1,0:T(8,128)(2,1)S(1)} %bitcast.52, bf16[1024,128]{1,0:T(8,128)(2,1)S(1)} %get-tuple-element.9.group_ref), custom_call_target="tpu_custom_call" | custom-call | flops 805306368 | bytes 6291456 | tf_op jit(solution)/shard_map/volume/pallas_call | solution.py:200
  45.6 1.3 %applied.1.refs_8_ = f32[1024,128]{1,0:T(8,128)S(1)} custom-call(s32[1]{0:T(128)} %bitcast.col_ref, f32[1024,128]{1,0:T(8,128)S(1)} %volume.2.prior_ref, bf16[1024,2048]{1,0:T(8,128)(2,1)S(1)} %copy-done.1, bf16[2048,128]{1,0:T(8,128)(2,1)S(1)} %bitcast.55), custom_call_target="tpu_custom_call" | custom-call | flops 536870912 | bytes 4194304 | tf_op jit(solution)/shard_map/applied/pallas_call | solution.py:215
  46.8 1.9 %collective-permute-done.9.refs_5_ = bf16[128,1024]{1,0:T(8,128)(2,1)} collective-permute-done((bf16[128,1024]{1,0:T(8,128)(2,1)}, bf16[128,1024]{1,0:T(8,128)(2,1)}, u32[]{:S(2)}, u32[]{:S(2)}) %collective-permute-start.9) | collective-permute-done | bytes 262176 | tf_op jit(solution)/shard_map/ppermute | solution.py:283
  48.8 3.4 %collective-permute-done.7.refs_3_ = bf16[128,1024]{1,0:T(8,128)(2,1)} collective-permute-done((bf16[128,1024]{1,0:T(8,128)(2,1)}, bf16[128,1024]{1,0:T(8,128)(2,1)}, u32[]{:S(2)}, u32[]{:S(2)}) %collective-permute-start.7) | collective-permute-done | bytes 262176 | tf_op jit(solution)/shard_map/ppermute | solution.py:283
  52.6 2.4 %collective-permute-done.5.refs_1_ = bf16[128,1024]{1,0:T(8,128)(2,1)} collective-permute-done((bf16[128,1024]{1,0:T(8,128)(2,1)}, bf16[128,1024]{1,0:T(8,128)(2,1)}, u32[]{:S(2)}, u32[]{:S(2)}) %collective-permute-start.5) | collective-permute-done | bytes 262176 | tf_op jit(solution)/shard_map/ppermute | solution.py:283
  55.0 2.8 %faces.2 = (f32[4,128,128]{2,1,0:T(8,128)S(1)}, bf16[4,128,128]{2,1,0:T(8,128)(2,1)S(1)}) custom-call(s32[1]{0:T(128)} %bitcast.col_ref, f32[8,16,128]{2,1,0:T(8,128)S(1)} %get-tuple-element.8.mix_ref, bf16[1024,128]{1,0:T(8,128)(2,1)S(1)} %get-tuple-element.9.group_ref, bf16[128,1024]{1,0:T(8,128)(2,1)S(1)} %get-tuple-element.25.refs_0_, ...), custom_call_target="tpu_custom_call" | custom-call | flops 536870912 | bytes 4194304 | tf_op jit(solution)/shard_map/faces/pallas_call | solution.py:232
  57.9 3.6 %collective-permute-start.12 = (bf16[4,128,128]{2,1,0:T(8,128)(2,1)S(1)}, bf16[4,128,128]{2,1,0:T(8,128)(2,1)S(1)}, u32[]{:S(2)}, u32[]{:S(2)}) collective-permute-start(bf16[4,128,128]{2,1,0:T(8,128)(2,1)S(1)} %get-tuple-element.11), channel_id=1, source_target_pairs={{0,1},{1,0},{2,3},{3,2},{4,5},{5,4},{6,7},{7,6},{8,9},{9,8},{10,11... | collective-permute-start | bytes 393224 | tf_op jit(solution)/shard_map/ppermute | solution.py:245
  62.6 3.1 %collective-permute-done.13 = bf16[2,128,128]{2,1,0:T(8,128)(2,1)S(1)} collective-permute-done((bf16[2,128,128]{2,1,0:T(8,128)(2,1)S(1)}, bf16[2,128,128]{2,1,0:T(8,128)(2,1)S(1)}, u32[]{:S(2)}, u32[]{:S(2)}) %collective-permute-start.13) | collective-permute-done | bytes 65568 | tf_op jit(solution)/shard_map/ppermute | solution.py:245
  66.1 3.6 %collective-permute-done.14 = bf16[128,128]{1,0:T(8,128)(2,1)S(1)} collective-permute-done((bf16[128,128]{1,0:T(8,128)(2,1)S(1)}, bf16[128,128]{1,0:T(8,128)(2,1)S(1)}, u32[]{:S(2)}, u32[]{:S(2)}) %collective-permute-start.14) | collective-permute-done | bytes 32800 | tf_op jit(solution)/shard_map/ppermute | solution.py:245
  70.4 6.1 %collective-permute-start.19 = (bf16[128,128]{1,0:T(8,128)(2,1)S(1)}, bf16[128,128]{1,0:T(8,128)(2,1)S(1)}, u32[]{:S(2)}, u32[]{:S(2)}) collective-permute-start(bf16[128,128]{1,0:T(8,128)(2,1)S(1)} %get-tuple-element.16), channel_id=1, source_target_pairs={{0,0},{1,8},{2,16},{3,24},{4,32},{5,40},{6,48},{7,56},{8,64},{9,72... | collective-permute-start | bytes 98312 | tf_op jit(solution)/shard_map/ppermute | solution.py:298
  76.5 3.1 %collective-permute-done.19 = bf16[128,128]{1,0:T(8,128)(2,1)S(1)} collective-permute-done((bf16[128,128]{1,0:T(8,128)(2,1)S(1)}, bf16[128,128]{1,0:T(8,128)(2,1)S(1)}, u32[]{:S(2)}, u32[]{:S(2)}) %collective-permute-start.19) | collective-permute-done | bytes 32800 | tf_op jit(solution)/shard_map/ppermute | solution.py:298
  80.5 6.9 %all-to-all-start.1 = ((bf16[16,128,128]{2,1,0:T(8,128)(2,1)}), bf16[16,128,128]{2,1,0:T(8,128)(2,1)S(1)}, u32[]{:S(2)}, u32[]{:S(2)}) async-start(bf16[16,128,128]{2,1,0:T(8,128)(2,1)} %broadcast_in_dim.20), calls=%async_computation.1 | async-start | bytes 1048576 | tf_op jit(solution)/shard_map/all_to_all | solution.py:32
  87.4 4.6 %collective-permute-start.15 = (bf16[128,128]{1,0:T(8,128)(2,1)}, bf16[128,128]{1,0:T(8,128)(2,1)S(1)}, u32[]{:S(2)}, u32[]{:S(2)}) collective-permute-start(bf16[128,128]{1,0:T(8,128)(2,1)} %copy-done.14), channel_id=1, source_target_pairs={{0,1},{1,0},{2,3},{3,2},{4,5},{5,4},{6,7},{7,6},{8,9},{9,8},{10,11... | collective-permute-start | bytes 98312 | tf_op jit(solution)/shard_map/ppermute | solution.py:245
  95.3 1.9 %collective-permute-done.18.refs_3_ = bf16[2,128,128]{2,1,0:T(8,128)(2,1)S(1)} collective-permute-done((bf16[2,128,128]{2,1,0:T(8,128)(2,1)S(1)}, bf16[2,128,128]{2,1,0:T(8,128)(2,1)S(1)}, u32[]{:S(2)}, u32[]{:S(2)}) %collective-permute-start.18) | collective-permute-done | bytes 65568 | tf_op jit(solution)/shard_map/ppermute | solution.py:249
  97.2 1.6 %collective-permute-done.17.refs_2_ = bf16[2,128,128]{2,1,0:T(8,128)(2,1)S(1)} collective-permute-done((bf16[2,128,128]{2,1,0:T(8,128)(2,1)S(1)}, bf16[2,128,128]{2,1,0:T(8,128)(2,1)S(1)}, u32[]{:S(2)}, u32[]{:S(2)}) %collective-permute-start.17) | collective-permute-done | bytes 65568 | tf_op jit(solution)/shard_map/ppermute | solution.py:249
  98.8 1.7 %collective-permute-done.16.refs_1_ = bf16[2,128,128]{2,1,0:T(8,128)(2,1)S(1)} collective-permute-done((bf16[2,128,128]{2,1,0:T(8,128)(2,1)S(1)}, bf16[2,128,128]{2,1,0:T(8,128)(2,1)S(1)}, u32[]{:S(2)}, u32[]{:S(2)}) %collective-permute-start.16) | collective-permute-done | bytes 65568 | tf_op jit(solution)/shard_map/ppermute | solution.py:249
  100.5 2.8 %faces.3.refs_0_ = f32[1024,128]{1,0:T(8,128)S(1)} custom-call(s32[1]{0:T(128)} %bitcast.col_ref, f32[8,16,128]{2,1,0:T(8,128)S(1)} %get-tuple-element.8.mix_ref, bf16[1024,128]{1,0:T(8,128)(2,1)S(1)} %assemble.3.group_ref, bf16[128,1024]{1,0:T(8,128)(2,1)S(1)} %get-tuple-element.25.refs_0_, bf16[128,1024]{1,0:T(8,128)(2,1)} %collective-permute-done.5.refs_1_, ...), custom_call_target="tpu_custom_call" | custom-call | flops 536870912 | bytes 4194304 | tf_op jit(solution)/shard_map/faces/pallas_call | solution.py:232
  103.3 2.8 %volume.3.prior_ref = f32[1024,128]{1,0:T(8,128)S(1)} custom-call(bf16[1024,1024]{1,0:T(8,128)(2,1)S(1)} %bitcast.51, bf16[1024,1024]{1,0:T(8,128)(2,1)S(1)} %bitcast.53, bf16[1024,128]{1,0:T(8,128)(2,1)S(1)} %assemble.3.group_ref, f32[1024,128]{1,0:T(8,128)S(1)} %faces.3.refs_0_), custom_call_target="tpu_custom_call" | custom-call | flops 805306368 | bytes 6291456 | tf_op jit(solution)/shard_map/volume/pallas_call | solution.py:200
  107.8 4.9 %streamed.1 = (f32[4,128,128]{2,1,0:T(8,128)}, bf16[4,128,128]{2,1,0:T(8,128)(2,1)}) custom-call(s32[1]{0:T(128)} %bitcast.col_ref, f32[1024,128]{1,0:T(8,128)} %copy-done.4, bf16[1024,2048]{1,0:T(8,128)(2,1)} %surface_ref.3, bf16[2048,128]{1,0:T(8,128)(2,1)} %bitcast.56), custom_call_target="tpu_custom_call" | custom-call | tf_op jit(solution)/shard_map/streamed/pallas_call | solution.py:140
  116.2 2.9 %collective-permute-done.21 = bf16[2,128,128]{2,1,0:T(8,128)(2,1)S(1)} collective-permute-done((bf16[2,128,128]{2,1,0:T(8,128)(2,1)S(1)}, bf16[2,128,128]{2,1,0:T(8,128)(2,1)S(1)}, u32[]{:S(2)}, u32[]{:S(2)}) %collective-permute-start.21) | collective-permute-done | bytes 65568 | tf_op jit(solution)/shard_map/ppermute | solution.py:245
  119.1 1.5 %collective-permute-start.22 = (bf16[128,128]{1,0:T(8,128)(2,1)S(1)}, bf16[128,128]{1,0:T(8,128)(2,1)S(1)}, u32[]{:S(2)}, u32[]{:S(2)}) collective-permute-start(bf16[128,128]{1,0:T(8,128)(2,1)S(1)} %fusion.11), channel_id=1, source_target_pairs={{0,6},{1,7},{2,4},{3,5},{4,2},{5,3},{6,0},{7,1},{8,14},{9,15},{10,... | collective-permute-start | bytes 98312 | tf_op jit(solution)/shard_map/ppermute | solution.py:245
  120.6 2.5 %collective-permute-done.22 = bf16[128,128]{1,0:T(8,128)(2,1)S(1)} collective-permute-done((bf16[128,128]{1,0:T(8,128)(2,1)S(1)}, bf16[128,128]{1,0:T(8,128)(2,1)S(1)}, u32[]{:S(2)}, u32[]{:S(2)}) %collective-permute-start.22) | collective-permute-done | bytes 32800 | tf_op jit(solution)/shard_map/ppermute | solution.py:245
  (79 shorter events, 22.2 us)
Async XLA Ops:
  1.5 12.8 %collective-permute-start.4 = (bf16[128,128]{1,0:T(8,128)(2,1)S(1)}, bf16[128,128]{1,0:T(8,128)(2,1)S(1)}, u32[]{:S(2)}, u32[]{:S(2)}) collective-permute-start(bf16[128,128]{1,0:T(8,128)(2,1)S(1)} %convert_element_type.49), channel_id=1, source_target_pairs={{0,0},{1,8},{2,16},{3,24},{4,32},{5,40},{6,48},{7,56},{8,64},{9,72... | collective-permute-start | bytes 98312 | tf_op jit(solution)/shard_map/ppermute | solution.py:298
  6.1 8.1 %copy-start.15 = (s32[1,6]{1,0:T(1,128)S(1)}, s32[1,6]{1,0:T(1,128)}, u32[]{:S(2)}) copy-start(s32[1,6]{1,0:T(1,128)} %param.9) | copy-start | bytes 76
  8.9 32.3 %copy-start = (bf16[1,1024,1024]{2,1,0:T(8,128)(2,1)S(1)}, bf16[1,1024,1024]{2,1,0:T(8,128)(2,1)}, u32[]{:S(2)}) copy-start(bf16[1,1024,1024]{2,1,0:T(8,128)(2,1)} %param.8) | copy-start | bytes 6291460
  8.9 28.4 %collective-permute-start.11 = (bf16[128,1024]{1,0:T(8,128)(2,1)}, bf16[128,1024]{1,0:T(8,128)(2,1)S(1)}, u32[]{:S(2)}, u32[]{:S(2)}) collective-permute-start(bf16[128,1024]{1,0:T(8,128)(2,1)} %get-tuple-element.18), channel_id=1, source_target_pairs={{0,7},{1,0},{2,1},{3,2},{4,3},{5,4},{6,5},{7,6},{8,15},{9,8},{10,9... | collective-permute-start | bytes 786440 | tf_op jit(solution)/shard_map/ppermute | solution.py:283
  8.9 29.6 %collective-permute-start.10 = (bf16[128,1024]{1,0:T(8,128)(2,1)}, bf16[128,1024]{1,0:T(8,128)(2,1)S(1)}, u32[]{:S(2)}, u32[]{:S(2)}) collective-permute-start(bf16[128,1024]{1,0:T(8,128)(2,1)} %get-tuple-element.19), channel_id=1, source_target_pairs={{0,6},{1,7},{2,0},{3,1},{4,2},{5,3},{6,4},{7,5},{8,14},{9,15},{10,... | collective-permute-start | bytes 786440 | tf_op jit(solution)/shard_map/ppermute | solution.py:283
  15.2 23.3 %all-to-all-start = ((bf16[16,128,128]{2,1,0:T(8,128)(2,1)}), bf16[16,128,128]{2,1,0:T(8,128)(2,1)S(1)}, u32[]{:S(2)}, u32[]{:S(2)}) async-start(bf16[16,128,128]{2,1,0:T(8,128)(2,1)} %broadcast_in_dim.19), calls=%async_computation | async-start | bytes 1048576 | tf_op jit(solution)/shard_map/all_to_all | solution.py:32
  20.4 2.4 %collective-permute-start = (bf16[144,128]{1,0:T(8,128)(2,1)S(1)}, bf16[144,128]{1,0:T(8,128)(2,1)S(1)}, u32[]{:S(2)}, u32[]{:S(2)}) collective-permute-start(bf16[144,128]{1,0:T(8,128)(2,1)S(1)} %get-tuple-element.27), channel_id=1, source_target_pairs={{0,1},{1,0},{2,3},{3,2},{4,5},{5,4},{6,7},{7,6},{8,9},{9,8},{10,11... | collective-permute-start | bytes 110600 | tf_op jit(solution)/shard_map/ppermute | solution.py:245
  22.8 6.1 %collective-permute-start.3 = (bf16[2,144,128]{2,1,0:T(8,128)(2,1)S(1)}, bf16[2,144,128]{2,1,0:T(8,128)(2,1)S(1)}, u32[]{:S(2)}, u32[]{:S(2)}) collective-permute-start(bf16[2,144,128]{2,1,0:T(8,128)(2,1)S(1)} %pad_maximum_fusion.refs_0_), channel_id=1, source_target_pairs={{0,6},{1,7},{2,0},{3,1},{4,2},{5,3},{6,4},{7,5},{8,14},{9,15},{10,... | collective-permute-start | bytes 221192 | tf_op jit(solution)/shard_map/ppermute | solution.py:249
  25.9 8.0 %collective-permute-start.2 = (bf16[2,144,128]{2,1,0:T(8,128)(2,1)S(1)}, bf16[2,144,128]{2,1,0:T(8,128)(2,1)S(1)}, u32[]{:S(2)}, u32[]{:S(2)}) collective-permute-start(bf16[2,144,128]{2,1,0:T(8,128)(2,1)S(1)} %pad_maximum_fusion.refs_0_), channel_id=1, source_target_pairs={{0,4},{1,5},{2,6},{3,7},{4,0},{5,1},{6,2},{7,3},{8,12},{9,13},{10,... | collective-permute-start | bytes 221192 | tf_op jit(solution)/shard_map/ppermute | solution.py:249
  26.8 7.7 %collective-permute-start.1 = (bf16[2,144,128]{2,1,0:T(8,128)(2,1)S(1)}, bf16[2,144,128]{2,1,0:T(8,128)(2,1)S(1)}, u32[]{:S(2)}, u32[]{:S(2)}) collective-permute-start(bf16[2,144,128]{2,1,0:T(8,128)(2,1)S(1)} %pad_maximum_fusion.refs_0_), channel_id=1, source_target_pairs={{0,2},{1,3},{2,4},{3,5},{4,6},{5,7},{6,0},{7,1},{8,10},{9,11},{10,... | collective-permute-start | bytes 221192 | tf_op jit(solution)/shard_map/ppermute | solution.py:249
  29.5 19.2 %collective-permute-start.9 = (bf16[128,1024]{1,0:T(8,128)(2,1)}, bf16[128,1024]{1,0:T(8,128)(2,1)}, u32[]{:S(2)}, u32[]{:S(2)}) collective-permute-start(bf16[128,1024]{1,0:T(8,128)(2,1)} %get-tuple-element.20), channel_id=1, source_target_pairs={{0,5},{1,6},{2,7},{3,0},{4,1},{5,2},{6,3},{7,4},{8,13},{9,14},{10,... | collective-permute-start | bytes 786440 | tf_op jit(solution)/shard_map/ppermute | solution.py:283
  34.5 14.2 %collective-permute-start.8 = (bf16[128,1024]{1,0:T(8,128)(2,1)}, bf16[128,1024]{1,0:T(8,128)(2,1)}, u32[]{:S(2)}, u32[]{:S(2)}) collective-permute-start(bf16[128,1024]{1,0:T(8,128)(2,1)} %get-tuple-element.21), channel_id=1, source_target_pairs={{0,4},{1,5},{2,6},{3,7},{4,0},{5,1},{6,2},{7,3},{8,12},{9,13},{10,... | collective-permute-start | bytes 786440 | tf_op jit(solution)/shard_map/ppermute | solution.py:283
  35.2 17.0 %collective-permute-start.7 = (bf16[128,1024]{1,0:T(8,128)(2,1)}, bf16[128,1024]{1,0:T(8,128)(2,1)}, u32[]{:S(2)}, u32[]{:S(2)}) collective-permute-start(bf16[128,1024]{1,0:T(8,128)(2,1)} %get-tuple-element.22), channel_id=1, source_target_pairs={{0,3},{1,4},{2,5},{3,6},{4,7},{5,0},{6,1},{7,2},{8,11},{9,12},{10,... | collective-permute-start | bytes 786440 | tf_op jit(solution)/shard_map/ppermute | solution.py:283
  37.3 15.3 %collective-permute-start.6 = (bf16[128,1024]{1,0:T(8,128)(2,1)}, bf16[128,1024]{1,0:T(8,128)(2,1)}, u32[]{:S(2)}, u32[]{:S(2)}) collective-permute-start(bf16[128,1024]{1,0:T(8,128)(2,1)} %get-tuple-element.23), channel_id=1, source_target_pairs={{0,2},{1,3},{2,4},{3,5},{4,6},{5,7},{6,0},{7,1},{8,10},{9,11},{10,... | collective-permute-start | bytes 786440 | tf_op jit(solution)/shard_map/ppermute | solution.py:283
  38.5 16.6 %collective-permute-start.5 = (bf16[128,1024]{1,0:T(8,128)(2,1)}, bf16[128,1024]{1,0:T(8,128)(2,1)}, u32[]{:S(2)}, u32[]{:S(2)}) collective-permute-start(bf16[128,1024]{1,0:T(8,128)(2,1)} %get-tuple-element.24), channel_id=1, source_target_pairs={{0,1},{1,2},{2,3},{3,4},{4,5},{5,6},{6,7},{7,0},{8,9},{9,10},{10,1... | collective-permute-start | bytes 786440 | tf_op jit(solution)/shard_map/ppermute | solution.py:283
  42.8 2.8 %copy-start.1 = (bf16[1024,2048]{1,0:T(8,128)(2,1)S(1)}, bf16[1024,2048]{1,0:T(8,128)(2,1)}, u32[]{:S(2)}) copy-start(bf16[1024,2048]{1,0:T(8,128)(2,1)} %surface_ref.3) | copy-start | bytes 12582916
  46.8 23.0 %copy-start.12 = (f32[128,128]{1,0:T(8,128)S(1)}, f32[128,128]{1,0:T(8,128)}, u32[]{:S(2)}) copy-start(f32[128,128]{1,0:T(8,128)} %param.6) | copy-start | bytes 196612
  57.9 4.6 %collective-permute-start.12 = (bf16[4,128,128]{2,1,0:T(8,128)(2,1)S(1)}, bf16[4,128,128]{2,1,0:T(8,128)(2,1)S(1)}, u32[]{:S(2)}, u32[]{:S(2)}) collective-permute-start(bf16[4,128,128]{2,1,0:T(8,128)(2,1)S(1)} %get-tuple-element.11), channel_id=1, source_target_pairs={{0,1},{1,0},{2,3},{3,2},{4,5},{5,4},{6,7},{7,6},{8,9},{9,8},{10,11... | collective-permute-start | bytes 393224 | tf_op jit(solution)/shard_map/ppermute | solution.py:245
  62.5 3.2 %collective-permute-start.13 = (bf16[2,128,128]{2,1,0:T(8,128)(2,1)S(1)}, bf16[2,128,128]{2,1,0:T(8,128)(2,1)S(1)}, u32[]{:S(2)}, u32[]{:S(2)}) collective-permute-start(bf16[2,128,128]{2,1,0:T(8,128)(2,1)S(1)} %slice.91), channel_id=1, source_target_pairs={{0,2},{1,3},{2,0},{3,1},{4,6},{5,7},{6,4},{7,5},{8,10},{9,11},{10,... | collective-permute-start | bytes 196616 | tf_op jit(solution)/shard_map/ppermute | solution.py:245
  65.7 4.1 %collective-permute-start.14 = (bf16[128,128]{1,0:T(8,128)(2,1)S(1)}, bf16[128,128]{1,0:T(8,128)(2,1)S(1)}, u32[]{:S(2)}, u32[]{:S(2)}) collective-permute-start(bf16[128,128]{1,0:T(8,128)(2,1)S(1)} %fusion.10), channel_id=1, source_target_pairs={{0,6},{1,7},{2,4},{3,5},{4,2},{5,3},{6,0},{7,1},{8,14},{9,15},{10,... | collective-permute-start | bytes 98312 | tf_op jit(solution)/shard_map/ppermute | solution.py:245
  70.4 10.1 %copy-start.14 = (bf16[128,128]{1,0:T(8,128)(2,1)}, bf16[128,128]{1,0:T(8,128)(2,1)S(1)}, u32[]{:S(2)}) copy-start(bf16[128,128]{1,0:T(8,128)(2,1)S(1)} %get-tuple-element.16) | copy-start | bytes 98308
  70.4 9.2 %collective-permute-start.19 = (bf16[128,128]{1,0:T(8,128)(2,1)S(1)}, bf16[128,128]{1,0:T(8,128)(2,1)S(1)}, u32[]{:S(2)}, u32[]{:S(2)}) collective-permute-start(bf16[128,128]{1,0:T(8,128)(2,1)S(1)} %get-tuple-element.16), channel_id=1, source_target_pairs={{0,0},{1,8},{2,16},{3,24},{4,32},{5,40},{6,48},{7,56},{8,64},{9,72... | collective-permute-start | bytes 98312 | tf_op jit(solution)/shard_map/ppermute | solution.py:298
  80.5 26.4 %all-to-all-start.1 = ((bf16[16,128,128]{2,1,0:T(8,128)(2,1)}), bf16[16,128,128]{2,1,0:T(8,128)(2,1)S(1)}, u32[]{:S(2)}, u32[]{:S(2)}) async-start(bf16[16,128,128]{2,1,0:T(8,128)(2,1)} %broadcast_in_dim.20), calls=%async_computation.1 | async-start | bytes 1048576 | tf_op jit(solution)/shard_map/all_to_all | solution.py:32
  87.4 15.9 %copy-start.3 = (bf16[1,1024,1024]{2,1,0:T(8,128)(2,1)S(1)}, bf16[1,1024,1024]{2,1,0:T(8,128)(2,1)}, u32[]{:S(2)}) copy-start(bf16[1,1024,1024]{2,1,0:T(8,128)(2,1)} %param.7) | copy-start | bytes 6291460
  87.4 5.6 %collective-permute-start.15 = (bf16[128,128]{1,0:T(8,128)(2,1)}, bf16[128,128]{1,0:T(8,128)(2,1)S(1)}, u32[]{:S(2)}, u32[]{:S(2)}) collective-permute-start(bf16[128,128]{1,0:T(8,128)(2,1)} %copy-done.14), channel_id=1, source_target_pairs={{0,1},{1,0},{2,3},{3,2},{4,5},{5,4},{6,7},{7,6},{8,9},{9,8},{10,11... | collective-permute-start | bytes 98312 | tf_op jit(solution)/shard_map/ppermute | solution.py:245
  93.8 3.4 %collective-permute-start.18 = (bf16[2,128,128]{2,1,0:T(8,128)(2,1)S(1)}, bf16[2,128,128]{2,1,0:T(8,128)(2,1)S(1)}, u32[]{:S(2)}, u32[]{:S(2)}) collective-permute-start(bf16[2,128,128]{2,1,0:T(8,128)(2,1)S(1)} %pad_maximum_fusion.1.refs_0_), channel_id=1, source_target_pairs={{0,6},{1,7},{2,0},{3,1},{4,2},{5,3},{6,4},{7,5},{8,14},{9,15},{10,... | collective-permute-start | bytes 196616 | tf_op jit(solution)/shard_map/ppermute | solution.py:249
  93.8 5.0 %collective-permute-start.17 = (bf16[2,128,128]{2,1,0:T(8,128)(2,1)S(1)}, bf16[2,128,128]{2,1,0:T(8,128)(2,1)S(1)}, u32[]{:S(2)}, u32[]{:S(2)}) collective-permute-start(bf16[2,128,128]{2,1,0:T(8,128)(2,1)S(1)} %pad_maximum_fusion.1.refs_0_), channel_id=1, source_target_pairs={{0,4},{1,5},{2,6},{3,7},{4,0},{5,1},{6,2},{7,3},{8,12},{9,13},{10,... | collective-permute-start | bytes 196616 | tf_op jit(solution)/shard_map/ppermute | solution.py:249
  94.9 5.6 %collective-permute-start.16 = (bf16[2,128,128]{2,1,0:T(8,128)(2,1)S(1)}, bf16[2,128,128]{2,1,0:T(8,128)(2,1)S(1)}, u32[]{:S(2)}, u32[]{:S(2)}) collective-permute-start(bf16[2,128,128]{2,1,0:T(8,128)(2,1)S(1)} %pad_maximum_fusion.1.refs_0_), channel_id=1, source_target_pairs={{0,2},{1,3},{2,4},{3,5},{4,6},{5,7},{6,0},{7,1},{8,10},{9,11},{10,... | collective-permute-start | bytes 196616 | tf_op jit(solution)/shard_map/ppermute | solution.py:249
  107.8 15.4 %copy-start.13 = (f32[128,128]{1,0:T(8,128)S(1)}, f32[128,128]{1,0:T(8,128)}, u32[]{:S(2)}) copy-start(f32[128,128]{1,0:T(8,128)} %get-tuple-element.17) | copy-start | bytes 196612
  112.7 2.2 %collective-permute-start.20 = (bf16[4,128,128]{2,1,0:T(8,128)(2,1)}, bf16[4,128,128]{2,1,0:T(8,128)(2,1)S(1)}, u32[]{:S(2)}, u32[]{:S(2)}) collective-permute-start(bf16[4,128,128]{2,1,0:T(8,128)(2,1)} %get-tuple-element.13), channel_id=1, source_target_pairs={{0,1},{1,0},{2,3},{3,2},{4,5},{5,4},{6,7},{7,6},{8,9},{9,8},{10,11... | collective-permute-start | bytes 393224 | tf_op jit(solution)/shard_map/ppermute | solution.py:245
  115.9 3.2 %collective-permute-start.21 = (bf16[2,128,128]{2,1,0:T(8,128)(2,1)S(1)}, bf16[2,128,128]{2,1,0:T(8,128)(2,1)S(1)}, u32[]{:S(2)}, u32[]{:S(2)}) collective-permute-start(bf16[2,128,128]{2,1,0:T(8,128)(2,1)S(1)} %slice.90), channel_id=1, source_target_pairs={{0,2},{1,3},{2,0},{3,1},{4,6},{5,7},{6,4},{7,5},{8,10},{9,11},{10,... | collective-permute-start | bytes 196616 | tf_op jit(solution)/shard_map/ppermute | solution.py:245
  119.1 4.1 %collective-permute-start.22 = (bf16[128,128]{1,0:T(8,128)(2,1)S(1)}, bf16[128,128]{1,0:T(8,128)(2,1)S(1)}, u32[]{:S(2)}, u32[]{:S(2)}) collective-permute-start(bf16[128,128]{1,0:T(8,128)(2,1)S(1)} %fusion.11), channel_id=1, source_target_pairs={{0,6},{1,7},{2,4},{3,5},{4,2},{5,3},{6,0},{7,1},{8,14},{9,15},{10,... | collective-permute-start | bytes 98312 | tf_op jit(solution)/shard_map/ppermute | solution.py:245
  (9 other events, 7.8 us)

commit v8 on v6

--- a/solution.py
+++ b/solution.py
@@ -30,10 +30,6 @@
 
 def exchange(blocks, axis):
     return lax.all_to_all(blocks, axis, split_axis=0, concat_axis=0, tiled=True)
-
-
-def copy_for_each(shard, axis):
-    return exchange(jnp.broadcast_to(shard, (lax.axis_size(axis), *shard.shape)), axis)
 
 
 def turned(rows, cols):
@@ -100,8 +96,8 @@
     peers, n, ne = blocks_ref.shape
     blocks_ref[...] = total.reshape(peers, n, ne)
     for d in range(peers // 2):
-        keep_ref[d] = blocks_ref[rotated(col, 2 * d, peers)]
-        give_ref[d] = blocks_ref[rotated(col, 2 * d, peers) ^ 1].astype(BF)
+        keep_ref[d] = blocks_ref[col ^ (2 * d)]
+        give_ref[d] = blocks_ref[col ^ (2 * d + 1)].astype(BF)
 
 
 def surface_kernel(col_ref, prior_ref, surface_ref, column_ref, *refs):
@@ -120,6 +116,28 @@
     ]
 
 
+def repeated_kernel(piece_ref, out_ref, sems):
+    copies = [
+        pltpu.make_async_copy(piece_ref, out_ref.at[i], sems.at[i]) for i in range(out_ref.shape[0])
+    ]
+    for copy in copies:
+        copy.start()
+    for copy in copies:
+        copy.wait()
+
+
+def repeated(piece, count):
+    return pl.pallas_call(
+        repeated_kernel,
+        out_shape=jax.ShapeDtypeStruct((count, *piece.shape), piece.dtype),
+        in_specs=[vmem()],
+        out_specs=pl.BlockSpec(memory_space=pl.ANY),
+        scratch_shapes=[pltpu.SemaphoreType.DMA((count,))],
+        compiler_params=PARAMS,
+        name="repeated",
+    )(piece)
+
+
 def vmem():
     return pl.BlockSpec(memory_space=pltpu.VMEM)
 
@@ -196,8 +214,8 @@
     )(place, mix, group, *slices, *prior)
 
 
-def swapped(shard, cols):
-    return lax.ppermute(shard, "col", [(i, i ^ 1) for i in range(cols)])
+def swapped(shard, cols, bits=1):
+    return lax.ppermute(shard, "col", [(i, i ^ bits) for i in range(cols)])
 
 
 def along(shard, d, cols):
@@ -207,10 +225,9 @@
 def summed_over(keep, give, cols):
     taken = swapped(give, cols)
     sums = keep + taken.astype(F32)
-    total = sums[0]
-    for d in range(1, cols // 2):
-        total = total + along(sums[d].astype(BF), d, cols).astype(F32)
-    return total
+    taken = swapped(sums[1:3].astype(BF), cols, 2).astype(F32)
+    last = swapped((sums[3] + taken[1]).astype(BF), cols, 6).astype(F32)
+    return sums[0] + taken[0] + last
 
 
 def gathered(shard, cols):
@@ -252,7 +269,7 @@
     for sweep in range(ITERS):
         rounded = current.astype(BF)
         piece = lax.ppermute(rounded, ("row", "col"), turned(rows, cols))
-        column_block = copy_for_each(piece, "row").reshape(rows * n, ne)
+        column_block = exchange(repeated(piece, rows), "row").reshape(rows * n, ne)
         sent = jnp.concatenate([rounded, extra], axis=0) if sweep == 0 else rounded
         pairs = gathered(sent, cols)
         group, *rows_got = assemble(place, pairs, n)

time: 120 us -> 121 us (level)
  waiting for transfers between devices: 30.8 us -> 34.4 us
  starting transfers between devices: 57.2 us -> 54.7 us
  Pallas kernels: 13.8 us -> 15.7 us
  local copies, waits for them, and re-layouts: 12 us -> 10.2 us
    ppermute x4 -> x8, waiting for transfers between devices: 3.91 us -> 16.1 us  [swapped(): return lax.ppermute(shard, 'col', [(i, i ^ bits) for i in range(cols)])]
    ppermute x12 -> x6, waiting for transfers between devices: 15.9 us -> 7.3 us  [along(): lax.ppermute(shard, 'col', [(i, (i + 2 * d) % cols) for i in range(cols)])]
    ppermute x12 -> x6, starting transfers between devices: 11 us -> 5.51 us  [along(): lax.ppermute(shard, 'col', [(i, (i + 2 * d) % cols) for i in range(cols)])]
    ppermute x4 -> x8, starting transfers between devices: 10.5 us -> 13.5 us  [swapped(): return lax.ppermute(shard, 'col', [(i, i ^ bits) for i in range(cols)])]
    pallas_call x0 -> x2, Pallas kernels: none -> 1.88 us  [repeated(): pl.pallas_call(repeated_kernel, out_shape=jax.ShapeDtypeStruct((count, *p...]
    broadcast_in_dim x2 -> x0, local copies, waits for them, and re-layouts: 1.78 us -> none  [copy_for_each(): jnp.broadcast_to(shard, (lax.axis_size(axis), *shard.shape))]
  transfers between devices with their start and end apart: 27 -> 25, of which waited for: 17 -> 17; matrix products, arithmetic and copies ran while one was open for 4% -> 3% of each run, Pallas kernels for 8% -> 9%
where the time goes in v8:
time: 121 us; the launch traced here: 119 us
  starting transfers between devices  54.7 us (45%)
  waiting for transfers between devices  34.4 us (28%)
  Pallas kernels  15.7 us (13%)
  local copies, waits for them, and re-layouts  10.2 us (8%)
  other arithmetic  3.15 us (3%)
    ppermute x8, waiting for transfers between devices, swapped(): return lax.ppermute(shard, 'col', [(i, i ^ bits) for i in range(cols)])  16.1 us
    ppermute x8, starting transfers between devices, swapped(): return lax.ppermute(shard, 'col', [(i, i ^ bits) for i in range(cols)])  13.5 us
    ppermute x7, starting transfers between devices, steps(): lax.ppermute(block, 'col', [(i, (i + k) % cols) for i in range(cols)])  13 us
    all_to_all x2, starting transfers between devices, exchange(): return lax.all_to_all(blocks, axis, split_axis=0, concat_axis=0, tiled=True)  12.1 us
    ppermute x2, starting transfers between devices, steps(): piece = lax.ppermute(rounded, ('row', 'col'), turned(rows, cols))  10.7 us
    ppermute x7, waiting for transfers between devices, steps(): lax.ppermute(block, 'col', [(i, (i + k) % cols) for i in range(cols)])  7.92 us
    unnamed x34, local copies, waits for them, and re-layouts  7.4 us
    ppermute x6, waiting for transfers between devices, along(): lax.ppermute(shard, 'col', [(i, (i + 2 * d) % cols) for i in range(cols)])  7.3 us
  transfers between devices with their start and end apart: 25, of which 17 were waited for; matrix products, arithmetic and copies ran while one was open for 3% of the time, Pallas kernels for 9%

profile of v8, /device:TPU:1, one launch (start us, length us, event | category | flops | bytes accessed | tf_op | source)
XLA Modules:
  0.0 119.1 jit_solution(17657749801534167657)
XLA Ops:
  1.5 4.6 %collective-permute-start.11 = (bf16[128,128]{1,0:T(8,128)(2,1)S(1)}, bf16[128,128]{1,0:T(8,128)(2,1)S(1)}, u32[]{:S(2)}, u32[]{:S(2)}) collective-permute-start(bf16[128,128]{1,0:T(8,128)(2,1)S(1)} %convert_element_type.49), channel_id=1, source_target_pairs={{0,0},{1,8},{2,16},{3,24},{4,32},{5,40},{6,48},{7,56},{8,64},{9,72... | collective-permute-start | bytes 98312 | tf_op jit(solution)/shard_map/ppermute | solution.py:271
  6.1 2.8 %dynamic-slice_bitcast_fusion = (bf16[128,1024]{1,0:T(8,128)(2,1)}, bf16[128,1024]{1,0:T(8,128)(2,1)}, bf16[128,1024]{1,0:T(8,128)(2,1)}, bf16[128,1024]{1,0:T(8...) fusion(bf16[1,1024,1024]{2,1,0:T(8,128)(2,1)} %param.8, ...), kind=kLoop, calls=%fused_computation.2 | loop fusion | bytes 4194336 | tf_op jit(solution)/shard_map/dynamic_slice | solution.py:254
  8.9 5.3 %collective-permute-start.9 = (bf16[128,1024]{1,0:T(8,128)(2,1)}, bf16[128,1024]{1,0:T(8,128)(2,1)S(1)}, u32[]{:S(2)}, u32[]{:S(2)}) collective-permute-start(bf16[128,1024]{1,0:T(8,128)(2,1)} %get-tuple-element.19), channel_id=1, source_target_pairs={{0,6},{1,7},{2,0},{3,1},{4,2},{5,3},{6,4},{7,5},{8,14},{9,15},{10,... | collective-permute-start | bytes 786440 | tf_op jit(solution)/shard_map/ppermute | solution.py:256
  15.2 5.2 %all-to-all-start = ((bf16[16,128,128]{2,1,0:T(8,128)(2,1)}), bf16[16,128,128]{2,1,0:T(8,128)(2,1)S(1)}, u32[]{:S(2)}, u32[]{:S(2)}) async-start(bf16[16,128,128]{2,1,0:T(8,128)(2,1)} %repeated.2), calls=%async_computation | async-start | bytes 1048576 | tf_op jit(solution)/shard_map/all_to_all | solution.py:32
  20.4 1.5 %collective-permute-start = (bf16[144,128]{1,0:T(8,128)(2,1)S(1)}, bf16[144,128]{1,0:T(8,128)(2,1)S(1)}, u32[]{:S(2)}, u32[]{:S(2)}) collective-permute-start(bf16[144,128]{1,0:T(8,128)(2,1)S(1)} %get-tuple-element.27), channel_id=1, source_target_pairs={{0,1},{1,0},{2,3},{3,2},{4,5},{5,4},{6,7},{7,6},{8,9},{9,8},{10,11... | collective-permute-start | bytes 110600 | tf_op jit(solution)/shard_map/ppermute | solution.py:218
  22.8 3.1 %collective-permute-start.3 = (bf16[2,144,128]{2,1,0:T(8,128)(2,1)S(1)}, bf16[2,144,128]{2,1,0:T(8,128)(2,1)S(1)}, u32[]{:S(2)}, u32[]{:S(2)}) collective-permute-start(bf16[2,144,128]{2,1,0:T(8,128)(2,1)S(1)} %pad_maximum_fusion.refs_0_), channel_id=1, source_target_pairs={{0,6},{1,7},{2,0},{3,1},{4,2},{5,3},{6,4},{7,5},{8,14},{9,15},{10,... | collective-permute-start | bytes 221192 | tf_op jit(solution)/shard_map/ppermute | solution.py:222
  26.9 2.1 %collective-permute-done.3.refs_3_ = bf16[2,144,128]{2,1,0:T(8,128)(2,1)S(1)} collective-permute-done((bf16[2,144,128]{2,1,0:T(8,128)(2,1)S(1)}, bf16[2,144,128]{2,1,0:T(8,128)(2,1)S(1)}, u32[]{:S(2)}, u32[]{:S(2)}) %collective-permute-start.3) | collective-permute-done | bytes 73760 | tf_op jit(solution)/shard_map/ppermute | solution.py:222
  28.9 4.4 %collective-permute-start.8 = (bf16[128,1024]{1,0:T(8,128)(2,1)}, bf16[128,1024]{1,0:T(8,128)(2,1)}, u32[]{:S(2)}, u32[]{:S(2)}) collective-permute-start(bf16[128,1024]{1,0:T(8,128)(2,1)} %get-tuple-element.20), channel_id=1, source_target_pairs={{0,5},{1,6},{2,7},{3,0},{4,1},{5,2},{6,3},{7,4},{8,13},{9,14},{10,... | collective-permute-start | bytes 786440 | tf_op jit(solution)/shard_map/ppermute | solution.py:256
  33.3 2.7 %collective-permute-start.6 = (bf16[128,1024]{1,0:T(8,128)(2,1)}, bf16[128,1024]{1,0:T(8,128)(2,1)}, u32[]{:S(2)}, u32[]{:S(2)}) collective-permute-start(bf16[128,1024]{1,0:T(8,128)(2,1)} %get-tuple-element.22), channel_id=1, source_target_pairs={{0,3},{1,4},{2,5},{3,6},{4,7},{5,0},{6,1},{7,2},{8,11},{9,12},{10,... | collective-permute-start | bytes 786440 | tf_op jit(solution)/shard_map/ppermute | solution.py:256
  37.4 1.6 %copy-done.3 = bf16[1,1024,1024]{2,1,0:T(8,128)(2,1)S(1)} copy-done((bf16[1,1024,1024]{2,1,0:T(8,128)(2,1)S(1)}, bf16[1,1024,1024]{2,1,0:T(8,128)(2,1)}, u32[]{:S(2)}) %copy-start.3) | copy-done | bytes 2097176
  39.0 2.8 %volume.2.prior_ref = f32[1024,128]{1,0:T(8,128)S(1)} custom-call(bf16[1024,1024]{1,0:T(8,128)(2,1)S(1)} %bitcast.50, bf16[1024,1024]{1,0:T(8,128)(2,1)S(1)} %bitcast.52, bf16[1024,128]{1,0:T(8,128)(2,1)S(1)} %get-tuple-element.9.group_ref), custom_call_target="tpu_custom_call" | custom-call | flops 805306368 | bytes 6291456 | tf_op jit(solution)/shard_map/volume/pallas_call | solution.py:173
  42.4 2.2 %copy-done.1 = bf16[1024,2048]{1,0:T(8,128)(2,1)S(1)} copy-done((bf16[1024,2048]{1,0:T(8,128)(2,1)S(1)}, bf16[1024,2048]{1,0:T(8,128)(2,1)}, u32[]{:S(2)}) %copy-start.1) | copy-done | bytes 4194328
  45.9 2.2 %collective-permute-done.8.refs_5_ = bf16[128,1024]{1,0:T(8,128)(2,1)} collective-permute-done((bf16[128,1024]{1,0:T(8,128)(2,1)}, bf16[128,1024]{1,0:T(8,128)(2,1)}, u32[]{:S(2)}, u32[]{:S(2)}) %collective-permute-start.8) | collective-permute-done | bytes 262176 | tf_op jit(solution)/shard_map/ppermute | solution.py:256
  48.2 3.3 %collective-permute-done.6.refs_3_ = bf16[128,1024]{1,0:T(8,128)(2,1)} collective-permute-done((bf16[128,1024]{1,0:T(8,128)(2,1)}, bf16[128,1024]{1,0:T(8,128)(2,1)}, u32[]{:S(2)}, u32[]{:S(2)}) %collective-permute-start.6) | collective-permute-done | bytes 262176 | tf_op jit(solution)/shard_map/ppermute | solution.py:256
  52.0 1.9 %collective-permute-done.4.refs_1_ = bf16[128,1024]{1,0:T(8,128)(2,1)} collective-permute-done((bf16[128,1024]{1,0:T(8,128)(2,1)}, bf16[128,1024]{1,0:T(8,128)(2,1)}, u32[]{:S(2)}, u32[]{:S(2)}) %collective-permute-start.4) | collective-permute-done | bytes 262176 | tf_op jit(solution)/shard_map/ppermute | solution.py:256
  53.8 2.8 %faces.2 = (f32[4,128,128]{2,1,0:T(8,128)S(1)}, bf16[4,128,128]{2,1,0:T(8,128)(2,1)S(1)}) custom-call(s32[1]{0:T(128)} %bitcast.col_ref, f32[8,16,128]{2,1,0:T(8,128)S(1)} %get-tuple-element.8.mix_ref, bf16[1024,128]{1,0:T(8,128)(2,1)S(1)} %copy-done.12, bf16[128,1024]{1,0:T(8,128)(2,1)S(1)} %get-tuple-element.25.refs_0_, ...), custom_call_target="tpu_custom_call" | custom-call | flops 536870912 | bytes 4194304 | tf_op jit(solution)/shard_map/faces/pallas_call | solution.py:205
  56.7 4.1 %collective-permute-start.12 = (bf16[4,128,128]{2,1,0:T(8,128)(2,1)S(1)}, bf16[4,128,128]{2,1,0:T(8,128)(2,1)S(1)}, u32[]{:S(2)}, u32[]{:S(2)}) collective-permute-start(bf16[4,128,128]{2,1,0:T(8,128)(2,1)S(1)} %get-tuple-element.11), channel_id=1, source_target_pairs={{0,1},{1,0},{2,3},{3,2},{4,5},{5,4},{6,7},{7,6},{8,9},{9,8},{10,11... | collective-permute-start | bytes 393224 | tf_op jit(solution)/shard_map/ppermute | solution.py:218
  62.0 3.1 %collective-permute-done.13 = bf16[2,128,128]{2,1,0:T(8,128)(2,1)S(1)} collective-permute-done((bf16[2,128,128]{2,1,0:T(8,128)(2,1)S(1)}, bf16[2,128,128]{2,1,0:T(8,128)(2,1)S(1)}, u32[]{:S(2)}, u32[]{:S(2)}) %collective-permute-start.13) | collective-permute-done | bytes 65568 | tf_op jit(solution)/shard_map/ppermute | solution.py:218
  65.5 3.6 %collective-permute-done.14 = bf16[128,128]{1,0:T(8,128)(2,1)S(1)} collective-permute-done((bf16[128,128]{1,0:T(8,128)(2,1)S(1)}, bf16[128,128]{1,0:T(8,128)(2,1)S(1)}, u32[]{:S(2)}, u32[]{:S(2)}) %collective-permute-start.14) | collective-permute-done | bytes 32800 | tf_op jit(solution)/shard_map/ppermute | solution.py:218
  69.8 6.1 %collective-permute-start.19 = (bf16[128,128]{1,0:T(8,128)(2,1)S(1)}, bf16[128,128]{1,0:T(8,128)(2,1)S(1)}, u32[]{:S(2)}, u32[]{:S(2)}) collective-permute-start(bf16[128,128]{1,0:T(8,128)(2,1)S(1)} %get-tuple-element.16), channel_id=1, source_target_pairs={{0,0},{1,8},{2,16},{3,24},{4,32},{5,40},{6,48},{7,56},{8,64},{9,72... | collective-permute-start | bytes 98312 | tf_op jit(solution)/shard_map/ppermute | solution.py:271
  75.9 3.1 %collective-permute-done.19.piece_ref = bf16[128,128]{1,0:T(8,128)(2,1)S(1)} collective-permute-done((bf16[128,128]{1,0:T(8,128)(2,1)S(1)}, bf16[128,128]{1,0:T(8,128)(2,1)S(1)}, u32[]{:S(2)}, u32[]{:S(2)}) %collective-permute-start.19) | collective-permute-done | bytes 32800 | tf_op jit(solution)/shard_map/ppermute | solution.py:271
  80.0 6.9 %all-to-all-start.1 = ((bf16[16,128,128]{2,1,0:T(8,128)(2,1)}), bf16[16,128,128]{2,1,0:T(8,128)(2,1)S(1)}, u32[]{:S(2)}, u32[]{:S(2)}) async-start(bf16[16,128,128]{2,1,0:T(8,128)(2,1)} %repeated.3), calls=%async_computation.1 | async-start | bytes 1048576 | tf_op jit(solution)/shard_map/all_to_all | solution.py:32
  86.9 4.6 %collective-permute-start.15 = (bf16[128,128]{1,0:T(8,128)(2,1)}, bf16[128,128]{1,0:T(8,128)(2,1)S(1)}, u32[]{:S(2)}, u32[]{:S(2)}) collective-permute-start(bf16[128,128]{1,0:T(8,128)(2,1)} %copy-done.15), channel_id=1, source_target_pairs={{0,1},{1,0},{2,3},{3,2},{4,5},{5,4},{6,7},{7,6},{8,9},{9,8},{10,11... | collective-permute-start | bytes 98312 | tf_op jit(solution)/shard_map/ppermute | solution.py:218
  94.8 1.9 %collective-permute-done.18.refs_3_ = bf16[2,128,128]{2,1,0:T(8,128)(2,1)S(1)} collective-permute-done((bf16[2,128,128]{2,1,0:T(8,128)(2,1)S(1)}, bf16[2,128,128]{2,1,0:T(8,128)(2,1)S(1)}, u32[]{:S(2)}, u32[]{:S(2)}) %collective-permute-start.18) | collective-permute-done | bytes 65568 | tf_op jit(solution)/shard_map/ppermute | solution.py:222
  96.7 1.6 %collective-permute-done.17.refs_2_ = bf16[2,128,128]{2,1,0:T(8,128)(2,1)S(1)} collective-permute-done((bf16[2,128,128]{2,1,0:T(8,128)(2,1)S(1)}, bf16[2,128,128]{2,1,0:T(8,128)(2,1)S(1)}, u32[]{:S(2)}, u32[]{:S(2)}) %collective-permute-start.17) | collective-permute-done | bytes 65568 | tf_op jit(solution)/shard_map/ppermute | solution.py:222
  98.3 1.7 %collective-permute-done.16.refs_1_ = bf16[2,128,128]{2,1,0:T(8,128)(2,1)S(1)} collective-permute-done((bf16[2,128,128]{2,1,0:T(8,128)(2,1)S(1)}, bf16[2,128,128]{2,1,0:T(8,128)(2,1)S(1)}, u32[]{:S(2)}, u32[]{:S(2)}) %collective-permute-start.16) | collective-permute-done | bytes 65568 | tf_op jit(solution)/shard_map/ppermute | solution.py:222
  100.0 2.8 %faces.3.refs_0_ = f32[1024,128]{1,0:T(8,128)S(1)} custom-call(s32[1]{0:T(128)} %bitcast.col_ref, f32[8,16,128]{2,1,0:T(8,128)S(1)} %get-tuple-element.8.mix_ref, bf16[1024,128]{1,0:T(8,128)(2,1)S(1)} %assemble.3.group_ref, bf16[128,1024]{1,0:T(8,128)(2,1)S(1)} %get-tuple-element.25.refs_0_, bf16[128,1024]{1,0:T(8,128)(2,1)} %collective-permute-done.4.refs_1_, ...), custom_call_target="tpu_custom_call" | custom-call | flops 536870912 | bytes 4194304 | tf_op jit(solution)/shard_map/faces/pallas_call | solution.py:205
  102.8 2.8 %volume.3.prior_ref = f32[1024,128]{1,0:T(8,128)S(1)} custom-call(bf16[1024,1024]{1,0:T(8,128)(2,1)S(1)} %bitcast.51, bf16[1024,1024]{1,0:T(8,128)(2,1)S(1)} %bitcast.53, bf16[1024,128]{1,0:T(8,128)(2,1)S(1)} %assemble.3.group_ref, f32[1024,128]{1,0:T(8,128)S(1)} %faces.3.refs_0_), custom_call_target="tpu_custom_call" | custom-call | flops 805306368 | bytes 6291456 | tf_op jit(solution)/shard_map/volume/pallas_call | solution.py:173
  105.6 2.2 %copy-done.2 = bf16[1024,2048]{1,0:T(8,128)(2,1)S(1)} copy-done((bf16[1024,2048]{1,0:T(8,128)(2,1)S(1)}, bf16[1024,2048]{1,0:T(8,128)(2,1)}, u32[]{:S(2)}) %copy-start.2) | copy-done | bytes 4194328
  111.5 2.9 %collective-permute-done.21 = bf16[2,128,128]{2,1,0:T(8,128)(2,1)S(1)} collective-permute-done((bf16[2,128,128]{2,1,0:T(8,128)(2,1)S(1)}, bf16[2,128,128]{2,1,0:T(8,128)(2,1)S(1)}, u32[]{:S(2)}, u32[]{:S(2)}) %collective-permute-start.21) | collective-permute-done | bytes 65568 | tf_op jit(solution)/shard_map/ppermute | solution.py:218
  114.4 1.5 %collective-permute-start.22 = (bf16[128,128]{1,0:T(8,128)(2,1)S(1)}, bf16[128,128]{1,0:T(8,128)(2,1)S(1)}, u32[]{:S(2)}, u32[]{:S(2)}) collective-permute-start(bf16[128,128]{1,0:T(8,128)(2,1)S(1)} %fusion.11), channel_id=1, source_target_pairs={{0,6},{1,7},{2,4},{3,5},{4,2},{5,3},{6,0},{7,1},{8,14},{9,15},{10,... | collective-permute-start | bytes 98312 | tf_op jit(solution)/shard_map/ppermute | solution.py:218
  115.9 2.6 %collective-permute-done.22 = bf16[128,128]{1,0:T(8,128)(2,1)S(1)} collective-permute-done((bf16[128,128]{1,0:T(8,128)(2,1)S(1)}, bf16[128,128]{1,0:T(8,128)(2,1)S(1)}, u32[]{:S(2)}, u32[]{:S(2)}) %collective-permute-start.22) | collective-permute-done | bytes 32800 | tf_op jit(solution)/shard_map/ppermute | solution.py:218
  (81 shorter events, 18.3 us)
Async XLA Ops:
  1.5 12.8 %collective-permute-start.11 = (bf16[128,128]{1,0:T(8,128)(2,1)S(1)}, bf16[128,128]{1,0:T(8,128)(2,1)S(1)}, u32[]{:S(2)}, u32[]{:S(2)}) collective-permute-start(bf16[128,128]{1,0:T(8,128)(2,1)S(1)} %convert_element_type.49), channel_id=1, source_target_pairs={{0,0},{1,8},{2,16},{3,24},{4,32},{5,40},{6,48},{7,56},{8,64},{9,72... | collective-permute-start | bytes 98312 | tf_op jit(solution)/shard_map/ppermute | solution.py:271
  8.9 28.5 %copy-start = (bf16[1,1024,1024]{2,1,0:T(8,128)(2,1)S(1)}, bf16[1,1024,1024]{2,1,0:T(8,128)(2,1)}, u32[]{:S(2)}) copy-start(bf16[1,1024,1024]{2,1,0:T(8,128)(2,1)} %param.8) | copy-start | bytes 6291460
  8.9 27.2 %collective-permute-start.10 = (bf16[128,1024]{1,0:T(8,128)(2,1)}, bf16[128,1024]{1,0:T(8,128)(2,1)S(1)}, u32[]{:S(2)}, u32[]{:S(2)}) collective-permute-start(bf16[128,1024]{1,0:T(8,128)(2,1)} %get-tuple-element.18), channel_id=1, source_target_pairs={{0,7},{1,0},{2,1},{3,2},{4,3},{5,4},{6,5},{7,6},{8,15},{9,8},{10,9... | collective-permute-start | bytes 786440 | tf_op jit(solution)/shard_map/ppermute | solution.py:256
  8.9 27.8 %collective-permute-start.9 = (bf16[128,1024]{1,0:T(8,128)(2,1)}, bf16[128,1024]{1,0:T(8,128)(2,1)S(1)}, u32[]{:S(2)}, u32[]{:S(2)}) collective-permute-start(bf16[128,1024]{1,0:T(8,128)(2,1)} %get-tuple-element.19), channel_id=1, source_target_pairs={{0,6},{1,7},{2,0},{3,1},{4,2},{5,3},{6,4},{7,5},{8,14},{9,15},{10,... | collective-permute-start | bytes 786440 | tf_op jit(solution)/shard_map/ppermute | solution.py:256
  15.2 27.2 %all-to-all-start = ((bf16[16,128,128]{2,1,0:T(8,128)(2,1)}), bf16[16,128,128]{2,1,0:T(8,128)(2,1)S(1)}, u32[]{:S(2)}, u32[]{:S(2)}) async-start(bf16[16,128,128]{2,1,0:T(8,128)(2,1)} %repeated.2), calls=%async_computation | async-start | bytes 1048576 | tf_op jit(solution)/shard_map/all_to_all | solution.py:32
  20.4 2.4 %collective-permute-start = (bf16[144,128]{1,0:T(8,128)(2,1)S(1)}, bf16[144,128]{1,0:T(8,128)(2,1)S(1)}, u32[]{:S(2)}, u32[]{:S(2)}) collective-permute-start(bf16[144,128]{1,0:T(8,128)(2,1)S(1)} %get-tuple-element.27), channel_id=1, source_target_pairs={{0,1},{1,0},{2,3},{3,2},{4,5},{5,4},{6,7},{7,6},{8,9},{9,8},{10,11... | collective-permute-start | bytes 110600 | tf_op jit(solution)/shard_map/ppermute | solution.py:218
  22.8 6.1 %collective-permute-start.3 = (bf16[2,144,128]{2,1,0:T(8,128)(2,1)S(1)}, bf16[2,144,128]{2,1,0:T(8,128)(2,1)S(1)}, u32[]{:S(2)}, u32[]{:S(2)}) collective-permute-start(bf16[2,144,128]{2,1,0:T(8,128)(2,1)S(1)} %pad_maximum_fusion.refs_0_), channel_id=1, source_target_pairs={{0,6},{1,7},{2,0},{3,1},{4,2},{5,3},{6,4},{7,5},{8,14},{9,15},{10,... | collective-permute-start | bytes 221192 | tf_op jit(solution)/shard_map/ppermute | solution.py:222
  25.9 7.4 %collective-permute-start.2 = (bf16[2,144,128]{2,1,0:T(8,128)(2,1)S(1)}, bf16[2,144,128]{2,1,0:T(8,128)(2,1)S(1)}, u32[]{:S(2)}, u32[]{:S(2)}) collective-permute-start(bf16[2,144,128]{2,1,0:T(8,128)(2,1)S(1)} %pad_maximum_fusion.refs_0_), channel_id=1, source_target_pairs={{0,4},{1,5},{2,6},{3,7},{4,0},{5,1},{6,2},{7,3},{8,12},{9,13},{10,... | collective-permute-start | bytes 221192 | tf_op jit(solution)/shard_map/ppermute | solution.py:222
  26.8 6.5 %collective-permute-start.1 = (bf16[2,144,128]{2,1,0:T(8,128)(2,1)S(1)}, bf16[2,144,128]{2,1,0:T(8,128)(2,1)S(1)}, u32[]{:S(2)}, u32[]{:S(2)}) collective-permute-start(bf16[2,144,128]{2,1,0:T(8,128)(2,1)S(1)} %pad_maximum_fusion.refs_0_), channel_id=1, source_target_pairs={{0,2},{1,3},{2,4},{3,5},{4,6},{5,7},{6,0},{7,1},{8,10},{9,11},{10,... | collective-permute-start | bytes 221192 | tf_op jit(solution)/shard_map/ppermute | solution.py:222
  28.9 19.2 %collective-permute-start.8 = (bf16[128,1024]{1,0:T(8,128)(2,1)}, bf16[128,1024]{1,0:T(8,128)(2,1)}, u32[]{:S(2)}, u32[]{:S(2)}) collective-permute-start(bf16[128,1024]{1,0:T(8,128)(2,1)} %get-tuple-element.20), channel_id=1, source_target_pairs={{0,5},{1,6},{2,7},{3,0},{4,1},{5,2},{6,3},{7,4},{8,13},{9,14},{10,... | collective-permute-start | bytes 786440 | tf_op jit(solution)/shard_map/ppermute | solution.py:256
  33.3 14.9 %collective-permute-start.7 = (bf16[128,1024]{1,0:T(8,128)(2,1)}, bf16[128,1024]{1,0:T(8,128)(2,1)}, u32[]{:S(2)}, u32[]{:S(2)}) collective-permute-start(bf16[128,1024]{1,0:T(8,128)(2,1)} %get-tuple-element.21), channel_id=1, source_target_pairs={{0,4},{1,5},{2,6},{3,7},{4,0},{5,1},{6,2},{7,3},{8,12},{9,13},{10,... | collective-permute-start | bytes 786440 | tf_op jit(solution)/shard_map/ppermute | solution.py:256
  33.3 18.2 %collective-permute-start.6 = (bf16[128,1024]{1,0:T(8,128)(2,1)}, bf16[128,1024]{1,0:T(8,128)(2,1)}, u32[]{:S(2)}, u32[]{:S(2)}) collective-permute-start(bf16[128,1024]{1,0:T(8,128)(2,1)} %get-tuple-element.22), channel_id=1, source_target_pairs={{0,3},{1,4},{2,5},{3,6},{4,7},{5,0},{6,1},{7,2},{8,11},{9,12},{10,... | collective-permute-start | bytes 786440 | tf_op jit(solution)/shard_map/ppermute | solution.py:256
  36.1 15.9 %collective-permute-start.5 = (bf16[128,1024]{1,0:T(8,128)(2,1)}, bf16[128,1024]{1,0:T(8,128)(2,1)}, u32[]{:S(2)}, u32[]{:S(2)}) collective-permute-start(bf16[128,1024]{1,0:T(8,128)(2,1)} %get-tuple-element.23), channel_id=1, source_target_pairs={{0,2},{1,3},{2,4},{3,5},{4,6},{5,7},{6,0},{7,1},{8,10},{9,11},{10,... | collective-permute-start | bytes 786440 | tf_op jit(solution)/shard_map/ppermute | solution.py:256
  37.3 16.5 %collective-permute-start.4 = (bf16[128,1024]{1,0:T(8,128)(2,1)}, bf16[128,1024]{1,0:T(8,128)(2,1)}, u32[]{:S(2)}, u32[]{:S(2)}) collective-permute-start(bf16[128,1024]{1,0:T(8,128)(2,1)} %get-tuple-element.24), channel_id=1, source_target_pairs={{0,1},{1,2},{2,3},{3,4},{4,5},{5,6},{6,7},{7,0},{8,9},{9,10},{10,1... | collective-permute-start | bytes 786440 | tf_op jit(solution)/shard_map/ppermute | solution.py:256
  45.9 23.3 %copy-start.13 = (f32[128,128]{1,0:T(8,128)S(1)}, f32[128,128]{1,0:T(8,128)}, u32[]{:S(2)}) copy-start(f32[128,128]{1,0:T(8,128)} %param.6) | copy-start | bytes 196612
  56.7 43.3 %copy-start.7 = (bf16[128,1024]{1,0:T(8,128)(2,1)S(1)}, bf16[128,1024]{1,0:T(8,128)(2,1)}, u32[]{:S(2)}) copy-start(bf16[128,1024]{1,0:T(8,128)(2,1)} %copy-done.5) | copy-start | bytes 786436
  56.7 43.3 %copy-start.10 = (bf16[128,1024]{1,0:T(8,128)(2,1)S(1)}, bf16[128,1024]{1,0:T(8,128)(2,1)}, u32[]{:S(2)}) copy-start(bf16[128,1024]{1,0:T(8,128)(2,1)} %copy-done.8) | copy-start | bytes 786436
  56.7 5.1 %collective-permute-start.12 = (bf16[4,128,128]{2,1,0:T(8,128)(2,1)S(1)}, bf16[4,128,128]{2,1,0:T(8,128)(2,1)S(1)}, u32[]{:S(2)}, u32[]{:S(2)}) collective-permute-start(bf16[4,128,128]{2,1,0:T(8,128)(2,1)S(1)} %get-tuple-element.11), channel_id=1, source_target_pairs={{0,1},{1,0},{2,3},{3,2},{4,5},{5,4},{6,7},{7,6},{8,9},{9,8},{10,11... | collective-permute-start | bytes 393224 | tf_op jit(solution)/shard_map/ppermute | solution.py:218
  61.9 3.2 %collective-permute-start.13 = (bf16[2,128,128]{2,1,0:T(8,128)(2,1)S(1)}, bf16[2,128,128]{2,1,0:T(8,128)(2,1)S(1)}, u32[]{:S(2)}, u32[]{:S(2)}) collective-permute-start(bf16[2,128,128]{2,1,0:T(8,128)(2,1)S(1)} %slice.91), channel_id=1, source_target_pairs={{0,2},{1,3},{2,0},{3,1},{4,6},{5,7},{6,4},{7,5},{8,10},{9,11},{10,... | collective-permute-start | bytes 196616 | tf_op jit(solution)/shard_map/ppermute | solution.py:218
  65.1 4.1 %collective-permute-start.14 = (bf16[128,128]{1,0:T(8,128)(2,1)S(1)}, bf16[128,128]{1,0:T(8,128)(2,1)S(1)}, u32[]{:S(2)}, u32[]{:S(2)}) collective-permute-start(bf16[128,128]{1,0:T(8,128)(2,1)S(1)} %fusion.10), channel_id=1, source_target_pairs={{0,6},{1,7},{2,4},{3,5},{4,2},{5,3},{6,0},{7,1},{8,14},{9,15},{10,... | collective-permute-start | bytes 98312 | tf_op jit(solution)/shard_map/ppermute | solution.py:218
  69.8 10.1 %copy-start.15 = (bf16[128,128]{1,0:T(8,128)(2,1)}, bf16[128,128]{1,0:T(8,128)(2,1)S(1)}, u32[]{:S(2)}) copy-start(bf16[128,128]{1,0:T(8,128)(2,1)S(1)} %get-tuple-element.16) | copy-start | bytes 98308
  69.8 9.2 %collective-permute-start.19 = (bf16[128,128]{1,0:T(8,128)(2,1)S(1)}, bf16[128,128]{1,0:T(8,128)(2,1)S(1)}, u32[]{:S(2)}, u32[]{:S(2)}) collective-permute-start(bf16[128,128]{1,0:T(8,128)(2,1)S(1)} %get-tuple-element.16), channel_id=1, source_target_pairs={{0,0},{1,8},{2,16},{3,24},{4,32},{5,40},{6,48},{7,56},{8,64},{9,72... | collective-permute-start | bytes 98312 | tf_op jit(solution)/shard_map/ppermute | solution.py:271
  80.0 25.6 %all-to-all-start.1 = ((bf16[16,128,128]{2,1,0:T(8,128)(2,1)}), bf16[16,128,128]{2,1,0:T(8,128)(2,1)S(1)}, u32[]{:S(2)}, u32[]{:S(2)}) async-start(bf16[16,128,128]{2,1,0:T(8,128)(2,1)} %repeated.3), calls=%async_computation.1 | async-start | bytes 1048576 | tf_op jit(solution)/shard_map/all_to_all | solution.py:32
  86.9 15.9 %copy-start.4 = (bf16[1,1024,1024]{2,1,0:T(8,128)(2,1)S(1)}, bf16[1,1024,1024]{2,1,0:T(8,128)(2,1)}, u32[]{:S(2)}) copy-start(bf16[1,1024,1024]{2,1,0:T(8,128)(2,1)} %param.7) | copy-start | bytes 6291460
  86.9 5.6 %collective-permute-start.15 = (bf16[128,128]{1,0:T(8,128)(2,1)}, bf16[128,128]{1,0:T(8,128)(2,1)S(1)}, u32[]{:S(2)}, u32[]{:S(2)}) collective-permute-start(bf16[128,128]{1,0:T(8,128)(2,1)} %copy-done.15), channel_id=1, source_target_pairs={{0,1},{1,0},{2,3},{3,2},{4,5},{5,4},{6,7},{7,6},{8,9},{9,8},{10,11... | collective-permute-start | bytes 98312 | tf_op jit(solution)/shard_map/ppermute | solution.py:218
  93.3 3.4 %collective-permute-start.18 = (bf16[2,128,128]{2,1,0:T(8,128)(2,1)S(1)}, bf16[2,128,128]{2,1,0:T(8,128)(2,1)S(1)}, u32[]{:S(2)}, u32[]{:S(2)}) collective-permute-start(bf16[2,128,128]{2,1,0:T(8,128)(2,1)S(1)} %pad_maximum_fusion.1.refs_0_), channel_id=1, source_target_pairs={{0,6},{1,7},{2,0},{3,1},{4,2},{5,3},{6,4},{7,5},{8,14},{9,15},{10,... | collective-permute-start | bytes 196616 | tf_op jit(solution)/shard_map/ppermute | solution.py:222
  93.3 5.0 %collective-permute-start.17 = (bf16[2,128,128]{2,1,0:T(8,128)(2,1)S(1)}, bf16[2,128,128]{2,1,0:T(8,128)(2,1)S(1)}, u32[]{:S(2)}, u32[]{:S(2)}) collective-permute-start(bf16[2,128,128]{2,1,0:T(8,128)(2,1)S(1)} %pad_maximum_fusion.1.refs_0_), channel_id=1, source_target_pairs={{0,4},{1,5},{2,6},{3,7},{4,0},{5,1},{6,2},{7,3},{8,12},{9,13},{10,... | collective-permute-start | bytes 196616 | tf_op jit(solution)/shard_map/ppermute | solution.py:222
  94.3 5.6 %collective-permute-start.16 = (bf16[2,128,128]{2,1,0:T(8,128)(2,1)S(1)}, bf16[2,128,128]{2,1,0:T(8,128)(2,1)S(1)}, u32[]{:S(2)}, u32[]{:S(2)}) collective-permute-start(bf16[2,128,128]{2,1,0:T(8,128)(2,1)S(1)} %pad_maximum_fusion.1.refs_0_), channel_id=1, source_target_pairs={{0,2},{1,3},{2,4},{3,5},{4,6},{5,7},{6,0},{7,1},{8,10},{9,11},{10,... | collective-permute-start | bytes 196616 | tf_op jit(solution)/shard_map/ppermute | solution.py:222
  107.8 10.6 %copy-start.14 = (f32[128,128]{1,0:T(8,128)S(1)}, f32[128,128]{1,0:T(8,128)}, u32[]{:S(2)}) copy-start(f32[128,128]{1,0:T(8,128)} %get-tuple-element.17) | copy-start | bytes 196612
  109.1 2.0 %collective-permute-start.20 = (bf16[4,128,128]{2,1,0:T(8,128)(2,1)S(1)}, bf16[4,128,128]{2,1,0:T(8,128)(2,1)S(1)}, u32[]{:S(2)}, u32[]{:S(2)}) collective-permute-start(bf16[4,128,128]{2,1,0:T(8,128)(2,1)S(1)} %get-tuple-element.13), channel_id=1, source_target_pairs={{0,1},{1,0},{2,3},{3,2},{4,5},{5,4},{6,7},{7,6},{8,9},{9,8},{10,11... | collective-permute-start | bytes 393224 | tf_op jit(solution)/shard_map/ppermute | solution.py:218
  111.2 3.2 %collective-permute-start.21 = (bf16[2,128,128]{2,1,0:T(8,128)(2,1)S(1)}, bf16[2,128,128]{2,1,0:T(8,128)(2,1)S(1)}, u32[]{:S(2)}, u32[]{:S(2)}) collective-permute-start(bf16[2,128,128]{2,1,0:T(8,128)(2,1)S(1)} %slice.90), channel_id=1, source_target_pairs={{0,2},{1,3},{2,0},{3,1},{4,6},{5,7},{6,4},{7,5},{8,10},{9,11},{10,... | collective-permute-start | bytes 196616 | tf_op jit(solution)/shard_map/ppermute | solution.py:218
  114.4 4.1 %collective-permute-start.22 = (bf16[128,128]{1,0:T(8,128)(2,1)S(1)}, bf16[128,128]{1,0:T(8,128)(2,1)S(1)}, u32[]{:S(2)}, u32[]{:S(2)}) collective-permute-start(bf16[128,128]{1,0:T(8,128)(2,1)S(1)} %fusion.11), channel_id=1, source_target_pairs={{0,6},{1,7},{2,4},{3,5},{4,2},{5,3},{6,0},{7,1},{8,14},{9,15},{10,... | collective-permute-start | bytes 98312 | tf_op jit(solution)/shard_map/ppermute | solution.py:218
  (10 other events, 44.4 us)

commit v9 on v6

--- a/solution.py
+++ b/solution.py
@@ -163,6 +163,38 @@
     )(interp, dtn, group, *prior)
 
 
+def traces_kernel(interp_ref, group_ref, out_ref):
+    out_ref[...] = dot(interp_ref[...], group_ref[...]).astype(BF)
+
+
+def response_kernel(interp_ref, dtn_ref, traces_ref, out_ref):
+    response = dot(dtn_ref[...], traces_ref[...]).astype(BF)
+    out_ref[...] = dot_t(interp_ref[...], response)
+
+
+def volume_in_two(interp, dtn, group):
+    m, rb = interp.shape
+    ne = group.shape[-1]
+    traces = pl.pallas_call(
+        traces_kernel,
+        out_shape=jax.ShapeDtypeStruct((m, ne), BF),
+        in_specs=[vmem()] * 2,
+        out_specs=vmem(),
+        compiler_params=PARAMS,
+        cost_estimate=cost(1, m, rb, ne),
+        name="traces",
+    )(interp, group)
+    return pl.pallas_call(
+        response_kernel,
+        out_shape=jax.ShapeDtypeStruct((rb, ne), F32),
+        in_specs=[vmem()] * 3,
+        out_specs=vmem(),
+        compiler_params=PARAMS,
+        cost_estimate=cost(2, m, rb, ne),
+        name="response",
+    )(interp, dtn, traces)
+
+
 def applied(place, prior, surface, column_block, peers=0):
     (m, k), ne = surface.shape, prior.shape[1]
     plain = [jax.ShapeDtypeStruct(prior.shape, F32)]
@@ -258,7 +290,7 @@
         group, *rows_got = assemble(place, pairs, n)
         if sweep == 0:
             mix = rows_got[0]
-            own = volume(interp, dtn, group)
+            own = volume_in_two(interp, dtn, group)
             wide = applied(place, own, surface, column_block)[0]
             keep, give = faces(place, mix, group, slices, wide)
         else:

time: 120 us -> 120 us (level)
  local copies, waits for them, and re-layouts: 12 us -> 9.04 us
  waiting for transfers between devices: 30.8 us -> 33.6 us
    unnamed x34, local copies, waits for them, and re-layouts: 7.43 us -> 4.44 us
    pallas_call x0 -> x2, Pallas kernels: none -> 2.92 us  [the longest x1 2.21 us: volume_in_two(): pl.pallas_call(response_kernel, out_shape=jax.ShapeDtypeStruct((rb, ne),...]
    ppermute x7, waiting for transfers between devices: 7.88 us -> 10.7 us  [steps(): lax.ppermute(block, 'col', [(i, (i + k) % cols) for i in range(cols)])]
    pallas_call x2 -> x1, Pallas kernels: 5.56 us -> 2.79 us  [volume(): pl.pallas_call(volume_kernel, out_shape=jax.ShapeDtypeStruct((rb, ne), F3...]
where the time goes in v9:
time: 120 us; the launch traced here: 118 us
  starting transfers between devices  57.2 us (48%)
  waiting for transfers between devices  33.6 us (28%)
  Pallas kernels  14 us (12%)
  local copies, waits for them, and re-layouts  9.04 us (8%)
  other arithmetic  3.15 us (3%)
    ppermute x12, waiting for transfers between devices, along(): lax.ppermute(shard, 'col', [(i, (i + 2 * d) % cols) for i in range(cols)])  15.9 us
    ppermute x7, starting transfers between devices, steps(): lax.ppermute(block, 'col', [(i, (i + k) % cols) for i in range(cols)])  13 us
    all_to_all x2, starting transfers between devices, exchange(): return lax.all_to_all(blocks, axis, split_axis=0, concat_axis=0, tiled=True)  12.6 us
    ppermute x12, starting transfers between devices, along(): lax.ppermute(shard, 'col', [(i, (i + 2 * d) % cols) for i in range(cols)])  11 us
    ppermute x7, waiting for transfers between devices, steps(): lax.ppermute(block, 'col', [(i, (i + k) % cols) for i in range(cols)])  10.7 us
    ppermute x4, starting transfers between devices, swapped(): return lax.ppermute(shard, 'col', [(i, i ^ 1) for i in range(cols)])  10.5 us
    ppermute x2, starting transfers between devices, steps(): piece = lax.ppermute(rounded, ('row', 'col'), turned(rows, cols))  10.1 us
    pallas_call x2, Pallas kernels, faces(): pl.pallas_call(functools.partial(faces_kernel, len(prior)), out_shape=sha...  5.64 us
  transfers between devices with their start and end apart: 27, of which 17 were waited for; matrix products, arithmetic and copies ran while one was open for 4% of the time, Pallas kernels for 8%

profile of v9, /device:TPU:1, one launch (start us, length us, event | category | flops | bytes accessed | tf_op | source)
XLA Modules:
  0.0 117.9 jit_solution(615697340570409377)
XLA Ops:
  1.5 4.6 %collective-permute-start.11 = (bf16[128,128]{1,0:T(8,128)(2,1)S(1)}, bf16[128,128]{1,0:T(8,128)(2,1)S(1)}, u32[]{:S(2)}, u32[]{:S(2)}) collective-permute-start(bf16[128,128]{1,0:T(8,128)(2,1)S(1)} %convert_element_type.65), channel_id=1, source_target_pairs={{0,0},{1,8},{2,16},{3,24},{4,32},{5,40},{6,48},{7,56},{8,64},{9,72... | collective-permute-start | bytes 98312 | tf_op jit(solution)/shard_map/ppermute | solution.py:286
  6.1 2.8 %dynamic-slice_bitcast_fusion = (bf16[128,1024]{1,0:T(8,128)(2,1)}, bf16[128,1024]{1,0:T(8,128)(2,1)}, bf16[128,1024]{1,0:T(8,128)(2,1)}, bf16[128,1024]{1,0:T(8...) fusion(bf16[1,1024,1024]{2,1,0:T(8,128)(2,1)} %param.8, ...), kind=kLoop, calls=%fused_computation.2 | loop fusion | bytes 4194336 | tf_op jit(solution)/shard_map/dynamic_slice | solution.py:269
  8.9 5.3 %collective-permute-start.9 = (bf16[128,1024]{1,0:T(8,128)(2,1)}, bf16[128,1024]{1,0:T(8,128)(2,1)S(1)}, u32[]{:S(2)}, u32[]{:S(2)}) collective-permute-start(bf16[128,1024]{1,0:T(8,128)(2,1)} %get-tuple-element.23), channel_id=1, source_target_pairs={{0,6},{1,7},{2,0},{3,1},{4,2},{5,3},{6,4},{7,5},{8,14},{9,15},{10,... | collective-permute-start | bytes 786440 | tf_op jit(solution)/shard_map/ppermute | solution.py:271
  15.2 5.1 %all-to-all-start = ((bf16[16,128,128]{2,1,0:T(8,128)(2,1)}), bf16[16,128,128]{2,1,0:T(8,128)(2,1)S(1)}, u32[]{:S(2)}, u32[]{:S(2)}) async-start(bf16[16,128,128]{2,1,0:T(8,128)(2,1)} %broadcast_in_dim.19), calls=%async_computation | async-start | bytes 1048576 | tf_op jit(solution)/shard_map/all_to_all | solution.py:32
  20.4 1.5 %collective-permute-start = (bf16[144,128]{1,0:T(8,128)(2,1)S(1)}, bf16[144,128]{1,0:T(8,128)(2,1)S(1)}, u32[]{:S(2)}, u32[]{:S(2)}) collective-permute-start(bf16[144,128]{1,0:T(8,128)(2,1)S(1)} %get-tuple-element.37), channel_id=1, source_target_pairs={{0,1},{1,0},{2,3},{3,2},{4,5},{5,4},{6,7},{7,6},{8,9},{9,8},{10,11... | collective-permute-start | bytes 110600 | tf_op jit(solution)/shard_map/ppermute | solution.py:232
  22.7 3.1 %collective-permute-start.3 = (bf16[2,144,128]{2,1,0:T(8,128)(2,1)S(1)}, bf16[2,144,128]{2,1,0:T(8,128)(2,1)S(1)}, u32[]{:S(2)}, u32[]{:S(2)}) collective-permute-start(bf16[2,144,128]{2,1,0:T(8,128)(2,1)S(1)} %pad_maximum_fusion.refs_0_), channel_id=1, source_target_pairs={{0,6},{1,7},{2,0},{3,1},{4,2},{5,3},{6,4},{7,5},{8,14},{9,15},{10,... | collective-permute-start | bytes 221192 | tf_op jit(solution)/shard_map/ppermute | solution.py:236
  26.8 2.1 %collective-permute-done.3.refs_3_ = bf16[2,144,128]{2,1,0:T(8,128)(2,1)S(1)} collective-permute-done((bf16[2,144,128]{2,1,0:T(8,128)(2,1)S(1)}, bf16[2,144,128]{2,1,0:T(8,128)(2,1)S(1)}, u32[]{:S(2)}, u32[]{:S(2)}) %collective-permute-start.3) | collective-permute-done | bytes 73760 | tf_op jit(solution)/shard_map/ppermute | solution.py:236
  28.9 4.4 %collective-permute-start.8 = (bf16[128,1024]{1,0:T(8,128)(2,1)}, bf16[128,1024]{1,0:T(8,128)(2,1)}, u32[]{:S(2)}, u32[]{:S(2)}) collective-permute-start(bf16[128,1024]{1,0:T(8,128)(2,1)} %get-tuple-element.24), channel_id=1, source_target_pairs={{0,5},{1,6},{2,7},{3,0},{4,1},{5,2},{6,3},{7,4},{8,13},{9,14},{10,... | collective-permute-start | bytes 786440 | tf_op jit(solution)/shard_map/ppermute | solution.py:271
  33.3 2.7 %collective-permute-start.6 = (bf16[128,1024]{1,0:T(8,128)(2,1)}, bf16[128,1024]{1,0:T(8,128)(2,1)}, u32[]{:S(2)}, u32[]{:S(2)}) collective-permute-start(bf16[128,1024]{1,0:T(8,128)(2,1)} %get-tuple-element.26), channel_id=1, source_target_pairs={{0,3},{1,4},{2,5},{3,6},{4,7},{5,0},{6,1},{7,2},{8,11},{9,12},{10,... | collective-permute-start | bytes 786440 | tf_op jit(solution)/shard_map/ppermute | solution.py:271
  37.4 2.2 %response.1.prior_ref = f32[1024,128]{1,0:T(8,128)S(1)} custom-call(bf16[1024,1024]{1,0:T(8,128)(2,1)S(1)} %bitcast.67, bf16[1024,1024]{1,0:T(8,128)(2,1)S(1)} %bitcast.69, bf16[1024,128]{1,0:T(8,128)(2,1)S(1)} %traces.1.traces_ref), custom_call_target="tpu_custom_call" | custom-call | flops 536870912 | bytes 4194304 | tf_op jit(solution)/shard_map/response/pallas_call | solution.py:187
  39.6 2.2 %copy-done.1 = bf16[1024,2048]{1,0:T(8,128)(2,1)S(1)} copy-done((bf16[1024,2048]{1,0:T(8,128)(2,1)S(1)}, bf16[1024,2048]{1,0:T(8,128)(2,1)}, u32[]{:S(2)}) %copy-start.1) | copy-done | bytes 4194328
  43.1 5.0 %collective-permute-done.8.refs_5_ = bf16[128,1024]{1,0:T(8,128)(2,1)} collective-permute-done((bf16[128,1024]{1,0:T(8,128)(2,1)}, bf16[128,1024]{1,0:T(8,128)(2,1)}, u32[]{:S(2)}, u32[]{:S(2)}) %collective-permute-start.8) | collective-permute-done | bytes 262176 | tf_op jit(solution)/shard_map/ppermute | solution.py:271
  48.1 3.3 %collective-permute-done.6.refs_3_ = bf16[128,1024]{1,0:T(8,128)(2,1)} collective-permute-done((bf16[128,1024]{1,0:T(8,128)(2,1)}, bf16[128,1024]{1,0:T(8,128)(2,1)}, u32[]{:S(2)}, u32[]{:S(2)}) %collective-permute-start.6) | collective-permute-done | bytes 262176 | tf_op jit(solution)/shard_map/ppermute | solution.py:271
  51.9 1.9 %collective-permute-done.4.refs_1_ = bf16[128,1024]{1,0:T(8,128)(2,1)} collective-permute-done((bf16[128,1024]{1,0:T(8,128)(2,1)}, bf16[128,1024]{1,0:T(8,128)(2,1)}, u32[]{:S(2)}, u32[]{:S(2)}) %collective-permute-start.4) | collective-permute-done | bytes 262176 | tf_op jit(solution)/shard_map/ppermute | solution.py:271
  53.8 2.8 %faces.2 = (f32[4,128,128]{2,1,0:T(8,128)S(1)}, bf16[4,128,128]{2,1,0:T(8,128)(2,1)S(1)}) custom-call(s32[1]{0:T(128)} %bitcast.col_ref, f32[8,16,128]{2,1,0:T(8,128)S(1)} %get-tuple-element.8.mix_ref, bf16[1024,128]{1,0:T(8,128)(2,1)S(1)} %copy-done.12, bf16[128,1024]{1,0:T(8,128)(2,1)S(1)} %get-tuple-element.29.refs_0_, ...), custom_call_target="tpu_custom_call" | custom-call | flops 536870912 | bytes 4194304 | tf_op jit(solution)/shard_map/faces/pallas_call | solution.py:219
  56.7 4.1 %collective-permute-start.12 = (bf16[4,128,128]{2,1,0:T(8,128)(2,1)S(1)}, bf16[4,128,128]{2,1,0:T(8,128)(2,1)S(1)}, u32[]{:S(2)}, u32[]{:S(2)}) collective-permute-start(bf16[4,128,128]{2,1,0:T(8,128)(2,1)S(1)} %get-tuple-element.11), channel_id=1, source_target_pairs={{0,1},{1,0},{2,3},{3,2},{4,5},{5,4},{6,7},{7,6},{8,9},{9,8},{10,11... | collective-permute-start | bytes 393224 | tf_op jit(solution)/shard_map/ppermute | solution.py:232
  61.9 2.7 %collective-permute-start.15 = (bf16[128,128]{1,0:T(8,128)(2,1)S(1)}, bf16[128,128]{1,0:T(8,128)(2,1)S(1)}, u32[]{:S(2)}, u32[]{:S(2)}) collective-permute-start(bf16[128,128]{1,0:T(8,128)(2,1)S(1)} %get-tuple-element.34), channel_id=1, source_target_pairs={{0,6},{1,7},{2,0},{3,1},{4,2},{5,3},{6,4},{7,5},{8,14},{9,15},{10,... | collective-permute-start | bytes 98312 | tf_op jit(solution)/shard_map/ppermute | solution.py:236
  64.6 1.3 %collective-permute-done.13 = bf16[128,128]{1,0:T(8,128)(2,1)S(1)} collective-permute-done((bf16[128,128]{1,0:T(8,128)(2,1)S(1)}, bf16[128,128]{1,0:T(8,128)(2,1)S(1)}, u32[]{:S(2)}, u32[]{:S(2)}) %collective-permute-start.13) | collective-permute-done | bytes 32800 | tf_op jit(solution)/shard_map/ppermute | solution.py:236
  65.9 3.0 %collective-permute-done.14 = bf16[128,128]{1,0:T(8,128)(2,1)S(1)} collective-permute-done((bf16[128,128]{1,0:T(8,128)(2,1)S(1)}, bf16[128,128]{1,0:T(8,128)(2,1)S(1)}, u32[]{:S(2)}, u32[]{:S(2)}) %collective-permute-start.14) | collective-permute-done | bytes 32800 | tf_op jit(solution)/shard_map/ppermute | solution.py:236
  69.5 5.5 %collective-permute-start.20 = (bf16[128,128]{1,0:T(8,128)(2,1)S(1)}, bf16[128,128]{1,0:T(8,128)(2,1)S(1)}, u32[]{:S(2)}, u32[]{:S(2)}) collective-permute-start(bf16[128,128]{1,0:T(8,128)(2,1)S(1)} %get-tuple-element.18), channel_id=1, source_target_pairs={{0,0},{1,8},{2,16},{3,24},{4,32},{5,40},{6,48},{7,56},{8,64},{9,72... | collective-permute-start | bytes 98312 | tf_op jit(solution)/shard_map/ppermute | solution.py:286
  75.0 3.1 %collective-permute-done.20 = bf16[128,128]{1,0:T(8,128)(2,1)S(1)} collective-permute-done((bf16[128,128]{1,0:T(8,128)(2,1)S(1)}, bf16[128,128]{1,0:T(8,128)(2,1)S(1)}, u32[]{:S(2)}, u32[]{:S(2)}) %collective-permute-start.20) | collective-permute-done | bytes 32800 | tf_op jit(solution)/shard_map/ppermute | solution.py:286
  79.0 7.5 %all-to-all-start.1 = ((bf16[16,128,128]{2,1,0:T(8,128)(2,1)}), bf16[16,128,128]{2,1,0:T(8,128)(2,1)S(1)}, u32[]{:S(2)}, u32[]{:S(2)}) async-start(bf16[16,128,128]{2,1,0:T(8,128)(2,1)} %broadcast_in_dim.20), calls=%async_computation.1 | async-start | bytes 1048576 | tf_op jit(solution)/shard_map/all_to_all | solution.py:32
  86.5 4.0 %collective-permute-start.16 = (bf16[128,128]{1,0:T(8,128)(2,1)}, bf16[128,128]{1,0:T(8,128)(2,1)S(1)}, u32[]{:S(2)}, u32[]{:S(2)}) collective-permute-start(bf16[128,128]{1,0:T(8,128)(2,1)} %copy-done.15), channel_id=1, source_target_pairs={{0,1},{1,0},{2,3},{3,2},{4,5},{5,4},{6,7},{7,6},{8,9},{9,8},{10,11... | collective-permute-start | bytes 98312 | tf_op jit(solution)/shard_map/ppermute | solution.py:232
  93.8 1.9 %collective-permute-done.19.refs_3_ = bf16[2,128,128]{2,1,0:T(8,128)(2,1)S(1)} collective-permute-done((bf16[2,128,128]{2,1,0:T(8,128)(2,1)S(1)}, bf16[2,128,128]{2,1,0:T(8,128)(2,1)S(1)}, u32[]{:S(2)}, u32[]{:S(2)}) %collective-permute-start.19) | collective-permute-done | bytes 65568 | tf_op jit(solution)/shard_map/ppermute | solution.py:236
  95.7 1.6 %collective-permute-done.18.refs_2_ = bf16[2,128,128]{2,1,0:T(8,128)(2,1)S(1)} collective-permute-done((bf16[2,128,128]{2,1,0:T(8,128)(2,1)S(1)}, bf16[2,128,128]{2,1,0:T(8,128)(2,1)S(1)}, u32[]{:S(2)}, u32[]{:S(2)}) %collective-permute-start.18) | collective-permute-done | bytes 65568 | tf_op jit(solution)/shard_map/ppermute | solution.py:236
  97.3 1.8 %collective-permute-done.17.refs_1_ = bf16[2,128,128]{2,1,0:T(8,128)(2,1)S(1)} collective-permute-done((bf16[2,128,128]{2,1,0:T(8,128)(2,1)S(1)}, bf16[2,128,128]{2,1,0:T(8,128)(2,1)S(1)}, u32[]{:S(2)}, u32[]{:S(2)}) %collective-permute-start.17) | collective-permute-done | bytes 65568 | tf_op jit(solution)/shard_map/ppermute | solution.py:236
  99.1 2.8 %faces.3.refs_0_ = f32[1024,128]{1,0:T(8,128)S(1)} custom-call(s32[1]{0:T(128)} %bitcast.col_ref, f32[8,16,128]{2,1,0:T(8,128)S(1)} %get-tuple-element.8.mix_ref, bf16[1024,128]{1,0:T(8,128)(2,1)S(1)} %assemble.3.group_ref, bf16[128,1024]{1,0:T(8,128)(2,1)S(1)} %get-tuple-element.29.refs_0_, bf16[128,1024]{1,0:T(8,128)(2,1)} %collective-permute-done.4.refs_1_, ...), custom_call_target="tpu_custom_call" | custom-call | flops 536870912 | bytes 4194304 | tf_op jit(solution)/shard_map/faces/pallas_call | solution.py:219
  102.0 2.8 %volume.1.prior_ref = f32[1024,128]{1,0:T(8,128)S(1)} custom-call(bf16[1024,1024]{1,0:T(8,128)(2,1)S(1)} %bitcast.68, bf16[1024,1024]{1,0:T(8,128)(2,1)S(1)} %bitcast.70, bf16[1024,128]{1,0:T(8,128)(2,1)S(1)} %assemble.3.group_ref, f32[1024,128]{1,0:T(8,128)S(1)} %faces.3.refs_0_), custom_call_target="tpu_custom_call" | custom-call | flops 805306368 | bytes 6291456 | tf_op jit(solution)/shard_map/volume/pallas_call | solution.py:155
  104.8 2.2 %copy-done.2 = bf16[1024,2048]{1,0:T(8,128)(2,1)S(1)} copy-done((bf16[1024,2048]{1,0:T(8,128)(2,1)S(1)}, bf16[1024,2048]{1,0:T(8,128)(2,1)}, u32[]{:S(2)}) %copy-start.2) | copy-done | bytes 4194328
  107.0 1.3 %applied.3 = (f32[4,128,128]{2,1,0:T(8,128)S(1)}, bf16[4,128,128]{2,1,0:T(8,128)(2,1)S(1)}) custom-call(s32[1]{0:T(128)} %bitcast.col_ref, f32[1024,128]{1,0:T(8,128)S(1)} %volume.1.prior_ref, bf16[1024,2048]{1,0:T(8,128)(2,1)S(1)} %copy-done.2, bf16[2048,128]{1,0:T(8,128)(2,1)S(1)} %bitcast.72), custom_call_target="tpu_custom_call" | custom-call | flops 536870912 | bytes 4194304 | tf_op jit(solution)/shard_map/applied/pallas_call | solution.py:202
  110.6 2.4 %collective-permute-start.24 = (bf16[128,128]{1,0:T(8,128)(2,1)S(1)}, bf16[128,128]{1,0:T(8,128)(2,1)S(1)}, u32[]{:S(2)}, u32[]{:S(2)}) collective-permute-start(bf16[128,128]{1,0:T(8,128)(2,1)S(1)} %get-tuple-element.31), channel_id=1, source_target_pairs={{0,6},{1,7},{2,0},{3,1},{4,2},{5,3},{6,4},{7,5},{8,14},{9,15},{10,... | collective-permute-start | bytes 98312 | tf_op jit(solution)/shard_map/ppermute | solution.py:236
  114.3 3.0 %collective-permute-done.23 = bf16[128,128]{1,0:T(8,128)(2,1)S(1)} collective-permute-done((bf16[128,128]{1,0:T(8,128)(2,1)S(1)}, bf16[128,128]{1,0:T(8,128)(2,1)S(1)}, u32[]{:S(2)}, u32[]{:S(2)}) %collective-permute-start.23) | collective-permute-done | bytes 32800 | tf_op jit(solution)/shard_map/ppermute | solution.py:236
  (82 shorter events, 17.0 us)
Async XLA Ops:
  1.5 12.8 %collective-permute-start.11 = (bf16[128,128]{1,0:T(8,128)(2,1)S(1)}, bf16[128,128]{1,0:T(8,128)(2,1)S(1)}, u32[]{:S(2)}, u32[]{:S(2)}) collective-permute-start(bf16[128,128]{1,0:T(8,128)(2,1)S(1)} %convert_element_type.65), channel_id=1, source_target_pairs={{0,0},{1,8},{2,16},{3,24},{4,32},{5,40},{6,48},{7,56},{8,64},{9,72... | collective-permute-start | bytes 98312 | tf_op jit(solution)/shard_map/ppermute | solution.py:286
  8.9 27.7 %copy-start = (bf16[1,1024,1024]{2,1,0:T(8,128)(2,1)S(1)}, bf16[1,1024,1024]{2,1,0:T(8,128)(2,1)}, u32[]{:S(2)}) copy-start(bf16[1,1024,1024]{2,1,0:T(8,128)(2,1)} %param.8) | copy-start | bytes 6291460
  8.9 27.1 %collective-permute-start.10 = (bf16[128,1024]{1,0:T(8,128)(2,1)}, bf16[128,1024]{1,0:T(8,128)(2,1)S(1)}, u32[]{:S(2)}, u32[]{:S(2)}) collective-permute-start(bf16[128,1024]{1,0:T(8,128)(2,1)} %get-tuple-element.22), channel_id=1, source_target_pairs={{0,7},{1,0},{2,1},{3,2},{4,3},{5,4},{6,5},{7,6},{8,15},{9,8},{10,9... | collective-permute-start | bytes 786440 | tf_op jit(solution)/shard_map/ppermute | solution.py:271
  8.9 27.7 %collective-permute-start.9 = (bf16[128,1024]{1,0:T(8,128)(2,1)}, bf16[128,1024]{1,0:T(8,128)(2,1)S(1)}, u32[]{:S(2)}, u32[]{:S(2)}) collective-permute-start(bf16[128,1024]{1,0:T(8,128)(2,1)} %get-tuple-element.23), channel_id=1, source_target_pairs={{0,6},{1,7},{2,0},{3,1},{4,2},{5,3},{6,4},{7,5},{8,14},{9,15},{10,... | collective-permute-start | bytes 786440 | tf_op jit(solution)/shard_map/ppermute | solution.py:271
  15.2 24.4 %all-to-all-start = ((bf16[16,128,128]{2,1,0:T(8,128)(2,1)}), bf16[16,128,128]{2,1,0:T(8,128)(2,1)S(1)}, u32[]{:S(2)}, u32[]{:S(2)}) async-start(bf16[16,128,128]{2,1,0:T(8,128)(2,1)} %broadcast_in_dim.19), calls=%async_computation | async-start | bytes 1048576 | tf_op jit(solution)/shard_map/all_to_all | solution.py:32
  20.4 17.0 %copy-start.3 = (bf16[1,1024,1024]{2,1,0:T(8,128)(2,1)S(1)}, bf16[1,1024,1024]{2,1,0:T(8,128)(2,1)}, u32[]{:S(2)}) copy-start(bf16[1,1024,1024]{2,1,0:T(8,128)(2,1)} %param.7) | copy-start | bytes 6291460
  20.4 2.3 %collective-permute-start = (bf16[144,128]{1,0:T(8,128)(2,1)S(1)}, bf16[144,128]{1,0:T(8,128)(2,1)S(1)}, u32[]{:S(2)}, u32[]{:S(2)}) collective-permute-start(bf16[144,128]{1,0:T(8,128)(2,1)S(1)} %get-tuple-element.37), channel_id=1, source_target_pairs={{0,1},{1,0},{2,3},{3,2},{4,5},{5,4},{6,7},{7,6},{8,9},{9,8},{10,11... | collective-permute-start | bytes 110600 | tf_op jit(solution)/shard_map/ppermute | solution.py:232
  22.7 6.1 %collective-permute-start.3 = (bf16[2,144,128]{2,1,0:T(8,128)(2,1)S(1)}, bf16[2,144,128]{2,1,0:T(8,128)(2,1)S(1)}, u32[]{:S(2)}, u32[]{:S(2)}) collective-permute-start(bf16[2,144,128]{2,1,0:T(8,128)(2,1)S(1)} %pad_maximum_fusion.refs_0_), channel_id=1, source_target_pairs={{0,6},{1,7},{2,0},{3,1},{4,2},{5,3},{6,4},{7,5},{8,14},{9,15},{10,... | collective-permute-start | bytes 221192 | tf_op jit(solution)/shard_map/ppermute | solution.py:236
  25.9 7.4 %collective-permute-start.2 = (bf16[2,144,128]{2,1,0:T(8,128)(2,1)S(1)}, bf16[2,144,128]{2,1,0:T(8,128)(2,1)S(1)}, u32[]{:S(2)}, u32[]{:S(2)}) collective-permute-start(bf16[2,144,128]{2,1,0:T(8,128)(2,1)S(1)} %pad_maximum_fusion.refs_0_), channel_id=1, source_target_pairs={{0,4},{1,5},{2,6},{3,7},{4,0},{5,1},{6,2},{7,3},{8,12},{9,13},{10,... | collective-permute-start | bytes 221192 | tf_op jit(solution)/shard_map/ppermute | solution.py:236
  26.8 6.5 %collective-permute-start.1 = (bf16[2,144,128]{2,1,0:T(8,128)(2,1)S(1)}, bf16[2,144,128]{2,1,0:T(8,128)(2,1)S(1)}, u32[]{:S(2)}, u32[]{:S(2)}) collective-permute-start(bf16[2,144,128]{2,1,0:T(8,128)(2,1)S(1)} %pad_maximum_fusion.refs_0_), channel_id=1, source_target_pairs={{0,2},{1,3},{2,4},{3,5},{4,6},{5,7},{6,0},{7,1},{8,10},{9,11},{10,... | collective-permute-start | bytes 221192 | tf_op jit(solution)/shard_map/ppermute | solution.py:236
  28.9 19.2 %collective-permute-start.8 = (bf16[128,1024]{1,0:T(8,128)(2,1)}, bf16[128,1024]{1,0:T(8,128)(2,1)}, u32[]{:S(2)}, u32[]{:S(2)}) collective-permute-start(bf16[128,1024]{1,0:T(8,128)(2,1)} %get-tuple-element.24), channel_id=1, source_target_pairs={{0,5},{1,6},{2,7},{3,0},{4,1},{5,2},{6,3},{7,4},{8,13},{9,14},{10,... | collective-permute-start | bytes 786440 | tf_op jit(solution)/shard_map/ppermute | solution.py:271
  33.2 14.9 %collective-permute-start.7 = (bf16[128,1024]{1,0:T(8,128)(2,1)}, bf16[128,1024]{1,0:T(8,128)(2,1)}, u32[]{:S(2)}, u32[]{:S(2)}) collective-permute-start(bf16[128,1024]{1,0:T(8,128)(2,1)} %get-tuple-element.25), channel_id=1, source_target_pairs={{0,4},{1,5},{2,6},{3,7},{4,0},{5,1},{6,2},{7,3},{8,12},{9,13},{10,... | collective-permute-start | bytes 786440 | tf_op jit(solution)/shard_map/ppermute | solution.py:271
  33.3 18.2 %collective-permute-start.6 = (bf16[128,1024]{1,0:T(8,128)(2,1)}, bf16[128,1024]{1,0:T(8,128)(2,1)}, u32[]{:S(2)}, u32[]{:S(2)}) collective-permute-start(bf16[128,1024]{1,0:T(8,128)(2,1)} %get-tuple-element.26), channel_id=1, source_target_pairs={{0,3},{1,4},{2,5},{3,6},{4,7},{5,0},{6,1},{7,2},{8,11},{9,12},{10,... | collective-permute-start | bytes 786440 | tf_op jit(solution)/shard_map/ppermute | solution.py:271
  36.0 15.9 %collective-permute-start.5 = (bf16[128,1024]{1,0:T(8,128)(2,1)}, bf16[128,1024]{1,0:T(8,128)(2,1)}, u32[]{:S(2)}, u32[]{:S(2)}) collective-permute-start(bf16[128,1024]{1,0:T(8,128)(2,1)} %get-tuple-element.27), channel_id=1, source_target_pairs={{0,2},{1,3},{2,4},{3,5},{4,6},{5,7},{6,0},{7,1},{8,10},{9,11},{10,... | collective-permute-start | bytes 786440 | tf_op jit(solution)/shard_map/ppermute | solution.py:271
  36.6 17.2 %collective-permute-start.4 = (bf16[128,1024]{1,0:T(8,128)(2,1)}, bf16[128,1024]{1,0:T(8,128)(2,1)}, u32[]{:S(2)}, u32[]{:S(2)}) collective-permute-start(bf16[128,1024]{1,0:T(8,128)(2,1)} %get-tuple-element.28), channel_id=1, source_target_pairs={{0,1},{1,2},{2,3},{3,4},{4,5},{5,6},{6,7},{7,0},{8,9},{9,10},{10,1... | collective-permute-start | bytes 786440 | tf_op jit(solution)/shard_map/ppermute | solution.py:271
  43.1 25.8 %copy-start.13 = (f32[128,128]{1,0:T(8,128)S(1)}, f32[128,128]{1,0:T(8,128)}, u32[]{:S(2)}) copy-start(f32[128,128]{1,0:T(8,128)} %param.6) | copy-start | bytes 196612
  56.6 42.5 %copy-start.7 = (bf16[128,1024]{1,0:T(8,128)(2,1)S(1)}, bf16[128,1024]{1,0:T(8,128)(2,1)}, u32[]{:S(2)}) copy-start(bf16[128,1024]{1,0:T(8,128)(2,1)} %copy-done.5) | copy-start | bytes 786436
  56.6 42.5 %copy-start.10 = (bf16[128,1024]{1,0:T(8,128)(2,1)S(1)}, bf16[128,1024]{1,0:T(8,128)(2,1)}, u32[]{:S(2)}) copy-start(bf16[128,1024]{1,0:T(8,128)(2,1)} %copy-done.8) | copy-start | bytes 786436
  56.7 5.1 %collective-permute-start.12 = (bf16[4,128,128]{2,1,0:T(8,128)(2,1)S(1)}, bf16[4,128,128]{2,1,0:T(8,128)(2,1)S(1)}, u32[]{:S(2)}, u32[]{:S(2)}) collective-permute-start(bf16[4,128,128]{2,1,0:T(8,128)(2,1)S(1)} %get-tuple-element.11), channel_id=1, source_target_pairs={{0,1},{1,0},{2,3},{3,2},{4,5},{5,4},{6,7},{7,6},{8,9},{9,8},{10,11... | collective-permute-start | bytes 393224 | tf_op jit(solution)/shard_map/ppermute | solution.py:232
  61.8 4.0 %collective-permute-start.13 = (bf16[128,128]{1,0:T(8,128)(2,1)S(1)}, bf16[128,128]{1,0:T(8,128)(2,1)S(1)}, u32[]{:S(2)}, u32[]{:S(2)}) collective-permute-start(bf16[128,128]{1,0:T(8,128)(2,1)S(1)} %get-tuple-element.33), channel_id=1, source_target_pairs={{0,2},{1,3},{2,4},{3,5},{4,6},{5,7},{6,0},{7,1},{8,10},{9,11},{10,... | collective-permute-start | bytes 98312 | tf_op jit(solution)/shard_map/ppermute | solution.py:236
  61.9 4.0 %collective-permute-start.15 = (bf16[128,128]{1,0:T(8,128)(2,1)S(1)}, bf16[128,128]{1,0:T(8,128)(2,1)S(1)}, u32[]{:S(2)}, u32[]{:S(2)}) collective-permute-start(bf16[128,128]{1,0:T(8,128)(2,1)S(1)} %get-tuple-element.34), channel_id=1, source_target_pairs={{0,6},{1,7},{2,0},{3,1},{4,2},{5,3},{6,4},{7,5},{8,14},{9,15},{10,... | collective-permute-start | bytes 98312 | tf_op jit(solution)/shard_map/ppermute | solution.py:236
  64.6 4.3 %collective-permute-start.14 = (bf16[128,128]{1,0:T(8,128)(2,1)S(1)}, bf16[128,128]{1,0:T(8,128)(2,1)S(1)}, u32[]{:S(2)}, u32[]{:S(2)}) collective-permute-start(bf16[128,128]{1,0:T(8,128)(2,1)S(1)} %get-tuple-element.35), channel_id=1, source_target_pairs={{0,4},{1,5},{2,6},{3,7},{4,0},{5,1},{6,2},{7,3},{8,12},{9,13},{10,... | collective-permute-start | bytes 98312 | tf_op jit(solution)/shard_map/ppermute | solution.py:236
  69.5 8.6 %collective-permute-start.20 = (bf16[128,128]{1,0:T(8,128)(2,1)S(1)}, bf16[128,128]{1,0:T(8,128)(2,1)S(1)}, u32[]{:S(2)}, u32[]{:S(2)}) collective-permute-start(bf16[128,128]{1,0:T(8,128)(2,1)S(1)} %get-tuple-element.18), channel_id=1, source_target_pairs={{0,0},{1,8},{2,16},{3,24},{4,32},{5,40},{6,48},{7,56},{8,64},{9,72... | collective-permute-start | bytes 98312 | tf_op jit(solution)/shard_map/ppermute | solution.py:286
  79.0 25.7 %all-to-all-start.1 = ((bf16[16,128,128]{2,1,0:T(8,128)(2,1)}), bf16[16,128,128]{2,1,0:T(8,128)(2,1)S(1)}, u32[]{:S(2)}, u32[]{:S(2)}) async-start(bf16[16,128,128]{2,1,0:T(8,128)(2,1)} %broadcast_in_dim.20), calls=%async_computation.1 | async-start | bytes 1048576 | tf_op jit(solution)/shard_map/all_to_all | solution.py:32
  86.5 5.0 %collective-permute-start.16 = (bf16[128,128]{1,0:T(8,128)(2,1)}, bf16[128,128]{1,0:T(8,128)(2,1)S(1)}, u32[]{:S(2)}, u32[]{:S(2)}) collective-permute-start(bf16[128,128]{1,0:T(8,128)(2,1)} %copy-done.15), channel_id=1, source_target_pairs={{0,1},{1,0},{2,3},{3,2},{4,5},{5,4},{6,7},{7,6},{8,9},{9,8},{10,11... | collective-permute-start | bytes 98312 | tf_op jit(solution)/shard_map/ppermute | solution.py:232
  92.3 3.4 %collective-permute-start.19 = (bf16[2,128,128]{2,1,0:T(8,128)(2,1)S(1)}, bf16[2,128,128]{2,1,0:T(8,128)(2,1)S(1)}, u32[]{:S(2)}, u32[]{:S(2)}) collective-permute-start(bf16[2,128,128]{2,1,0:T(8,128)(2,1)S(1)} %pad_maximum_fusion.1.refs_0_), channel_id=1, source_target_pairs={{0,6},{1,7},{2,0},{3,1},{4,2},{5,3},{6,4},{7,5},{8,14},{9,15},{10,... | collective-permute-start | bytes 196616 | tf_op jit(solution)/shard_map/ppermute | solution.py:236
  92.3 5.0 %collective-permute-start.18 = (bf16[2,128,128]{2,1,0:T(8,128)(2,1)S(1)}, bf16[2,128,128]{2,1,0:T(8,128)(2,1)S(1)}, u32[]{:S(2)}, u32[]{:S(2)}) collective-permute-start(bf16[2,128,128]{2,1,0:T(8,128)(2,1)S(1)} %pad_maximum_fusion.1.refs_0_), channel_id=1, source_target_pairs={{0,4},{1,5},{2,6},{3,7},{4,0},{5,1},{6,2},{7,3},{8,12},{9,13},{10,... | collective-permute-start | bytes 196616 | tf_op jit(solution)/shard_map/ppermute | solution.py:236
  93.3 5.8 %collective-permute-start.17 = (bf16[2,128,128]{2,1,0:T(8,128)(2,1)S(1)}, bf16[2,128,128]{2,1,0:T(8,128)(2,1)S(1)}, u32[]{:S(2)}, u32[]{:S(2)}) collective-permute-start(bf16[2,128,128]{2,1,0:T(8,128)(2,1)S(1)} %pad_maximum_fusion.1.refs_0_), channel_id=1, source_target_pairs={{0,2},{1,3},{2,4},{3,5},{4,6},{5,7},{6,0},{7,1},{8,10},{9,11},{10,... | collective-permute-start | bytes 196616 | tf_op jit(solution)/shard_map/ppermute | solution.py:236
  108.3 1.9 %collective-permute-start.21 = (bf16[4,128,128]{2,1,0:T(8,128)(2,1)S(1)}, bf16[4,128,128]{2,1,0:T(8,128)(2,1)S(1)}, u32[]{:S(2)}, u32[]{:S(2)}) collective-permute-start(bf16[4,128,128]{2,1,0:T(8,128)(2,1)S(1)} %get-tuple-element.13), channel_id=1, source_target_pairs={{0,1},{1,0},{2,3},{3,2},{4,5},{5,4},{6,7},{7,6},{8,9},{9,8},{10,11... | collective-permute-start | bytes 393224 | tf_op jit(solution)/shard_map/ppermute | solution.py:232
  110.2 4.0 %collective-permute-start.22 = (bf16[128,128]{1,0:T(8,128)(2,1)S(1)}, bf16[128,128]{1,0:T(8,128)(2,1)S(1)}, u32[]{:S(2)}, u32[]{:S(2)}) collective-permute-start(bf16[128,128]{1,0:T(8,128)(2,1)S(1)} %get-tuple-element.30), channel_id=1, source_target_pairs={{0,2},{1,3},{2,4},{3,5},{4,6},{5,7},{6,0},{7,1},{8,10},{9,11},{10,... | collective-permute-start | bytes 98312 | tf_op jit(solution)/shard_map/ppermute | solution.py:236
  110.6 3.7 %collective-permute-start.24 = (bf16[128,128]{1,0:T(8,128)(2,1)S(1)}, bf16[128,128]{1,0:T(8,128)(2,1)S(1)}, u32[]{:S(2)}, u32[]{:S(2)}) collective-permute-start(bf16[128,128]{1,0:T(8,128)(2,1)S(1)} %get-tuple-element.31), channel_id=1, source_target_pairs={{0,6},{1,7},{2,0},{3,1},{4,2},{5,3},{6,4},{7,5},{8,14},{9,15},{10,... | collective-permute-start | bytes 98312 | tf_op jit(solution)/shard_map/ppermute | solution.py:236
  113.0 4.3 %collective-permute-start.23 = (bf16[128,128]{1,0:T(8,128)(2,1)S(1)}, bf16[128,128]{1,0:T(8,128)(2,1)S(1)}, u32[]{:S(2)}, u32[]{:S(2)}) collective-permute-start(bf16[128,128]{1,0:T(8,128)(2,1)S(1)} %get-tuple-element.32), channel_id=1, source_target_pairs={{0,4},{1,5},{2,6},{3,7},{4,0},{5,1},{6,2},{7,3},{8,12},{9,13},{10,... | collective-permute-start | bytes 98312 | tf_op jit(solution)/shard_map/ppermute | solution.py:236
  (12 other events, 86.6 us)
